TPU v7x, 32 devices: a whole 2x2x4 slice. The times are simulated.
32 devices in a mesh: dp: 8 (over z, y), seq: 4 (over x, core).
Axes of the slice: x: 2, y: 2, z: 4, core: 2. Of those that a mesh axis runs over, the one named last changes fastest.
Arguments:
- tokens: bfloat16 [3, 8, 2048, 768], P(None, 'dp', 'seq'), may hold values from -6 to 6
- norm_gain: float32 [768], P(('dp', 'seq')), may hold values from 0.1 to 1.9
- w_in: float32 [768, 3352], P(('dp', 'seq')), may hold values from -0.21875 to 0.21875
- conv_weight: float32 [4, 1792], P(None, ('dp', 'seq')), may hold values from -3 to 3
- conv_bias: float32 [1792], P(('dp', 'seq')), may hold values from -3 to 3
- dt_bias: float32 [24], replicated, may hold values from -3 to 0.5
- a_log: float32 [24], replicated, may hold values from -6 to 0
- d_skip: float32 [24], replicated, may hold values from -3 to 3
- gated_gain: float32 [1536], P(('dp', 'seq')), may hold values from 0.1 to 1.9
- w_out: float32 [1536, 768], P(('dp', 'seq')), may hold values from -0.15625 to 0.15625
- lengths: int32 [3, 8], P(None, 'dp'), may hold values from 1024 to 2048, as said below
- cotangent: bfloat16 [3, 8, 2048, 768], P(None, 'dp', 'seq'), may hold values from -6 to 6
Outputs:
- block_out: bfloat16 [3, 8, 2048, 768], P(None, 'dp', 'seq')
- tokens_grad: bfloat16 [3, 8, 2048, 768], P(None, 'dp', 'seq')
- norm_gain_grad: float32 [768], P(('dp', 'seq'))
- w_in_grad: float32 [768, 3352], P(('dp', 'seq'))
- conv_weight_grad: float32 [4, 1792], P(None, ('dp', 'seq'))
- conv_bias_grad: float32 [1792], P(('dp', 'seq'))
- dt_bias_grad: float32 [24], replicated
- a_log_grad: float32 [24], replicated
- d_skip_grad: float32 [24], replicated
- gated_gain_grad: float32 [1536], P(('dp', 'seq'))
- w_out_grad: float32 [1536, 768], P(('dp', 'seq'))
Inputs may be any that keep to these rules, and one draw needn't show every extreme that they name: `lengths`: one sequence of the draw has length exactly 2048.
All inputs are finite; a program needn't handle non-finite values.
Results may differ from a plain program's by a relative error of at most 0.0085.
The roundings to bfloat16 on the way count: a program that leaves them out, or rounds other values in their place, can miss the bound.
Values may be sent and summed in bfloat16 or wider, within the bound.
A program may use at most 320 MiB of HBM per device.

v0:
```python
from functools import partial

import jax
import jax.numpy as jnp
from jax import lax
from jax.sharding import PartitionSpec as P

D = 768
NH = 24
HD = 64
NS = 128
DCONV = 4
CH = 256
MB = 3
PIECE = 512
DI = 1536
XBC = 1792
PROJ = 3352


EPSILON = 1e-05
PRECISE = lax.Precision.HIGHEST


def from_behind(block, axis, distance):
    devices = range(lax.axis_size(axis))
    route = [(i - distance, i) for i in devices if i - distance in devices]
    return lax.ppermute(block, axis, route)


def prefix(part, axis, combine, identity, reverse):
    count = lax.axis_size(axis)
    place = lax.axis_index(axis)
    ahead = count - 1 - place if reverse else place
    gathered = jax.tree.map(lambda a: lax.all_gather(a, axis), part)
    state = jax.tree.map(lambda a, e: jnp.zeros_like(a) + jnp.asarray(e, a.dtype), part, identity)

    def one(lap, state):
        source = count - 1 - lap if reverse else lap
        return combine(
            state, jax.tree.map(lambda a: lax.dynamic_index_in_dim(a, source, 0, False), gathered)
        )

    return lax.fori_loop(0, ahead, one, state)


def rms_scale(values, scale_gain):
    return (
        values * lax.rsqrt(jnp.mean(values * values, axis=-1, keepdims=True) + EPSILON) * scale_gain
    )


def conv_part(projected, edge_rows, conv_weight, conv_bias, dt_bias, a_log, validity):
    row_count = projected.shape[0]
    gate_part = projected[:, :DI]
    conv_input = projected[:, DI : DI + XBC]
    dt_raw = projected[:, DI + XBC :]
    padded = jnp.concatenate([edge_rows, conv_input], axis=0)
    running = conv_bias + jnp.zeros_like(conv_input)
    for tap_index in range(DCONV):
        running = running + padded[tap_index : tap_index + row_count] * conv_weight[tap_index]
    activated = jax.nn.silu(running)
    inputs_ssm = activated[:, :DI].reshape(row_count, NH, HD)
    b_rows = activated[:, DI : DI + NS]
    c_rows = activated[:, DI + NS :]
    step_size = jax.nn.softplus(dt_raw + dt_bias) * validity[:, None]
    decay_rate = -jnp.exp(a_log)
    return (gate_part, inputs_ssm, b_rows, c_rows, step_size, decay_rate)


def local_states(inputs_ssm, b_rows, step_size, decay_rate):
    blocks = inputs_ssm.shape[0] // CH
    input_blocks = inputs_ssm.reshape(blocks, CH, NH, HD)
    b_blocks = b_rows.reshape(blocks, CH, NS)
    step_blocks = step_size.reshape(blocks, CH, NH)
    log_decay = jnp.cumsum(step_blocks * decay_rate, axis=1)
    block_decay = jnp.exp(log_decay[:, -1])
    tail_weight = jnp.exp(log_decay[:, -1:] - log_decay) * step_blocks
    weighted = input_blocks * tail_weight[..., None]
    block_local = jnp.einsum("kshp,ksn->khpn", weighted, b_blocks, precision=PRECISE)
    states = jnp.zeros((NH, HD, NS), jnp.float32)
    product = jnp.ones((NH,), jnp.float32)
    for block_index in range(blocks):
        states = block_decay[block_index][:, None, None] * states + block_local[block_index]
        product = product * block_decay[block_index]
    return (product, states, block_decay, block_local)


def out_part(
    gate_part,
    inputs_ssm,
    b_rows,
    c_rows,
    step_size,
    decay_rate,
    block_decay,
    block_local,
    incoming,
    d_skip,
    gated_gain,
):
    row_count = inputs_ssm.shape[0]
    blocks = row_count // CH
    input_blocks = inputs_ssm.reshape(blocks, CH, NH, HD)
    b_blocks = b_rows.reshape(blocks, CH, NS)
    c_blocks = c_rows.reshape(blocks, CH, NS)
    step_blocks = step_size.reshape(blocks, CH, NH)
    log_decay = jnp.cumsum(step_blocks * decay_rate, axis=1)
    starts = []
    states = incoming
    for block_index in range(blocks):
        starts.append(states)
        states = block_decay[block_index][:, None, None] * states + block_local[block_index]
    start_states = jnp.stack(starts)
    causal = lax.broadcasted_iota(jnp.int32, (CH, CH), 0) >= lax.broadcasted_iota(
        jnp.int32, (CH, CH), 1
    )
    heads_first = jnp.transpose(log_decay, (0, 2, 1))
    log_gaps = heads_first[:, :, :, None] - heads_first[:, :, None, :]
    weights = jnp.where(causal, jnp.exp(jnp.where(causal, log_gaps, 0.0)), 0.0)
    scores = jnp.einsum("ktn,ksn->kts", c_blocks, b_blocks, precision=PRECISE)
    mixing = weights * scores[:, None] * jnp.transpose(step_blocks, (0, 2, 1))[:, :, None, :]
    y_diag = jnp.einsum("khts,kshp->kthp", mixing, input_blocks, precision=PRECISE)
    y_off = (
        jnp.einsum("ktn,khpn->kthp", c_blocks, start_states, precision=PRECISE)
        * jnp.exp(log_decay)[..., None]
    )
    y_full = (y_diag + y_off).reshape(row_count, NH, HD) + d_skip[:, None] * inputs_ssm
    gated_rows = y_full.reshape(row_count, DI) * jax.nn.silu(gate_part)
    return rms_scale(gated_rows, gated_gain)


def combine_affine(earlier, later):
    return (earlier[0] * later[0], later[0][:, None, None] * earlier[1] + later[1])


def contract_rows(left, right):
    return lax.dot_general(
        left, right, (((0,), (0,)), ((), ())), preferred_element_type=jnp.float32
    )


def contract_cols(left, right):
    return lax.dot_general(
        left, right, (((1,), (1,)), ((), ())), preferred_element_type=jnp.float32
    )


def local(
    tokens,
    norm_gain,
    w_in,
    conv_weight,
    conv_bias,
    dt_bias,
    a_log,
    d_skip,
    gated_gain,
    w_out,
    lengths,
    cotangent,
):
    full_gain, full_gated, full_conv_bias, full_conv_weight = (
        lax.all_gather(norm_gain, ("dp", "seq"), axis=0, tiled=True),
        lax.all_gather(gated_gain, ("dp", "seq"), axis=0, tiled=True),
        lax.all_gather(conv_bias, ("dp", "seq"), axis=0, tiled=True),
        lax.all_gather(conv_weight, ("dp", "seq"), axis=1, tiled=True),
    )
    w_in_low = w_in.astype(jnp.bfloat16)
    w_out_low = w_out.astype(jnp.bfloat16)
    positions = lax.axis_index("seq") * PIECE + lax.broadcasted_iota(jnp.int32, (PIECE,), 0)
    identity = (jnp.ones((NH,), jnp.float32), jnp.zeros((NH, HD, NS), jnp.float32))
    grad_w_in = jnp.zeros((D, PROJ), jnp.float32)
    grad_w_out = jnp.zeros((DI, D), jnp.float32)
    grad_gain = jnp.zeros((D,), jnp.float32)
    grad_gated = jnp.zeros((DI,), jnp.float32)
    grad_conv_bias = jnp.zeros((XBC,), jnp.float32)
    grad_conv_weight = jnp.zeros((DCONV, XBC), jnp.float32)
    grad_dt_bias = jnp.zeros((NH,), jnp.float32)
    grad_a_log = jnp.zeros((NH,), jnp.float32)
    grad_d_skip = jnp.zeros((NH,), jnp.float32)
    results = []
    token_grads = []
    for section in range(MB):
        whole_in, whole_out = (
            lax.all_gather(w_in_low, ("dp", "seq"), axis=0, tiled=True),
            lax.all_gather(w_out_low, ("dp", "seq"), axis=0, tiled=True),
        )
        validity = (positions < lengths[section, 0]).astype(jnp.float32)
        token_rows = tokens[section, 0].astype(jnp.float32)
        normed, pull_norm = jax.vjp(rms_scale, token_rows, full_gain)
        normed_low = normed.astype(jnp.bfloat16)
        projected = jnp.dot(normed_low, whole_in, preferred_element_type=jnp.float32)
        edge_rows = from_behind(projected[PIECE - (DCONV - 1) :, DI : DI + XBC], "seq", 1)
        conv_outputs, pull_conv = jax.vjp(
            partial(conv_part, validity=validity),
            projected,
            edge_rows,
            full_conv_weight,
            full_conv_bias,
            dt_bias,
            a_log,
        )
        gate_part, inputs_ssm, b_rows, c_rows, step_size, decay_rate = conv_outputs
        state_outputs, pull_states = jax.vjp(
            local_states, inputs_ssm, b_rows, step_size, decay_rate
        )
        piece_decay, piece_state, block_decay, block_local = state_outputs
        incoming = prefix((piece_decay, piece_state), "seq", combine_affine, identity, False)[1]
        gated_norm, pull_out = jax.vjp(
            out_part,
            gate_part,
            inputs_ssm,
            b_rows,
            c_rows,
            step_size,
            decay_rate,
            block_decay,
            block_local,
            incoming,
            d_skip,
            full_gated,
        )
        gated_low = gated_norm.astype(jnp.bfloat16)
        branch = jnp.dot(gated_low, whole_out, preferred_element_type=jnp.float32)
        results.append((validity[:, None] * (token_rows + branch)).astype(jnp.bfloat16))
        back_in, back_out = (
            lax.all_gather(w_in_low, ("dp", "seq"), axis=0, tiled=True),
            lax.all_gather(w_out_low, ("dp", "seq"), axis=0, tiled=True),
        )
        cot_rows = cotangent[section, 0].astype(jnp.float32)
        d_branch = (validity[:, None] * cot_rows).astype(jnp.bfloat16)
        grad_w_out = grad_w_out + contract_rows(gated_low, d_branch)
        d_gated = contract_cols(d_branch, back_out)
        (
            d_gate,
            d_inputs,
            d_brows,
            d_crows,
            d_step,
            d_rate,
            d_block_decay,
            d_block_local,
            d_incoming,
            d_dskip,
            d_gated_gain,
        ) = pull_out(d_gated)
        later_sum = prefix((piece_decay, d_incoming), "seq", combine_affine, identity, True)[1]
        d_piece_decay = jnp.sum(later_sum * incoming, axis=(1, 2))
        d_inputs_b, d_brows_b, d_step_b, d_rate_b = pull_states(
            (d_piece_decay, later_sum, d_block_decay, d_block_local)
        )
        d_projected, d_edge, d_conv_weight, d_conv_bias, d_dt_bias, d_alog = pull_conv(
            (
                d_gate,
                d_inputs + d_inputs_b,
                d_brows + d_brows_b,
                d_crows,
                d_step + d_step_b,
                d_rate + d_rate_b,
            )
        )
        back_edge = from_behind(d_edge, "seq", -1)
        d_projected = d_projected.at[PIECE - (DCONV - 1) :, DI : DI + XBC].add(back_edge)
        d_proj_low = d_projected.astype(jnp.bfloat16)
        grad_w_in = grad_w_in + contract_rows(normed_low, d_proj_low)
        d_normed = contract_cols(d_proj_low, back_in)
        d_token_norm, d_gain = pull_norm(d_normed)
        token_grads.append((validity[:, None] * cot_rows + d_token_norm).astype(jnp.bfloat16))
        grad_gain = grad_gain + d_gain
        grad_gated = grad_gated + d_gated_gain
        grad_conv_bias = grad_conv_bias + d_conv_bias
        grad_conv_weight = grad_conv_weight + d_conv_weight
        grad_dt_bias = grad_dt_bias + d_dt_bias
        grad_a_log = grad_a_log + d_alog
        grad_d_skip = grad_d_skip + d_dskip
    shard_w_in, shard_w_out, shard_gain, shard_gated, shard_conv_bias, shard_conv_weight = (
        lax.psum_scatter(grad_w_in, ("dp", "seq"), scatter_dimension=0, tiled=True),
        lax.psum_scatter(grad_w_out, ("dp", "seq"), scatter_dimension=0, tiled=True),
        lax.psum_scatter(grad_gain, ("dp", "seq"), scatter_dimension=0, tiled=True),
        lax.psum_scatter(grad_gated, ("dp", "seq"), scatter_dimension=0, tiled=True),
        lax.psum_scatter(grad_conv_bias, ("dp", "seq"), scatter_dimension=0, tiled=True),
        lax.psum_scatter(grad_conv_weight, ("dp", "seq"), scatter_dimension=1, tiled=True),
    )
    total_dt_bias, total_a_log, total_d_skip = lax.psum(
        (grad_dt_bias, grad_a_log, grad_d_skip), ("dp", "seq")
    )
    return (
        jnp.stack(results)[:, None],
        jnp.stack(token_grads)[:, None],
        shard_gain,
        shard_w_in,
        shard_conv_weight,
        shard_conv_bias,
        total_dt_bias,
        total_a_log,
        total_d_skip,
        shard_gated,
        shard_w_out,
    )


def solution(mesh):
    return jax.shard_map(
        local,
        mesh=mesh,
        in_specs=(
            P(None, "dp", "seq", None),
            P(("dp", "seq")),
            P(("dp", "seq"), None),
            P(None, ("dp", "seq")),
            P(("dp", "seq")),
            P(),
            P(),
            P(),
            P(("dp", "seq")),
            P(("dp", "seq"), None),
            P(None, "dp"),
            P(None, "dp", "seq", None),
        ),
        out_specs=(
            P(None, "dp", "seq", None),
            P(None, "dp", "seq", None),
            P(("dp", "seq")),
            P(("dp", "seq"), None),
            P(None, ("dp", "seq")),
            P(("dp", "seq")),
            P(),
            P(),
            P(),
            P(("dp", "seq")),
            P(("dp", "seq"), None),
        ),
        check_vma=False,
    )
```

profile of v0, /device:TPU:0, one launch (start us, length us, event | category | flops | bytes accessed | tf_op | source)
XLA Modules:
  0.0 1160.4 jit_solution(8254419771751811653)
XLA Ops:
  15.6 43.7 %all-gather = f32[32,56,4]{1,2,0:T(4,128)S(1)} all-gather(f32[1,56,4]{1,2,0:T(4,128)S(1)} %bitcast.910), channel_id=1, replica_groups=mesh['dp'=8,'seq'=4] {'dp','seq'}, dimensions={0}, use_global_device_ids=true | all-gather | bytes 29568 | tf_op jit(solution)/shard_map/all_gather | solution.py:167
  62.3 37.4 %all-reduce.81 = (f32[768]{0:T(1024)S(1)}, f32[1792]{0:T(1024)S(1)}, f32[1536]{0:T(1024)}) all-reduce(f32[768]{0:T(1024)S(1)} %dynamic-update-slice.7, f32[1792]{0:T(1024)S(1)} %dynamic-update-slice.6, f32[1536]{0:T(1024)S(1)} %dynamic-update-slice.8), channel_id=1, replica_groups=mesh['dp'=8,'seq'=4] {'dp','seq'}, use_global_device_ids=true, to_apply=%add.73 | all-reduce | flops 4096 | bytes 32768
  138.9 12.0 %fusion.75 = (f32[512,1792]{0,1:T(8,128)S(1)}, f32[512,1792]{0,1:T(8,128)}) fusion(f32[512,1792]{0,1:T(8,128)} %slice.438, f32[1792]{0:T(1024)S(1)} %get-tuple-element.577, f32[1792]{0:T(1024)S(1)} %get-tuple-element.578, f32[3,1792]{0,1:T(8,128)S(1)} %copy.529, f32[1792]{0:T(1024)S(1)} %get-tuple-element.579, f32[1792]{0:T(1024)S(1)} %get-tuple-element.576, ...), kind=kLoop, calls=%fused_computation.138 | loop fusion | flops 13762560 | bytes 11067392 | tf_op jit(solution)/shard_map/jvp(jit(silu))/mul | solution.py:62
  193.7 21.6 %fusion.77 = (f32[512,1792]{0,1:T(8,128)S(1)}, f32[512,1792]{0,1:T(8,128)}, f32[512,1792]{0,1:T(8,128)S(1)}, f32[512,1792]{0,1:T(8,128)}) fusion(f32[512,1792]{0,1:T(8,128)} %slice.402, f32[1792]{0:T(1024)S(1)} %copy-done.155, f32[1792]{0:T(1024)S(1)} %copy-done.158, f32[3,1792]{0,1:T(8,128)} %copy.500, f32[1792]{0:T(1024)S(1)} %copy-done.161, ...), kind=kLoop, calls=%fused_computation.144 | loop fusion | flops 27525120 | bytes 22098944 | tf_op jit(solution)/shard_map/jvp(jit(silu))/mul | solution.py:62
  319.7 14.9 %bitcast_add_fusion.6 = f32[2,256,24,64]{1,3,2,0:T(8,128)S(1)} fusion(f32[2,256,24,64]{1,3,2,0:T(8,128)S(1)} %fusion.233, f32[2,24,256]{2,1,0:T(8,128)S(1)} %copy-done.192, f32[2,256,256]{2,1,0:T(8,128)S(1)} %copy-done.126, f32[2,24,256]{2,1,0:T(8,128)S(1)} %copy-done.195, pred[256,256]{1,0:T(8,128)(4,1)S(1)} %copy-done.171, ...), kind=kOutput, calls=%fused_computation.161 | convolution fusion | flops 2433220608 | bytes 10174464 | tf_op jit(solution)/shard_map/jvp(khts,kshp->kthp)/dot_general | solution.py:123
  345.6 14.6 %bitcast_add_fusion.8 = f32[2,256,24,64]{1,3,2,0:T(8,128)S(1)} fusion(f32[2,256,24,64]{1,3,2,0:T(8,128)S(1)} %fusion.235, f32[2,24,256]{2,1,0:T(8,128)S(1)} %copy-done.186, f32[2,256,256]{2,1,0:T(8,128)S(1)} %copy-done.131, f32[2,24,256]{2,1,0:T(8,128)S(1)} %copy-done.198, pred[256,256]{1,0:T(8,128)(4,1)S(1)} %copy-done.172, ...), kind=kOutput, calls=%fused_computation.173 | convolution fusion | flops 2433220608 | bytes 10174464 | tf_op jit(solution)/shard_map/jvp(khts,kshp->kthp)/dot_general | solution.py:123
  373.7 14.9 %bitcast_add_fusion.7 = f32[2,256,24,64]{1,3,2,0:T(8,128)S(1)} fusion(f32[2,256,24,64]{1,3,2,0:T(8,128)S(1)} %fusion.234, f32[2,24,256]{2,1,0:T(8,128)S(1)} %copy-done.189, f32[2,256,256]{2,1,0:T(8,128)S(1)} %copy-done.129, f32[2,24,256]{2,1,0:T(8,128)S(1)} %copy-done.201, pred[256,256]{1,0:T(8,128)(4,1)S(1)} %copy-done.173, ...), kind=kOutput, calls=%fused_computation.167 | convolution fusion | flops 2433220608 | bytes 10174464 | tf_op jit(solution)/shard_map/jvp(khts,kshp->kthp)/dot_general | solution.py:123
  394.4 11.0 multiply_reduce_fusion.35
  413.5 13.6 %multiply_reduce_fusion.22 = (f32[1536]{0:T(1024)}, f32[512,1536]{0,1:T(8,128)}, f32[512,1536]{0,1:T(8,128)}, f32[512]{0:T(512)S(1)}, f32[1536]{0:T(1024)}, /*in...) fusion(f32[512,1792]{0,1:T(8,128)S(1)} %copy-done.35, f32[512,3352]{0,1:T(8,128)} %copy-done.44, ...), kind=kOutput, calls=%fused_computation.183 | convolution fusion | flops 1235085824 | bytes 37793792 | tf_op jit(solution)/shard_map/dot_general | solution.py:144
  459.7 13.2 %fusion.149 = f32[2,256,24,64]{1,3,2,0:T(8,128)S(1)} fusion(f32[2,24,256]{2,1,0:T(8,128)S(1)} %copy-done.190, f32[2,256,256]{2,1,0:T(8,128)} %fusion.411, f32[2,24,256]{2,1,0:T(8,128)S(1)} %copy-done.202, pred[256,256]{1,0:T(8,128)(4,1)S(1)} %copy-done.174, f32[2,256,24,64]{1,0,3,2:T(2,128)} %reshape.835), kind=kOutput, calls=%fused_computation.266 | convolution fusion | flops 2431647744 | bytes 6979584 | tf_op jit(solution)/shard_map/transpose(jvp(khts,kshp->kthp))/dot_general | solution.py:123
  478.5 11.4 fusion.144
  547.9 17.2 %multiply_reduce_fusion.21 = (f32[1536]{0:T(1024)}, f32[512,1536]{0,1:T(8,128)}, f32[512,1536]{0,1:T(8,128)}, f32[512,1536]{0,1:T(8,128)}, f32[512,1536]{0,1:T(8,128)}) fusion(f32[512,1792]{0,1:T(8,128)S(1)} %copy-done.16, f32[512,3352]{0,1:T(8,128)} %copy-done.31, f32[512,1536]{0,1:T(8,128)} %get-tuple-element.756, f32[512]{0:T(512)S(1)} %multiply_multiply_fusion.1, ...), kind=kLoop, calls=%fused_computation.182 | loop fusion | flops 21232128 | bytes 47208448 | tf_op jit(solution)/shard_map/transpose(jvp())/reduce_sum | solution.py:128
  601.8 12.9 %fusion.88 = f32[2,24,256,256]{3,2,1,0:T(8,128)} fusion(f32[2,256,24,64]{1,0,3,2:T(2,128)S(1)} %copy-done.4, f32[2,256,24,64]{1,0,3,2:T(2,128)S(1)} %copy-done.3), kind=kOutput, calls=%fused_computation.156 | convolution fusion | flops 2415919104 | bytes 18874368 | tf_op jit(solution)/shard_map/transpose(jvp(khts,kshp->kthp))/dot_general | solution.py:123
  640.7 12.5 %fusion.154 = f32[2,256,24,64]{1,3,2,0:T(8,128)} fusion(f32[2,24,256]{2,1,0:T(8,128)S(1)} %copy-done.193, f32[2,256,256]{2,1,0:T(8,128)S(1)} %copy-done.127, f32[2,24,256]{2,1,0:T(8,128)S(1)} %copy-done.196, pred[256,256]{1,0:T(8,128)(4,1)S(1)} %copy-done.175, f32[2,256,24,64]{1,0,3,2:T(2,128)S(1)} %copy-done.5), kind=kOutput, calls=%fused_computation.267 | convolution fusion | flops 2431647744 | bytes 6979584 | tf_op jit(solution)/shard_map/transpose(jvp(khts,kshp->kthp))/dot_general | solution.py:123
  653.3 12.9 %fusion.85 = f32[2,24,256,256]{3,2,1,0:T(8,128)} fusion(f32[2,256,24,64]{1,0,3,2:T(2,128)S(1)} %copy-done.5, f32[2,256,24,64]{1,0,3,2:T(2,128)S(1)} %copy-done.1), kind=kOutput, calls=%fused_computation.153 | convolution fusion | flops 2415919104 | bytes 18874368 | tf_op jit(solution)/shard_map/transpose(jvp(khts,kshp->kthp))/dot_general | solution.py:123
  695.3 37.5 %fusion.22 = (f32[2,24,256]{2,1,0:T(8,128)}, f32[2,24,256]{2,1,0:T(8,128)}, f32[2,24,256]{2,1,0:T(8,128)}, f32[2,256,256]{2,1,0:T(8,128)S(1)}, f32[2,256,256]{2,...) fusion(f32[2,24,256]{2,1,0:T(8,128)S(1)} %copy-done.188, ...), kind=kOutput, calls=%fused_computation.44 | convolution fusion | flops 2556973056 | bytes 35405824 | tf_op jit(solution)/shard_map/transpose(jvp(khts,kshp->kthp))/dot_general | solution.py:123
  782.1 13.6 %multiply_reduce_fusion.16 = (f32[1792]{0:T(1024)}, f32[1792]{0:T(1024)}, f32[1792]{0:T(1024)S(1)}, f32[1792]{0:T(1024)}, f32[1792]{0:T(1024)S(1)}, /*index=5*/f32[512,1792]{0,1:T(8,128)}) fusion(f32[512,1792]{0,1:T(8,128)} %slice.402, f32[3,1792]{0,1:T(8,128)} %copy.500, f32[512,3352]{0,1:T(8,128)} %copy-done.32, f32[512,1792]{0,1:T(8,128)} %get-tuple-element.674, ...), kind=kLoop, calls=%fused_computation.135 | loop fusion | flops 21093632 | bytes 18407424 | tf_op jit(solution)/shard_map/transpose(jvp())/reduce_sum | solution.py:61
  795.7 10.7 multiply_reduce_fusion.12
  854.7 13.4 %broadcast_multiply_fusion = (f32[512,1792]{0,1:T(8,128)S(1)}, f32[512,1792]{0,1:T(8,128)}, f32[512,1792]{0,1:T(8,128)}, f32[512,1792]{0,1:T(8,128)}, f32[512,17...) fusion(f32[512,1792]{0,1:T(8,128)} %get-tuple-element.664, ...), kind=kLoop, calls=%fused_computation.274 | loop fusion | flops 11010048 | bytes 55078912 | tf_op jit(solution)/shard_map/transpose(jvp())/mul | solution.py:61
  872.3 11.0 pad_add_fusion.3
  885.5 11.0 pad_add_fusion.5
  994.7 11.7 %add_add_fusion = f32[768,3352]{1,0:T(8,128)} fusion(f32[768,3352]{1,0:T(8,128)} %fusion.172, f32[768,3352]{1,0:T(8,128)} %fusion.168, f32[512,3352]{0,1:T(8,128)S(1)} %bitcast.840, f32[512]{0:T(512)S(1)} %copy-done.235, f32[768]{0:T(1024)S(1)} %copy-done.146, bf16[3,1,512,768]{3,2,1,0:T(8,128)(2,1)S(1)} %copy-done.41), kind=kOutput, calls=%fused_computation.39 | convolution fusion | flops 2644557824 | bytes 38549504 | tf_op jit(solution)/shard_map/dot_general | solution.py:138
  1042.7 46.4 %all-reduce.80 = (f32[768]{0:T(1024)S(1)}, f32[4,1792]{1,0:T(4,128)S(1)}, f32[1792]{0:T(1024)S(1)}, f32[24]{0:T(128)}, f32[24]{0:T(128)}, /*index=5*/f32[24]{0:T(128)}, f32[1536]{0:T(1024)S(1)}) all-reduce(f32[768]{0:T(1024)S(1)} %add_add_fusion.14, ...), channel_id=2, replica_groups=mesh['dp'=8,'seq'=4] {'dp','seq'}, use_global_device_ids=true, to_apply=%region_78.80.clone | all-reduce | flops 11336 | bytes 90688
  1097.4 56.0 %reduce-scatter.8.cloned.1.call-done = f32[24,3352]{1,0:T(8,128)} async-done(((f32[768,3352]{1,0:T(8,128)}), f32[24,3352]{1,0:T(8,128)}) %reduce-scatter.8.cloned.1.call-update) | async-done | bytes 321808
  (980 shorter events, 695.4 us)
Async XLA Ops:
  7.2 92.5 %all-gather.13.cloned.1.call-start = ((), (), s32[]{:S(2)}) async-start(), calls=%async_computation.2 | async-start | bytes 5474304 | tf_op jit(solution)/shard_map/all_gather | solution.py:186
  9.1 226.3 %all-gather.17.cloned.1.call-start = ((), (), s32[]{:S(2)}) async-start(), calls=%async_computation.4 | async-start | bytes 2433024 | tf_op jit(solution)/shard_map/all_gather | solution.py:187
  10.7 299.9 %all-gather.21.cloned.1.call-start = ((), (), s32[]{:S(2)}) async-start(), calls=%async_computation.6 | async-start | bytes 3932160 | tf_op jit(solution)/shard_map/all_gather | solution.py:35
  11.5 117.7 %copy-start.251 = (f32[24]{0:T(128)}, f32[24]{0:T(128)S(1)}, u32[]{:S(2)}) copy-start(f32[24]{0:T(128)S(1)} %exponential_negate_fusion) | copy-start | bytes 292
  108.7 29.8 %collective-permute-start.2 = (f32[3,1792]{1,0:T(4,128)S(1)}, f32[3,1792]{1,0:T(4,128)S(1)}, u32[]{:S(2)}, u32[]{:S(2)}) collective-permute-start(f32[3,1792]{1,0:T(4,128)S(1)} %copy.528), channel_id=1, source_target_pairs={{0,1},{1,2},{2,3},{4,5},{5,6},{6,7},{8,9},{9,10},{10,11},{12,13},{... | collective-permute-start | bytes 64520 | tf_op jit(solution)/shard_map/ppermute | solution.py:28
  129.2 111.3 %copy-start.106 = (f32[512,24]{0,1:T(8,128)}, f32[512,24]{0,1:T(8,128)S(1)}, u32[]{:S(2)}) copy-start(f32[512,24]{0,1:T(8,128)S(1)} %get-tuple-element.779) | copy-start | bytes 147460
  129.2 112.0 %copy-start.104 = (f32[512,24]{0,1:T(8,128)}, f32[512,24]{0,1:T(8,128)S(1)}, u32[]{:S(2)}) copy-start(f32[512,24]{0,1:T(8,128)S(1)} %get-tuple-element.781) | copy-start | bytes 147460
  159.4 158.6 %copy-start = (f32[2,256,24,64]{1,0,3,2:T(2,128)}, f32[2,256,24,64]{1,0,3,2:T(2,128)S(1)}, u32[]{:S(2)}) copy-start(f32[2,256,24,64]{1,0,3,2:T(2,128)S(1)} %reshape.819) | copy-start | bytes 9437188
  164.7 174.5 %all-gather.15.cloned.1.call-start = ((), (), s32[]{:S(2)}) async-start(), calls=%async_computation.3 | async-start | bytes 3932160 | tf_op jit(solution)/shard_map/all_gather | solution.py:35
  171.0 20.1 %collective-permute-start.1 = (f32[3,1792]{1,0:T(4,128)S(1)}, f32[3,1792]{1,0:T(4,128)S(1)}, u32[]{:S(2)}, u32[]{:S(2)}) collective-permute-start(f32[3,1792]{1,0:T(4,128)S(1)} %copy.514), channel_id=1, source_target_pairs={{0,1},{1,2},{2,3},{4,5},{5,6},{6,7},{8,9},{9,10},{10,11},{12,13},{... | collective-permute-start | bytes 64520 | tf_op jit(solution)/shard_map/ppermute | solution.py:28
  178.8 13.6 %collective-permute-start = (f32[3,1792]{1,0:T(4,128)S(1)}, f32[3,1792]{1,0:T(4,128)S(1)}, u32[]{:S(2)}, u32[]{:S(2)}) collective-permute-start(f32[3,1792]{1,0:T(4,128)S(1)} %copy.499), channel_id=1, source_target_pairs={{0,1},{1,2},{2,3},{4,5},{5,6},{6,7},{8,9},{9,10},{10,11},{12,13},{... | collective-permute-start | bytes 64520 | tf_op jit(solution)/shard_map/ppermute | solution.py:28
  234.0 130.7 %all-gather.19.cloned.1.call-start = ((), (), s32[]{:S(2)}) async-start(), calls=%async_computation.5 | async-start | bytes 3932160 | tf_op jit(solution)/shard_map/all_gather | solution.py:35
  265.9 106.1 %copy-start.138 = (f32[2,256,24]{1,2,0:T(8,128)}, f32[2,256,24]{1,2,0:T(8,128)S(1)}, u32[]{:S(2)}) copy-start(f32[2,256,24]{1,2,0:T(8,128)S(1)} %get-tuple-element.729) | copy-start | bytes 147460
  310.6 184.1 %all-gather.23.cloned.1.call-start = ((), (), s32[]{:S(2)}) async-start(), calls=%async_computation.7 | async-start | bytes 3932160 | tf_op jit(solution)/shard_map/all_gather | solution.py:35
  405.4 191.5 %copy-start.218 = (f32[512]{0:T(512)}, f32[512]{0:T(512)S(1)}, u32[]{:S(2)}) copy-start(f32[512]{0:T(512)S(1)} %fusion.356) | copy-start | bytes 6148
  405.4 194.6 %copy-start.236 = (f32[512]{0:T(512)}, f32[512]{0:T(512)S(1)}, u32[]{:S(2)}) copy-start(f32[512]{0:T(512)S(1)} %fusion.358) | copy-start | bytes 6148
  405.5 209.2 %copy-start.238 = (f32[512]{0:T(512)}, f32[512]{0:T(512)S(1)}, u32[]{:S(2)}) copy-start(f32[512]{0:T(512)S(1)} %fusion.360) | copy-start | bytes 6148
  447.1 77.7 %all-gather.25.cloned.1.call-start = ((), (), s32[]{:S(2)}) async-start(), calls=%async_computation.8 | async-start | bytes 3932160 | tf_op jit(solution)/shard_map/all_gather | solution.py:35
  459.6 346.8 %all-gather.27.cloned.1.call-start = ((), (), s32[]{:S(2)}) async-start(), calls=%async_computation.9 | async-start | bytes 3932160 | tf_op jit(solution)/shard_map/all_gather | solution.py:35
  577.6 519.8 %reduce-scatter.6.cloned.1.call-start = ((), (), s32[]{:S(2)}) async-start(), calls=%async_computation.10 | async-start | bytes 4866048 | tf_op jit(solution)/shard_map/reduce_scatter | solution.py:279
  618.6 534.8 %reduce-scatter.8.cloned.1.call-start = ((), (), s32[]{:S(2)}) async-start(), calls=%async_computation.11 | async-start | bytes 10948608
  920.2 32.9 %collective-permute-start.5 = (f32[3,1792]{1,0:T(4,128)S(1)}, f32[3,1792]{1,0:T(4,128)S(1)}, u32[]{:S(2)}, u32[]{:S(2)}) collective-permute-start(f32[3,1792]{1,0:T(4,128)S(1)} %copy.615), channel_id=1, source_target_pairs={{1,0},{2,1},{3,2},{5,4},{6,5},{7,6},{9,8},{10,9},{11,10},{13,12},{... | collective-permute-start | bytes 64520 | tf_op jit(solution)/shard_map/ppermute | solution.py:28
  927.0 26.5 %collective-permute-start.3 = (f32[3,1792]{1,0:T(4,128)S(1)}, f32[3,1792]{1,0:T(4,128)S(1)}, u32[]{:S(2)}, u32[]{:S(2)}) collective-permute-start(f32[3,1792]{1,0:T(4,128)S(1)} %copy.565), channel_id=1, source_target_pairs={{1,0},{2,1},{3,2},{5,4},{6,5},{7,6},{9,8},{10,9},{11,10},{13,12},{... | collective-permute-start | bytes 64520 | tf_op jit(solution)/shard_map/ppermute | solution.py:28
  935.1 34.2 %collective-permute-start.4 = (f32[3,1792]{1,0:T(4,128)S(1)}, f32[3,1792]{1,0:T(4,128)S(1)}, u32[]{:S(2)}, u32[]{:S(2)}) collective-permute-start(f32[3,1792]{1,0:T(4,128)S(1)} %copy.590), channel_id=1, source_target_pairs={{1,0},{2,1},{3,2},{5,4},{6,5},{7,6},{9,8},{10,9},{11,10},{13,12},{... | collective-permute-start | bytes 64520 | tf_op jit(solution)/shard_map/ppermute | solution.py:28
  (291 other events, 3686.2 us)
Sparse Core Ops, SparseCore 0:
  11.5 68.9 all-gather.12
  84.0 56.0 all-gather.16
  164.8 29.1 all-gather.20
  234.1 27.5 all-gather.14
  310.7 27.4 all-gather.18
  447.2 47.4 all-gather.22
  496.2 28.4 all-gather.24
  577.7 28.4 all-gather.26
  618.7 107.5 reduce-scatter.5
  1006.7 146.5 reduce-scatter.7
where the time goes:
time: 1170 us; the launch traced here: 1160 us
  matrix products  361 us (31%)
  other arithmetic  310 us (26%)
  local copies, waits for them, and re-layouts  249 us (21%)
  blocking collectives  144 us (12%)
  waiting for transfers between devices  63.4 us (5%)
  between operations  18 us (2%)
  starting transfers between devices  13.8 us (1%)
    dot_general x9, matrix products, out_part(): jnp.einsum('khts,kshp->kthp', mixing, input_blocks, precision=PRECISE)  145 us
    unnamed x2, blocking collectives  83.8 us
    unnamed x618, local copies, waits for them, and re-layouts  62.4 us
    unnamed x11, waiting for transfers between devices  56.1 us
    dot_general x6, matrix products, contract_cols(): lax.dot_general(left, right, (((1,), (1,)), ((), ())), preferred_element_...  50.2 us
    another operation x27, other arithmetic  49.1 us
    dot_general x9, matrix products, out_part(): jnp.einsum('ktn,khpn->kthp', c_blocks, start_states, precision=PRECISE)  45.1 us
    all_gather x1, blocking collectives, local(): lax.all_gather(conv_weight, ('dp', 'seq'), axis=1, tiled=True)  43.7 us
  transfers between devices with their start and end apart: 16, of which 3 were waited for; matrix products, arithmetic and copies ran while one was open for 65% of the time, Pallas kernels for 0%

commit v1 on v0

v1 whole, which is shorter than its diff:
```python
from functools import partial

import jax
import jax.numpy as jnp
from jax import lax
from jax.experimental import pallas as pl
from jax.experimental.pallas import tpu as pltpu
from jax.sharding import PartitionSpec as P

D = 768
NH = 24
HD = 64
NS = 128
DCONV = 4
CL = 128
DI = 1536
XBC = 1792
PROJ = 3352
XD = 1920
LN = 128
EPSILON = 1e-05

F32 = jnp.float32
BF = jnp.bfloat16
SROWS = 144


def nn(a, b):
    return lax.dot_general(a, b, (((1,), (0,)), ((), ())), preferred_element_type=F32)


def nt(a, b):
    return lax.dot_general(a, b, (((1,), (1,)), ((), ())), preferred_element_type=F32)


def tn(a, b):
    return lax.dot_general(a, b, (((0,), (0,)), ((), ())), preferred_element_type=F32)


def exact_nn(a, b):
    return lax.dot_general(
        a, b, (((1,), (0,)), ((), ())), precision=lax.Precision.HIGHEST, preferred_element_type=F32
    )


def sigmoid(v):
    return 0.5 * jnp.tanh(0.5 * v) + 0.5


def halves(v):
    top = v.astype(BF)
    return top, (v - top.astype(F32)).astype(BF)


def three(op, a, b):
    ah, al = halves(a)
    bh, bl = halves(b)
    return op(ah, bh) + op(al, bh) + op(ah, bl)


def expander():
    head = lax.broadcasted_iota(jnp.int32, (LN, DI), 0)
    lane = lax.broadcasted_iota(jnp.int32, (LN, DI), 1)
    return jnp.where(head == lane // HD, 1.0, 0.0).astype(BF)


def expand(v, e):
    top, low = halves(v)
    return nn(top, e) + nn(low, e)


def lower_mask(strict):
    row = lax.broadcasted_iota(jnp.int32, (CL, CL), 0)
    col = lax.broadcasted_iota(jnp.int32, (CL, CL), 1)
    return row > col if strict else row >= col


def half_masks():
    lane = lax.broadcasted_iota(jnp.int32, (1, 2 * HD), 1)
    left = jnp.where(lane < HD, 1.0, 0.0).astype(BF)
    right = jnp.where(lane < HD, 0.0, 1.0).astype(BF)
    return left, right


def lanes(j):
    return slice(j * LN, (j + 1) * LN)


def conv_running(ext, cw, cb):
    total = cb
    for tap in range(DCONV):
        total = total + ext[5 + tap : 5 + tap + CL] * cw[tap : tap + 1]
    return total


def project_kernel(
    vlen_ref,
    x_ref,
    xh_ref,
    g_ref,
    w_ref,
    cw_ref,
    cb_ref,
    dtb_ref,
    rate_ref,
    nrm_ref,
    ci_ref,
    act_ref,
    step_ref,
    l_ref,
    sig_ref,
    sloc_ref,
    s_ref,
    nx,
    xw,
    state,
    *,
    first,
):
    piece = x_ref.shape[0]
    chunks = piece // CL
    valid = vlen_ref[first + pl.program_id(0)]

    def norm(v):
        v = v.astype(F32)
        r = lax.rsqrt(jnp.mean(v * v, axis=-1, keepdims=True) + EPSILON)
        return (v * r * g_ref[...]).astype(BF)

    nx[0:16] = norm(xh_ref[...])

    def norm_rows(i, c):
        rows = pl.ds(pl.multiple_of(i * 64, 64), 64)
        v = norm(x_ref[rows, :])
        nx[pl.ds(pl.multiple_of(i * 64 + 16, 16), 64), :] = v
        nrm_ref[rows, :] = v
        return c

    lax.fori_loop(0, piece // 64, norm_rows, 0)

    for j in range(XBC // 256):
        cols = slice(j * 256, (j + 1) * 256)
        ci_ref[:, cols] = nn(nx[...], w_ref[:, cols])[8:]
    dt_raw = nn(nx[16:], w_ref[:, XBC:]) + dtb_ref[...]
    row = lax.broadcasted_iota(jnp.int32, (piece, LN), 0)
    mask = jnp.where(row < valid, 1.0, 0.0)
    step_ref[...] = (jnp.maximum(dt_raw, 0.0) + jnp.log1p(jnp.exp(-jnp.abs(dt_raw)))) * mask
    sig_ref[...] = mask / (1.0 + jnp.exp(-dt_raw))

    e = expander()
    tri = jnp.where(lower_mask(False), 1.0, 0.0)
    state[...] = jnp.zeros_like(state)

    def chunk(k, total):
        base = pl.multiple_of(k * CL, CL)
        rows = pl.ds(base, CL)
        step = step_ref[rows, :]
        ld = exact_nn(tri, step * rate_ref[...])
        l_ref[rows, :] = ld
        end = ld[CL - 1 :]
        tail = expand(step * jnp.exp(end - ld), e)
        for j in range(XBC // LN):
            ext = ci_ref[pl.ds(base, CL + 8), lanes(j)]
            run = conv_running(ext, cw_ref[:, lanes(j)], cb_ref[:, lanes(j)])
            act = run * sigmoid(run)
            act_ref[rows, lanes(j)] = act
            if j < DI // LN:
                xw[:, lanes(j)] = (act * tail[:, lanes(j)]).astype(BF)
        b = act_ref[rows, DI : DI + NS].astype(BF)
        sloc_ref[k] = state[...].astype(BF)
        keep = expand(jnp.exp(jnp.broadcast_to(end, (8, LN))), e)[0:1]
        state[...] = keep * state[...] + tn(b, xw[...])
        return total + end

    total = lax.fori_loop(0, chunks, chunk, jnp.zeros((1, LN), F32))
    s_ref[0:NS] = state[...].astype(BF)
    keep = expand(jnp.exp(jnp.broadcast_to(total, (8, LN))), e)[0:1]
    top, low = halves(keep)
    s_ref[NS : NS + 16] = jnp.concatenate([top, low, jnp.zeros((14, DI), BF)], axis=0)


def whole(shape):
    return pl.BlockSpec(shape, lambda i: (0,) * len(shape))


def kept(shape):
    return pl.BlockSpec(shape, lambda i: (0,) * len(shape), pipeline_mode=pl.Buffered(1))


def per(shape, first=0, **mode):
    rest = (0,) * len(shape)
    return pl.BlockSpec((None,) + shape, lambda i: (first + i,) + rest, **mode)


ONE = dict(pipeline_mode=pl.Buffered(1))


SMEM = pl.BlockSpec(memory_space=pltpu.SMEM)
LIMIT = 67_000_000


def project(first, count, valid, tokens, halo, gain, w_xd, cw, cb, dtb, rate):
    piece = tokens.shape[1]
    chunks = piece // CL
    sds = jax.ShapeDtypeStruct
    return pl.pallas_call(
        partial(project_kernel, first=first),
        grid=(count,),
        in_specs=[
            SMEM,
            per((piece, D), first),
            per((16, D), first),
            whole((1, D)),
            kept((D, XD)),
            whole((DCONV, XBC)),
            whole((1, XBC)),
            whole((1, LN)),
            whole((1, LN)),
        ],
        out_specs=[
            per((piece, D)),
            per((piece + 8, XBC)),
            per((piece, XBC)),
            per((piece, LN)),
            per((piece, LN)),
            per((piece, LN)),
            per((chunks, NS, DI)),
            per((SROWS, DI)),
        ],
        out_shape=[
            sds((count, piece, D), BF),
            sds((count, piece + 8, XBC), F32),
            sds((count, piece, XBC), F32),
            sds((count, piece, LN), F32),
            sds((count, piece, LN), F32),
            sds((count, piece, LN), F32),
            sds((count, chunks, NS, DI), BF),
            sds((count, SROWS, DI), BF),
        ],
        scratch_shapes=[
            pltpu.VMEM((piece + 16, D), BF),
            pltpu.VMEM((CL, DI), BF),
            pltpu.VMEM((NS, DI), F32),
        ],
        compiler_params=pltpu.CompilerParams(vmem_limit_bytes=LIMIT),
        name="project",
    )(valid, tokens, halo, gain, w_xd, cw, cb, dtb, rate)


def mix_kernel(
    vlen_ref,
    place_ref,
    x_ref,
    cot_ref,
    nrm_ref,
    act_ref,
    step_ref,
    l_ref,
    sloc_ref,
    sg_ref,
    wz_ref,
    wo_ref,
    gg_ref,
    dsk_ref,
    out_ref,
    gn_ref,
    dbr_ref,
    dz_ref,
    dy_ref,
    y_ref,
    sst_ref,
    dsin_ref,
    ggrad_ref,
    zs,
    dgn,
    incoming,
    dsacc,
    yf,
    work,
    *,
    first,
    places,
):
    piece = x_ref.shape[0]
    chunks = piece // CL
    valid = vlen_ref[first + pl.program_id(0)]
    place = place_ref[0]

    @pl.when(pl.program_id(0) == 0)
    def _():
        ggrad_ref[...] = jnp.zeros_like(ggrad_ref)

    incoming[...] = jnp.zeros_like(incoming)
    for j in range(places - 1):

        @pl.when(j < place)
        def _():
            keep = sg_ref[j, NS : NS + 1].astype(F32) + sg_ref[j, NS + 1 : NS + 2].astype(F32)
            incoming[...] = keep * incoming[...] + sg_ref[j, 0:NS].astype(F32)

    row = lax.broadcasted_iota(jnp.int32, (piece, 1), 0)
    live = row < valid
    dbr_ref[...] = jnp.where(live, cot_ref[...].astype(F32), 0.0).astype(BF)
    for j in range(DI // 256):
        cols = slice(j * 256, (j + 1) * 256)
        zs[:, cols] = nn(nrm_ref[...], wz_ref[:, cols])
        dgn[:, cols] = nt(dbr_ref[...], wo_ref[cols, :])

    e = expander()
    low = lower_mask(False)
    left, right = half_masks()
    dsacc[...] = jnp.zeros_like(dsacc)

    def chunk(k, prefix):
        base = pl.multiple_of(k * CL, CL)
        rows = pl.ds(base, CL)
        step = step_ref[rows, :]
        ld = l_ref[rows, :]
        ldt = ld.T
        end = ld[CL - 1 :]
        before = expand(jnp.exp(jnp.broadcast_to(prefix, (8, LN))), e)[0:1]
        startf = before * incoming[...] + sloc_ref[k].astype(F32)
        start = startf.astype(BF)
        sst_ref[k] = startf
        step_e = expand(step, e)
        grow = expand(jnp.exp(ld), e)
        b = act_ref[rows, DI : DI + NS].astype(BF)
        c, c_low = halves(act_ref[rows, DI + NS :])
        scores = jnp.where(low, nt(c, b), 0.0)
        squares = jnp.zeros((CL, LN), F32)
        for j in range(DI // LN):
            x = act_ref[rows, lanes(j)]
            xd = (x * step_e[:, lanes(j)]).astype(BF)
            mixes = []
            for h in (2 * j, 2 * j + 1):
                gap = jnp.minimum(ld[:, h : h + 1] - ldt[h : h + 1, :], 0.0)
                mixes.append((jnp.exp(gap) * scores).astype(BF))
            block = jnp.concatenate([xd * left, xd * right], axis=0)
            st = start[:, lanes(j)]
            y = nn(jnp.concatenate(mixes, axis=1), block) + (nn(c, st) + nn(c_low, st)) * grow[:, lanes(j)]
            y_ref[rows, lanes(j)] = y
            full = y + dsk_ref[:, lanes(j)] * x
            yf[:, lanes(j)] = full
            z = zs[rows, lanes(j)]
            u = full * (z * sigmoid(z))
            squares = squares + u * u
        r = lax.rsqrt(jnp.sum(squares, axis=-1, keepdims=True) * (1.0 / DI) + EPSILON)
        inner = jnp.zeros((CL, LN), F32)
        for j in range(DI // LN):
            z = zs[rows, lanes(j)]
            v = yf[:, lanes(j)] * (z * sigmoid(z)) * r
            gain = gg_ref[:, lanes(j)]
            gn_ref[rows, lanes(j)] = (v * gain).astype(BF)
            dg = dgn[rows, lanes(j)]
            gv = dg * v
            ggrad_ref[:, lanes(j)] += jnp.sum(gv.reshape(CL // 8, 8, LN), axis=0)
            inner = inner + gv * gain
        q = jnp.sum(inner, axis=-1, keepdims=True) * (1.0 / DI)
        for j in range(DI // LN):
            z = zs[rows, lanes(j)]
            s = sigmoid(z)
            sz = z * s
            full = yf[:, lanes(j)]
            v = full * sz * r
            du = r * (dgn[rows, lanes(j)] * gg_ref[:, lanes(j)] - v * q)
            dy = du * sz
            dy_ref[rows, lanes(j)] = dy
            dz_ref[rows, lanes(j)] = (du * full * (s + sz * (1.0 - s))).astype(BF)
            work[:, lanes(j)] = (dy * grow[:, lanes(j)]).astype(BF)
        dsacc[...] += before * tn(c, work[...])
        return prefix + end

    lax.fori_loop(0, chunks, chunk, jnp.zeros((1, LN), F32))
    dsin_ref[...] = dsacc[...].astype(BF)
    for j in range(D // 256):
        cols = slice(j * 256, (j + 1) * 256)
        branch = nn(gn_ref[...], wo_ref[:, cols])
        out_ref[:, cols] = jnp.where(live, x_ref[:, cols].astype(F32) + branch, 0.0).astype(BF)


def mix(first, count, valid, place, tokens, cot, normed, act, step, ld, sloc, gathered, w_z, w_o, gg, dsk):
    piece = tokens.shape[1]
    chunks = piece // CL
    places = gathered.shape[0]
    sds = jax.ShapeDtypeStruct
    return pl.pallas_call(
        partial(mix_kernel, first=first, places=places),
        grid=(count,),
        in_specs=[
            SMEM,
            SMEM,
            per((piece, D), first),
            per((piece, D), first),
            per((piece, D)),
            per((piece, XBC), **ONE),
            per((piece, LN)),
            per((piece, LN)),
            per((chunks, NS, DI), **ONE),
            pl.BlockSpec((places, None, SROWS, DI), lambda i: (0, i, 0, 0), **ONE),
            kept((D, DI)),
            kept((DI, D)),
            whole((1, DI)),
            whole((1, DI)),
        ],
        out_specs=[
            per((piece, D)),
            per((piece, DI)),
            per((piece, D)),
            per((piece, DI)),
            per((piece, DI)),
            per((piece, DI)),
            per((chunks, NS, DI)),
            per((NS, DI)),
            whole((8, DI)),
        ],
        out_shape=[
            sds((count, piece, D), BF),
            sds((count, piece, DI), BF),
            sds((count, piece, D), BF),
            sds((count, piece, DI), BF),
            sds((count, piece, DI), F32),
            sds((count, piece, DI), F32),
            sds((count, chunks, NS, DI), F32),
            sds((count, NS, DI), BF),
            sds((8, DI), F32),
        ],
        scratch_shapes=[
            pltpu.VMEM((piece, DI), F32),
            pltpu.VMEM((piece, DI), F32),
            pltpu.VMEM((NS, DI), F32),
            pltpu.VMEM((NS, DI), F32),
            pltpu.VMEM((CL, DI), F32),
            pltpu.VMEM((CL, DI), BF),
        ],
        compiler_params=pltpu.CompilerParams(vmem_limit_bytes=LIMIT),
        name="mix",
    )(valid, place, tokens, cot, normed, act, step, ld, sloc, gathered, w_z, w_o, gg, dsk)


def scan_back_kernel(
    place_ref,
    ci_ref,
    step_ref,
    l_ref,
    sig_ref,
    dy_ref,
    y_ref,
    sst_ref,
    dsg_ref,
    keep_ref,
    cw_ref,
    cb_ref,
    rate_ref,
    dsk_ref,
    dxd_ref,
    fix_ref,
    edge_ref,
    cgrad_ref,
    hgrad_ref,
    skip_ref,
    ds,
    xa,
    dsl,
    dact,
    xdt,
    xt,
    dr,
    *,
    places,
):
    piece = dy_ref.shape[0]
    chunks = piece // CL
    place = place_ref[0]

    @pl.when(pl.program_id(0) == 0)
    def _():
        cgrad_ref[...] = jnp.zeros_like(cgrad_ref)
        hgrad_ref[...] = jnp.zeros_like(hgrad_ref)
        skip_ref[...] = jnp.zeros_like(skip_ref)

    ds[...] = jnp.zeros_like(ds)
    for j in reversed(range(1, places)):

        @pl.when(j > place)
        def _():
            keep = keep_ref[j, 0:1].astype(F32) + keep_ref[j, 1:2].astype(F32)
            ds[...] = keep * ds[...] + dsg_ref[j].astype(F32)

    e = expander()
    upper = jnp.logical_not(lower_mask(True))
    upper_one = jnp.where(upper, 1.0, 0.0)
    before_one = jnp.where(lower_mask(True), 1.0, 0.0)
    left, right = half_masks()
    dr[CL:] = jnp.zeros((8, XBC), F32)

    def chunk(i, carry):
        k = chunks - 1 - i
        base = pl.multiple_of(k * CL, CL)
        rows = pl.ds(base, CL)
        step = step_ref[rows, :]
        ld = l_ref[rows, :]
        ldt = ld.T
        end = ld[CL - 1 :]
        step_e = expand(step, e)
        grow = expand(jnp.exp(ld), e)
        tail = expand(jnp.exp(end - ld), e)
        keep = expand(jnp.exp(jnp.broadcast_to(end, (8, LN))), e)[0:1]
        for j in range(XBC // LN):
            ext = ci_ref[pl.ds(base, CL + 8), lanes(j)]
            run = conv_running(ext, cw_ref[:, lanes(j)], cb_ref[:, lanes(j)])
            s = sigmoid(run)
            a = run * s
            xa[:, lanes(j)] = a
            dsl[:, lanes(j)] = s + a * (1.0 - s)
            if j < DI // LN:
                xd = a * step_e[:, lanes(j)]
                xdt[:, lanes(j)] = xd
                xt[:, lanes(j)] = xd * tail[:, lanes(j)]
        b = xa[:, DI : DI + NS].astype(BF)
        c = xa[:, DI + NS :].astype(BF)
        scores = jnp.where(upper, nt(b, c), 0.0)
        dsb = ds[...].astype(BF)
        start = sst_ref[k]
        dscores = jnp.zeros((CL, CL), F32)
        db = three(nt, xt[...], ds[...])
        dc = jnp.zeros((CL, NS), F32)
        r_u = jnp.zeros((CL, LN), F32)
        r_f = jnp.zeros((CL, LN), F32)
        r_v = jnp.zeros((CL, LN), F32)
        r_c = jnp.zeros((8, LN), F32)
        for j in range(DI // LN):
            et = e[:, lanes(j)]
            dyf = dy_ref[rows, lanes(j)]
            dyb, dyl = halves(dyf)
            block = jnp.concatenate([dyb * left, dyb * right], axis=0)
            xdb, xdl = halves(xdt[:, lanes(j)])
            dmix = nt(xdb, block)
            dmix = dmix + nt(xdl, block) + nt(xdb, jnp.concatenate([dyl * left, dyl * right], axis=0))
            mixes = []
            for p, h in enumerate((2 * j, 2 * j + 1)):
                gap = jnp.minimum(ldt[h : h + 1, :] - ld[:, h : h + 1], 0.0)
                w = jnp.exp(gap)
                mixes.append((w * scores).astype(BF))
                dscores = dscores + dmix[:, lanes(p)] * w
            diag = nn(jnp.concatenate(mixes, axis=1), block)
            far = nn(b, dsb[:, lanes(j)]) * tail[:, lanes(j)]
            xdf = xdb.astype(F32)
            u_top, u_low = halves(dyb.astype(F32) * y_ref[rows, lanes(j)] - xdf * diag)
            r_u = r_u + nt(u_top, et) + nt(u_low, et)
            r_f = r_f + nt((xdf * far).astype(BF), et)
            dxd = diag + far
            x = xa[:, lanes(j)]
            r_v = r_v + nt((x * dxd).astype(BF), et)
            dact[:, lanes(j)] = dxd * step_e[:, lanes(j)] + dsk_ref[:, lanes(j)] * dyf
            skip_ref[:, lanes(j)] += jnp.sum((dyf * x).reshape(CL // 8, 8, LN), axis=0)
            dygf = dyf * grow[:, lanes(j)]
            dyg = dygf.astype(BF)
            st = start[:, lanes(j)]
            dc = dc + three(nt, dygf, st)
            dsj = ds[:, lanes(j)]
            const = jnp.sum((st * dsj).reshape(NS // 8, 8, LN), axis=0) * keep[:, lanes(j)]
            c_top, c_low = halves(const)
            r_c = r_c + nt(c_top, et) + nt(c_low, et)
            ds[:, lanes(j)] = keep[:, lanes(j)] * dsj + tn(c, dyg)
        dsc = jnp.where(upper, dscores, 0.0).astype(BF)
        dact[:, DI : DI + NS] = db + nn(dsc, c)
        dact[:, DI + NS :] = dc + tn(dsc, b)
        da = exact_nn(upper_one, r_u) + exact_nn(before_one, r_f) + jnp.sum(r_c, axis=0, keepdims=True)
        dstep = r_v + rate_ref[...] * da
        ddt = dstep * sig_ref[rows, :]
        hgrad_ref[0:8] += jnp.sum(ddt.reshape(CL // 8, 8, LN), axis=0)
        hgrad_ref[8:16] += jnp.sum((da * step).reshape(CL // 8, 8, LN), axis=0)
        dxd_ref[rows, XBC:] = ddt.astype(BF)
        for j in range(XBC // LN):
            g = dact[:, lanes(j)] * dsl[:, lanes(j)]
            dr[0:CL, lanes(j)] = g
            ext = ci_ref[pl.ds(base, CL + 8), lanes(j)]
            gext = dr[:, lanes(j)]
            total = jnp.zeros((CL, LN), F32)
            for tap in range(DCONV):
                total = total + gext[DCONV - 1 - tap : DCONV - 1 - tap + CL] * cw_ref[tap : tap + 1, lanes(j)]
                part = g * ext[5 + tap : 5 + tap + CL]
                cgrad_ref[8 * tap : 8 * tap + 8, lanes(j)] += jnp.sum(part.reshape(CL // 8, 8, LN), axis=0)
            cgrad_ref[32:40, lanes(j)] += jnp.sum(g.reshape(CL // 8, 8, LN), axis=0)
            dxd_ref[rows, lanes(j)] = total.astype(BF)

            @pl.when(i == 0)
            def _():
                fix_ref[:, lanes(j)] = total[CL - 16 :]

            dr[CL:, lanes(j)] = g[0:8]
        return carry

    lax.fori_loop(0, chunks, chunk, 0)
    edge_ref[...] = dr[CL:]


def scan_back(count, place, ci, step, ld, sig, dy, y, sst, dsg, gathered, cw, cb, rate, dsk):
    piece = dy.shape[1]
    chunks = piece // CL
    places = gathered.shape[0]
    sds = jax.ShapeDtypeStruct
    return pl.pallas_call(
        partial(scan_back_kernel, places=places),
        grid=(count,),
        in_specs=[
            SMEM,
            per((piece + 8, XBC)),
            per((piece, LN)),
            per((piece, LN)),
            per((piece, LN)),
            per((piece, DI)),
            per((piece, DI)),
            per((chunks, NS, DI)),
            pl.BlockSpec((places, None, NS, DI), lambda i: (0, i, 0, 0), **ONE),
            pl.BlockSpec((places, None, 16, DI), lambda i: (0, i, NS // 16, 0)),
            whole((DCONV, XBC)),
            whole((1, XBC)),
            whole((1, LN)),
            whole((1, DI)),
        ],
        out_specs=[
            per((piece, XD)),
            per((16, XBC)),
            per((8, XBC)),
            whole((40, XBC)),
            whole((16, LN)),
            whole((8, DI)),
        ],
        out_shape=[
            sds((count, piece, XD), BF),
            sds((count, 16, XBC), F32),
            sds((count, 8, XBC), F32),
            sds((40, XBC), F32),
            sds((16, LN), F32),
            sds((8, DI), F32),
        ],
        scratch_shapes=[
            pltpu.VMEM((NS, DI), F32),
            pltpu.VMEM((CL, XBC), F32),
            pltpu.VMEM((CL, XBC), F32),
            pltpu.VMEM((CL, XBC), F32),
            pltpu.VMEM((CL, DI), F32),
            pltpu.VMEM((CL, DI), F32),
            pltpu.VMEM((CL + 8, XBC), F32),
        ],
        compiler_params=pltpu.CompilerParams(vmem_limit_bytes=LIMIT),
        name="scan_back",
    )(place, ci, step, ld, sig, dy, y, sst, dsg, gathered, cw, cb, rate, dsk)


def input_grad_kernel(x_ref, dbr_ref, g_ref, dz_ref, dxd_ref, wz_ref, wx_ref, out_ref, gain_ref, dn):
    piece = x_ref.shape[0]

    @pl.when(pl.program_id(0) == 0)
    def _():
        gain_ref[...] = jnp.zeros_like(gain_ref)

    for j in range(D // 256):
        cols = slice(j * 256, (j + 1) * 256)
        dn[:, cols] = nt(dz_ref[...], wz_ref[cols, :]) + nt(dxd_ref[...], wx_ref[cols, :])

    def rows_of(i, c):
        rows = pl.ds(pl.multiple_of(i * 64, 64), 64)
        x = x_ref[rows, :].astype(F32)
        d = dn[rows, :]
        r = lax.rsqrt(jnp.mean(x * x, axis=-1, keepdims=True) + EPSILON)
        v = x * r
        gain_ref[...] += jnp.sum((d * v).reshape(8, 8, D), axis=0)
        dv = d * g_ref[...]
        q = jnp.mean(dv * v, axis=-1, keepdims=True)
        out_ref[rows, :] = (dbr_ref[rows, :].astype(F32) + r * (dv - v * q)).astype(BF)
        return c

    lax.fori_loop(0, piece // 64, rows_of, 0)


def input_grad(first, count, tokens, dbr, gain, dz, dxd, w_z, w_xd):
    piece = tokens.shape[1]
    sds = jax.ShapeDtypeStruct
    return pl.pallas_call(
        input_grad_kernel,
        grid=(count,),
        in_specs=[
            per((piece, D), first),
            per((piece, D)),
            whole((1, D)),
            per((piece, DI)),
            per((piece, XD)),
            kept((D, DI)),
            kept((D, XD)),
        ],
        out_specs=[per((piece, D)), whole((8, D))],
        out_shape=[sds((count, piece, D), BF), sds((8, D), F32)],
        scratch_shapes=[pltpu.VMEM((piece, D), F32)],
        compiler_params=pltpu.CompilerParams(vmem_limit_bytes=LIMIT),
        name="input_grad",
    )(tokens, dbr, gain, dz, dxd, w_z, w_xd)


MESH_ID = pl.DeviceIdType.MESH


class Here:
    def __init__(self, depth):
        dp, seq = lax.axis_index("dp"), lax.axis_index("seq")
        self.depth = depth
        self.levels = depth.bit_length() - 1
        self.z, self.y = dp // 2, dp % 2
        self.x, self.c = seq // 2, seq % 2
        self.rank = dp * 4 + seq

    def device(self, z=None, y=None, x=None, c=None):
        z = self.z if z is None else z
        y = self.y if y is None else y
        x = self.x if x is None else x
        c = self.c if c is None else c
        return (z * 2 + y, x * 2 + c)

    def across(self, level):
        size = 1 << level
        return self.z + size * (1 - 2 * ((self.z // size) % 2))

    def block(self, level):
        size = 1 << level
        return (self.z // size) * size, size

    def block_across(self, level):
        size = 1 << level
        return (self.z // size) * size + size * (1 - 2 * ((self.z // size) % 2)), size

    def greet(self, ranks):
        barrier = pltpu.get_barrier_semaphore()

        def hail(i, carry):
            other = (self.rank + i) % ranks
            pl.semaphore_signal(
                barrier, inc=1, device_id=(other // 4, other % 4), device_id_type=MESH_ID
            )
            return carry

        lax.fori_loop(1, ranks, hail, 0)
        pl.semaphore_wait(barrier, ranks - 1)


class Copies:
    def __init__(self, send, recv):
        self.send, self.recv, self.made = send, recv, []

    def start(self, pairs, device):
        waits = []
        for source, target, landing in pairs:
            i = len(self.made)
            copy = pltpu.make_async_remote_copy(
                src_ref=source,
                dst_ref=target,
                send_sem=self.send.at[i],
                recv_sem=self.recv.at[i],
                device_id=device,
                device_id_type=MESH_ID,
            )
            copy.start()
            self.made.append(copy)
            waits.append(
                pltpu.make_async_remote_copy(
                    src_ref=source,
                    dst_ref=landing,
                    send_sem=self.send.at[i],
                    recv_sem=self.recv.at[i],
                    device_id=device,
                    device_id_type=MESH_ID,
                )
            )
        return waits

    def finish(self):
        for copy in self.made:
            copy.wait_send()


def arrived(waits):
    for w in waits:
        w.wait_recv()


BOTH = slice(None)


def at(item, z, y, x, c):
    ref, half = item
    index = (z, y, x, c)
    return ref.at[index if half is None else index + (half,)]


def everyone(rank, ranks, source, target, send, recv, own):
    def one(i, starting):
        other = (rank + i) % ranks
        copy = pltpu.make_async_remote_copy(
            src_ref=source(other),
            dst_ref=target(rank),
            send_sem=send.at[i],
            recv_sem=recv.at[i],
            device_id=(other // 4, other % 4),
            device_id_type=MESH_ID,
        )
        return copy

    def begin(i, carry):
        one(i, True).start()
        return carry

    def end(i, carry):
        copy = one(i, False)
        copy.wait_send()
        copy.wait_recv()
        return carry

    def start():
        lax.fori_loop(1, ranks, begin, 0)

    def finish():
        lax.fori_loop(1, ranks, end, 0)

    return start, finish


def gather_stream(here, copies, items, first):
    z, y, x, c = here.z, here.y, here.x, here.c
    a_dev = here.device(x=1 - x) if first == "x" else here.device(y=1 - y)
    b_dev = here.device(y=1 - y) if first == "x" else here.device(x=1 - x)
    sibling = here.device(c=1 - c)
    cores = []

    def a_there(item, zs, core):
        return at(item, zs, y, 1 - x, core) if first == "x" else at(item, zs, 1 - y, x, core)

    def line(item, zs, core):
        return at(item, zs, y, BOTH, core) if first == "x" else at(item, zs, BOTH, x, core)

    def line_there(item, zs, core):
        return at(item, zs, 1 - y, BOTH, core) if first == "x" else at(item, zs, BOTH, 1 - x, core)

    def same(where, zs):
        return [(where(i, zs, c), where(i, zs, c), where(i, zs, 1 - c)) for i in items]

    def to_core(where, zs):
        cores.extend(copies.start(same(where, zs), sibling))

    def mine(item, zs, core):
        return at(item, zs, y, x, core)

    def start_a(zs):
        waits = copies.start([(mine(i, zs, c), mine(i, zs, c), a_there(i, zs, c)) for i in items], a_dev)
        to_core(mine, zs)
        return waits

    def start_b(zs, waits):
        arrived(waits)
        out = copies.start([(line(i, zs, c), line(i, zs, c), line_there(i, zs, c)) for i in items], b_dev)
        to_core(a_there, zs)
        return out

    def end_b(zs, waits):
        arrived(waits)
        to_core(line_there, zs)

    sets = [pl.ds(z, 1)]
    waiting_a, waiting_b = [], []
    for level in range(here.levels):
        base, size = here.block(level)
        far, _ = here.block_across(level)
        own, theirs = pl.ds(base, size), pl.ds(far, size)
        zwait = copies.start(
            [(mine(i, own, c), mine(i, own, c), mine(i, theirs, c)) for i in items],
            here.device(z=here.across(level)),
        )
        waiting_a.append((sets[-1], start_a(sets[-1])))
        sets.append(theirs)
        yield
        if level:
            zs, w = waiting_a.pop(0)
            waiting_b.append((zs, start_b(zs, w)))
            yield
        arrived(zwait)
    waiting_a.append((sets[-1], start_a(sets[-1])))
    while waiting_a:
        yield
        zs, w = waiting_a.pop(0)
        waiting_b.append((zs, start_b(zs, w)))
    while waiting_b:
        yield
        zs, w = waiting_b.pop(0)
        end_b(zs, w)
    yield
    arrived(cores)


def side_by_side(streams):
    streams = list(streams)
    while streams:
        for s in list(streams):
            try:
                next(s)
            except StopIteration:
                streams.remove(s)


def gather_kernel(
    xd_in, z_in, o_in, small_in, xd_out, z_out, o_out, small_out, send, recv, ssend, srecv, place_sem, *, depth, ranks
):
    here = Here(depth)
    z, y, x, c = here.z, here.y, here.x, here.c
    own = []
    for i, (source, target) in enumerate(((xd_in, xd_out), (z_in, z_out), (o_in, o_out))):
        own.append(pltpu.make_async_copy(source, target.at[z, y, x, c], place_sem.at[i]))
    own.append(pltpu.make_async_copy(small_in, small_out.at[here.rank], place_sem.at[3]))
    for copy in own:
        copy.start()
    here.greet(ranks)
    start, finish = everyone(
        here.rank, ranks, lambda other: small_in, lambda rank: small_out.at[rank], ssend, srecv, None
    )
    for copy in own:
        copy.wait()
    copies = Copies(send, recv)
    streams = [
        gather_stream(here, copies, [(xd_out, None), (o_out, 0)], "x"),
        gather_stream(here, copies, [(z_out, None), (o_out, 1)], "y"),
    ]
    start()
    side_by_side(streams)
    finish()
    copies.finish()


def copies_needed(levels):
    return 2 * 2 * (levels + 5 * (levels + 1))


def gather(xd, wz, wo, small, depth):
    ranks = depth * 8
    lead = (depth, 2, 2, 2)
    sds = jax.ShapeDtypeStruct
    n = copies_needed(depth.bit_length() - 1)
    any_space = pl.BlockSpec(memory_space=pl.ANY)
    in_vmem = pl.BlockSpec(memory_space=pltpu.VMEM)
    dma = pltpu.SemaphoreType.DMA
    return pl.pallas_call(
        partial(gather_kernel, depth=depth, ranks=ranks),
        in_specs=[in_vmem] * 4,
        out_specs=[any_space] * 4,
        out_shape=[sds(lead + a.shape, a.dtype) for a in (xd, wz, wo)] + [sds((ranks,) + small.shape, small.dtype)],
        scratch_shapes=[dma((n,)), dma((n,)), dma((ranks,)), dma((ranks,)), dma((4,))],
        compiler_params=pltpu.CompilerParams(collective_id=0, has_side_effects=True),
        name="gather",
    )(xd, wz, wo, small)


def reduce_stream(here, copies, items, first):
    z, y, x, c = here.z, here.y, here.x, here.c
    one_dev = here.device(y=1 - y) if first == "y" else here.device(x=1 - x)
    two_dev = here.device(x=1 - x) if first == "y" else here.device(y=1 - y)
    sibling = here.device(c=1 - c)

    def part(item, zs, core):
        return at((item[0], item[1]), zs, BOTH, BOTH, core)

    def keep_line(zs):
        return (zs, y, BOTH) if first == "y" else (zs, BOTH, x)

    def give_line(zs):
        return (zs, 1 - y, BOTH) if first == "y" else (zs, BOTH, 1 - x)

    def give_one(zs):
        return (zs, y, 1 - x) if first == "y" else (zs, 1 - y, x)

    def keep_one(zs):
        return (zs, y, x)

    sets = []
    for level in reversed(range(here.levels)):
        far, size = here.block_across(level)
        sets.append((far, size))
    sets.append((z, 1))

    def slots(zs):
        return pl.ds(zs[0], zs[1])

    def over(zs, body):
        for k in range(zs[1]):
            body(zs[0] + k)

    def core_phase(zs):
        s = slots(zs)
        return copies.start([(part(i, s, 1 - c), i[3].at[s], i[3].at[s]) for i in items], sibling)

    def line_phase(zs, waits):
        arrived(waits)

        def add(k):
            for item in items:
                for a in range(2):
                    for b in range(2):
                        index = (k, a, b, c) if item[1] is None else (k, a, b, c, item[1])
                        item[2][k, a, b] = (item[0][index].astype(F32) + item[3][k, a, b].astype(F32)).astype(BF)

        over(zs, add)
        s = slots(zs)
        return copies.start([(i[2].at[give_line(s)], i[4].at[s], i[4].at[s]) for i in items], one_dev)

    def side_phase(zs, waits):
        arrived(waits)

        def add(k):
            for item in items:
                for a in range(2):
                    index = (k, y, a) if first == "y" else (k, a, x)
                    item[2][index] = (item[2][index].astype(F32) + item[4][k, a].astype(F32)).astype(BF)

        over(zs, add)
        s = slots(zs)
        return copies.start([(i[2].at[give_one(s)], i[5].at[s], i[5].at[s]) for i in items], two_dev)

    def last_phase(zs, waits):
        arrived(waits)

        def add(k):
            for item in items:
                item[2][k, y, x] = (item[2][k, y, x].astype(F32) + item[5][k].astype(F32)).astype(BF)

        over(zs, add)

    cores = [core_phase(zs) for zs in sets]
    yield
    lines, sides = [], []
    n = len(sets)
    for step in range(n + 2):
        if step < n:
            lines.append(line_phase(sets[step], cores[step]))
            yield
        if 1 <= step <= n:
            sides.append(side_phase(sets[step - 1], lines[step - 1]))
            yield
        if step >= 2:
            last_phase(sets[step - 2], sides[step - 2])
            if step == 2:
                level = here.levels - 1
                far, size = here.block_across(level)
                base, _ = here.block(level)
                s, own = pl.ds(far, size), pl.ds(base, size)
                zwait = copies.start(
                    [(i[2].at[s, y, x], i[6][0].at[0:size], i[6][0].at[0:size]) for i in items],
                    here.device(z=here.across(level)),
                )
            yield
    for depth_at, level in enumerate(reversed(range(here.levels))):
        size = 1 << level
        base, _ = here.block(level)
        arrived(zwait)
        for k in range(size):
            for item in items:
                got = item[6][depth_at][k].astype(F32) + item[2][base + k, y, x].astype(F32)
                if level:
                    item[2][base + k, y, x] = got.astype(BF)
                else:
                    item[7](got)
        if level:
            size = 1 << (level - 1)
            far, _ = here.block_across(level - 1)
            zwait = copies.start(
                [
                    (i[2].at[pl.ds(far, size), y, x], i[6][depth_at + 1].at[0:size], i[6][depth_at + 1].at[0:size])
                    for i in items
                ],
                here.device(z=here.across(level - 1)),
            )
            yield


def reduce_kernel(*refs, depth, ranks, names):
    here = Here(depth)
    levels = here.levels
    count = len(names)
    parts = refs[:count]
    small_in = refs[count]
    outs = refs[count + 1 : 2 * count + 1]
    small_out = refs[2 * count + 1]
    scratch = list(refs[2 * count + 2 :])
    send, recv, ssend, srecv, small_got = scratch[:5]
    scratch = scratch[5:]
    here.greet(ranks)
    start, finish = everyone(
        here.rank, ranks, lambda other: small_in.at[other], lambda rank: small_got.at[rank], ssend, srecv, None
    )
    start()
    copies = Copies(send, recv)
    streams = []
    at_scratch = 0
    for first, members in (("y", [m for m in STREAM_Y if m[0] in names]), ("x", [m for m in STREAM_X if m[0] in names])):
        items = []
        for name, half in members:
            k = names.index(name)
            acc, core_in, line_in, side_in = scratch[at_scratch : at_scratch + 4]
            z_in = scratch[at_scratch + 4 : at_scratch + 4 + levels]
            at_scratch += 4 + levels

            def put(v, k=k, half=half):
                if half is None:
                    outs[k][...] = v
                else:
                    outs[k][half] = v

            items.append((parts[k], half, acc, core_in, line_in, side_in, z_in, put))
        if items:
            streams.append(reduce_stream(here, copies, items, first))
    side_by_side(streams)
    finish()

    def add(i, total):
        return total + jnp.where(i == here.rank, small_in[i], small_got[i])

    small_out[...] = lax.fori_loop(0, ranks, add, jnp.zeros(small_out.shape, F32))
    copies.finish()


STREAM_Y = [("xd", None), ("o", 0)]
STREAM_X = [("z", None), ("o", 1)]


def reduce(parts, small, depth, ident):
    ranks = depth * 8
    levels = depth.bit_length() - 1
    names = list(parts)
    arrays = [parts[n] for n in names]
    sds = jax.ShapeDtypeStruct
    dma = pltpu.SemaphoreType.DMA
    in_vmem = pl.BlockSpec(memory_space=pltpu.VMEM)
    n = 2 * 2 * (3 * (levels + 1) + levels)
    scratch = [dma((n,)), dma((n,)), dma((ranks,)), dma((ranks,)), pltpu.VMEM(small.shape, F32)]
    for name, half in [m for m in STREAM_Y + STREAM_X if m[0] in names]:
        tile = parts[name].shape[-2:]
        scratch.append(pltpu.VMEM((depth, 2, 2) + tile, BF))
        scratch.append(pltpu.VMEM((depth, 2, 2) + tile, BF))
        scratch.append(pltpu.VMEM((depth, 2) + tile, BF))
        scratch.append(pltpu.VMEM((depth,) + tile, BF))
        for level in reversed(range(levels)):
            scratch.append(pltpu.VMEM((1 << level,) + tile, BF))
    return pl.pallas_call(
        partial(reduce_kernel, depth=depth, ranks=ranks, names=names),
        in_specs=[in_vmem] * (len(arrays) + 1),
        out_specs=[in_vmem] * (len(arrays) + 1),
        out_shape=[sds(a.shape[4:], F32) for a in arrays] + [sds(small.shape[1:], F32)],
        scratch_shapes=scratch,
        compiler_params=pltpu.CompilerParams(collective_id=ident, has_side_effects=True, vmem_limit_bytes=LIMIT),
        name="reduce",
    )(*arrays, small)


def pass_on(block, axis, distance):
    devices = range(lax.axis_size(axis))
    route = [(i - distance, i) for i in devices if i - distance in devices]
    return lax.ppermute(block, axis, route)


def contract_rows(left, right):
    return lax.dot_general(left, right, (((0, 1), (0, 1)), ((), ())), preferred_element_type=F32)


def local(
    tokens,
    norm_gain,
    w_in,
    conv_weight,
    conv_bias,
    dt_bias,
    a_log,
    d_skip,
    gated_gain,
    w_out,
    lengths,
    cotangent,
):
    ranks = lax.axis_size("dp") * lax.axis_size("seq")
    place = lax.axis_index("seq")
    tokens = tokens[:, 0]
    cot = cotangent[:, 0]
    batches, piece, _ = tokens.shape
    rows = w_in.shape[0]

    depth = lax.axis_size("dp") // 2
    n0, n1, n2 = norm_gain.shape[0], gated_gain.shape[0], conv_bias.shape[0]
    small = jnp.concatenate([norm_gain, gated_gain, conv_bias, conv_weight.reshape(-1)])
    small = jnp.pad(small, (0, 8 * LN - small.shape[0])).reshape(8, LN)
    w_low = w_in.astype(BF)
    w_xd = jnp.pad(w_low[:, DI:], ((0, 0), (0, XD - (PROJ - DI))))
    w_xd, w_z, w_o, small = gather(w_xd, w_low[:, :DI], w_out.astype(BF).reshape(2, n1 // 2, D), small, depth)
    w_xd, w_z, w_o = w_xd.reshape(D, XD), w_z.reshape(D, DI), w_o.reshape(DI, D)
    small = small.reshape(ranks, 8 * LN)
    gain = small[:, :n0].reshape(1, D)
    gg = small[:, n0 : n0 + n1].reshape(1, DI)
    cb = small[:, n0 + n1 : n0 + n1 + n2].reshape(1, XBC)
    cw = small[:, n0 + n1 + n2 : n0 + n1 + 5 * n2].reshape(ranks, DCONV, n2).transpose(1, 0, 2).reshape(DCONV, XBC)

    halo = pass_on(tokens[:, piece - 16 :], "seq", 1)
    valid = lengths[:, 0].astype(jnp.int32) - place.astype(jnp.int32) * piece
    where_am_i = place.astype(jnp.int32).reshape(1)
    lane_pad = ((0, 0), (0, LN - NH))
    dtb = jnp.pad(dt_bias[None], lane_pad)
    rate = -jnp.exp(a_log)
    rate_row = jnp.pad(rate[None], lane_pad)
    dsk = jnp.repeat(d_skip, HD)[None]

    first, count = 0, batches
    normed, ci, act, step, ld, sig, sloc, s = project(
        first, count, valid, tokens, halo, gain, w_xd, cw, cb, dtb, rate_row
    )
    gathered = lax.all_gather(s, "seq")
    out, gn, dbr, dz, dy, y, sst, dsin, ggrad = mix(
        first, count, valid, where_am_i, tokens, cot, normed, act, step, ld, sloc, gathered, w_z, w_o, gg, dsk
    )
    dsg = lax.all_gather(dsin, "seq")
    dxd, fix, edge, cgrad, hgrad, skip = scan_back(
        count, where_am_i, ci, step, ld, sig, dy, y, sst, dsg, gathered, cw, cb, rate_row, dsk
    )
    next_edge = pass_on(edge, "seq", -1)[:, : DCONV - 1]
    late = []
    for j in range(DCONV - 1):
        late.append(sum(cw[t][None] * next_edge[:, j - t] for t in range(j + 1)))
    late = jnp.stack(late, axis=1)
    fixed = fix.at[:, 16 - (DCONV - 1) :].add(late).astype(BF)
    dxd = dxd.at[:, piece - 16 :, :XBC].set(fixed)
    tgrad, gain_grad = input_grad(first, count, tokens, dbr, gain, dz, dxd, w_z, w_xd)

    grad_wo = contract_rows(gn, dbr)
    grad_wz = contract_rows(normed, dz)
    grad_wx = contract_rows(normed, dxd)
    lead = (depth, 2, 2, 2)
    grad_cw = cgrad[:32].reshape(DCONV, 8, XBC).sum(1)
    heads = hgrad.reshape(2, 8, LN).sum(1)[:, :NH]
    heads = jnp.concatenate([heads[0], heads[1] * rate, skip.sum(0).reshape(NH, HD).sum(1)])
    packed = jnp.concatenate(
        [
            gain_grad.sum(0).reshape(ranks, n0),
            ggrad.sum(0).reshape(ranks, n1),
            cgrad[32:].sum(0).reshape(ranks, n2),
            grad_cw.reshape(DCONV, ranks, n2).transpose(1, 0, 2).reshape(ranks, DCONV * n2),
            jnp.broadcast_to(heads[None], (ranks, 3 * NH)),
        ],
        axis=1,
    )
    used = packed.shape[1]
    packed = jnp.pad(packed, ((0, 0), (0, 8 * LN - used))).reshape(ranks, 8, LN)
    parts = {
        "xd": grad_wx.astype(BF).reshape(lead + (rows, XD)),
        "z": grad_wz.astype(BF).reshape(lead + (rows, DI)),
        "o": grad_wo.astype(BF).reshape(lead + (2, n1 // 2, D)),
    }
    shard_wx, shard_wz, shard_wo, total = reduce(parts, packed, depth, 1)
    shard_win = jnp.concatenate([shard_wz, shard_wx[:, : PROJ - DI]], axis=1)
    total = total.reshape(-1)[:used]
    sizes = [n0, n1, n2, DCONV * n2, NH, NH, NH]
    starts = [sum(sizes[:i]) for i in range(len(sizes))]
    mine = [total[a : a + n] for a, n in zip(starts, sizes)]
    return (
        out[:, None],
        tgrad[:, None],
        mine[0],
        shard_win,
        mine[3].reshape(DCONV, n2),
        mine[2],
        mine[4],
        mine[5],
        mine[6],
        mine[1],
        shard_wo.reshape(n1, D),
    )


def solution(mesh):
    shard = P(("dp", "seq"))
    row_shard = P(("dp", "seq"), None)
    col_shard = P(None, ("dp", "seq"))
    acts = P(None, "dp", "seq", None)
    return jax.shard_map(
        local,
        mesh=mesh,
        in_specs=(
            acts,
            shard,
            row_shard,
            col_shard,
            shard,
            P(),
            P(),
            P(),
            shard,
            row_shard,
            P(None, "dp"),
            acts,
        ),
        out_specs=(
            acts,
            acts,
            shard,
            row_shard,
            col_shard,
            shard,
            P(),
            P(),
            P(),
            shard,
            row_shard,
        ),
        check_vma=False,
    )
```

time: 1170 us -> 491 us (0.42)
  Pallas kernels: 0 us -> 348 us
  matrix products: 361 us -> 23.2 us
  other arithmetic: 310 us -> 15.9 us
  local copies, waits for them, and re-layouts: 249 us -> 25.4 us
  blocking collectives: 144 us -> 0 us
    pallas_call x0 -> x6, Pallas kernels: none -> 348 us  [the longest x1 102 us: scan_back(): pl.pallas_call(partial(scan_back_kernel, places=places), grid=(count,), i...]
    dot_general x54 -> x3, matrix products: 361 us -> 23.2 us  [contract_rows(): lax.dot_general(left, right, (((0, 1), (0, 1)), ((), ())), preferred_elem...]
    reduce_sum x23 -> x7, other arithmetic: 96.6 us -> 4.33 us  [the longest x1 1.01 us: local(): grad_cw = cgrad[:32].reshape(DCONV, 8, XBC).sum(1)]
    unnamed x2 -> x0, blocking collectives: 83.8 us -> none
    all_gather x4 -> x0, blocking collectives: 60.7 us -> none  [the longest x1 43.7 us: local(): lax.all_gather(conv_weight, ('dp', 'seq'), axis=1, tiled=True)]
    another operation x34 -> x0, other arithmetic: 60.3 us -> none
    unnamed x618 -> x28, local copies, waits for them, and re-layouts: 62.4 us -> 5.05 us
    unnamed x11 -> x2, waiting for transfers between devices: 56.1 us -> 0.03 us
  transfers between devices with their start and end apart: 16 -> 4, of which waited for: 3 -> 2; matrix products, arithmetic and copies ran while one was open for 65% -> 7% of each run, Pallas kernels for 0% -> 13%
where the time goes in v1:
time: 491 us; the launch traced here: 490 us
  Pallas kernels  348 us (71%)
  waiting for transfers between devices  59.6 us (12%)
  local copies, waits for them, and re-layouts  25.4 us (5%)
  matrix products  23.2 us (5%)
  other arithmetic  15.9 us (3%)
  between operations  14.3 us (3%)
    pallas_call x1, Pallas kernels, scan_back(): pl.pallas_call(partial(scan_back_kernel, places=places), grid=(count,), i...  102 us
    pallas_call x1, Pallas kernels, reduce(): pl.pallas_call(partial(reduce_kernel, depth=depth, ranks=ranks, names=nam...  67.8 us
    pallas_call x1, Pallas kernels, gather(): pl.pallas_call(partial(gather_kernel, depth=depth, ranks=ranks), in_specs...  63.1 us
    pallas_call x1, Pallas kernels, mix(): pl.pallas_call(partial(mix_kernel, first=first, places=places), grid=(cou...  60.1 us
    all_gather x1, waiting for transfers between devices, local(): gathered = lax.all_gather(s, 'seq')  38.9 us
    pallas_call x1, Pallas kernels, project(): pl.pallas_call(partial(project_kernel, first=first), grid=(count,), in_sp...  35.8 us
    dot_general x3, matrix products, contract_rows(): lax.dot_general(left, right, (((0, 1), (0, 1)), ((), ())), preferred_elem...  23.2 us
    all_gather x1, waiting for transfers between devices, local(): dsg = lax.all_gather(dsin, 'seq')  20.7 us
  transfers between devices with their start and end apart: 4, of which 2 were waited for; matrix products, arithmetic and copies ran while one was open for 7% of the time, Pallas kernels for 13%

profile of v1, /device:TPU:0, one launch (start us, length us, event | category | flops | bytes accessed | tf_op | source)
XLA Modules:
  0.0 490.3 jit_solution(15982206355920467477)
XLA Ops:
  8.1 2.4 collective-permute-start
  13.6 1.6 convert_element_type.28
  15.2 1.2 subtract_bitcast_fusion.vlen_ref
  17.0 1.4 fusion.2.small_in
  18.3 63.1 %gather.1 = (bf16[4,2,2,2,24,1920]{5,4,3,2,1,0:T(8,128)(2,1)}, bf16[4,2,2,2,24,1536]{5,4,3,2,1,0:T(8,128)(2,1)}, bf16[4,2,2,2,2,24,768]{6,5,4,3,2,1,0:T(8,128)(2,1)}, f32[32,8,128]{2,1,0:T(8,128)}) custom-call(bf16[24,1920]{1,0:T(8,128)(2,1)} %pad.25.xd_in, bf16[24,1536]{1,0:T(8,128)(2,1)} %slice.179.z_in, bf16[2,24,768]{2,1,0:T(8,128)(2,1)} %bitcast.82, ...), custom_call_target="tpu_custom_call" | custom-call | tf_op jit(solution)/shard_map/gather/pallas_call | solution.py:947
  83.0 1.2 pad.27.dtb_ref
  88.1 35.8 %project.1 = (bf16[3,512,768]{2,1,0:T(8,128)(2,1)}, f32[3,520,1792]{2,1,0:T(8,128)}, f32[3,512,1792]{2,1,0:T(8,128)}, f32[3,512,128]{2,1,0:T(8,128)}, f32[3,512,...) custom-call(s32[3]{0:T(128)} %subtract_bitcast_fusion.vlen_ref, ...), custom_call_target="tpu_custom_call" | custom-call | tf_op jit(solution)/shard_map/project/pallas_call | solution.py:205
  126.4 38.9 %all-gather.5.cloned.1.call-done = bf16[12,144,1536]{2,1,0:T(8,128)(2,1)} async-done(((bf16[3,144,1536]{2,1,0:T(8,128)(2,1)}), bf16[12,144,1536]{2,1,0:T(8,128)(2,1)}) %all-gather.5.cloned.1.call-update) | async-done | bytes 5308432 | tf_op jit(solution)/shard_map/all_gather | solution.py:1216
  165.3 60.1 %mix.1 = (bf16[3,512,768]{2,1,0:T(8,128)(2,1)}, bf16[3,512,1536]{2,1,0:T(8,128)(2,1)}, bf16[3,512,768]{2,1,0:T(8,128)(2,1)}, bf16[3,512,1536]{2,1,0:T(8,128)(2,1...) custom-call(s32[3]{0:T(128)} %subtract_bitcast_fusion.vlen_ref, ...), custom_call_target="tpu_custom_call" | custom-call | tf_op jit(solution)/shard_map/mix/pallas_call | solution.py:385
  229.2 8.6 %bitcast_convert_fusion.2 = bf16[768,1536]{1,0:T(8,128)(2,1)} fusion(bf16[3,512,768]{2,1,0:T(8,128)(2,1)} %get-tuple-element.70.nrm_ref, bf16[3,512,1536]{2,1,0:T(8,128)(2,1)} %get-tuple-element.80.dz_ref), kind=kOutput, calls=%fused_computation.2 | convolution fusion | flops 3625058304 | bytes 9437184 | tf_op jit(solution)/shard_map/dot_general | solution.py:1165
  237.7 5.2 %bitcast_convert_fusion.1 = bf16[1536,768]{1,0:T(8,128)(2,1)} fusion(bf16[3,512,1536]{2,1,0:T(8,128)(2,1)S(1)} %bitcast.92, bf16[3,512,768]{2,1,0:T(8,128)(2,1)S(1)} %copy-done), kind=kOutput, calls=%fused_computation.1 | convolution fusion | flops 3625058304 | bytes 9437184 | tf_op jit(solution)/shard_map/dot_general | solution.py:1165
  242.9 20.7 %all-gather.7.cloned.1.call-done = bf16[12,128,1536]{2,1,0:T(8,128)(2,1)} async-done(((bf16[3,128,1536]{2,1,0:T(8,128)(2,1)}), bf16[12,128,1536]{2,1,0:T(8,128)(2,1)}) %all-gather.7.cloned.1.call-update) | async-done | bytes 4718608 | tf_op jit(solution)/shard_map/all_gather | solution.py:1220
  263.6 101.6 %scan_back.1 = (bf16[3,512,1920]{2,1,0:T(8,128)(2,1)}, f32[3,16,1792]{2,1,0:T(8,128)}, f32[3,8,1792]{2,1,0:T(8,128)}, f32[40,1792]{1,0:T(8,128)}, f32[16,128]{1,0:T(8,128)}, /*index=5*/f32[8,1536]{1,0:T(8,128)}) custom-call(s32[1]{0:T(128)} %bitcast.1.place_ref, f32[3,520,1792]{2,1,0:T(8,128)} %get-tuple-element.81.ci_ref, ...), custom_call_target="tpu_custom_call" | custom-call | tf_op jit(solution)/shard_map/scan_back/pallas_call | solution.py:602
  368.0 1.3 collective-permute-start.1
  373.5 1.9 scatter-add.4
  375.4 1.7 convert_dynamic-update-slice_fusion.dxd_ref
  377.1 19.5 %input_grad.1 = (bf16[3,512,768]{2,1,0:T(8,128)(2,1)}, f32[8,768]{1,0:T(8,128)}) custom-call(bf16[3,512,768]{2,1,0:T(8,128)(2,1)} %bitcast.62, bf16[3,512,768]{2,1,0:T(8,128)(2,1)} %get-tuple-element.79.dbr_ref, f32[1,768]{1,0:T(1,128)} %reshape.229.g_ref, bf16[3,512,1536]{2,1,0:T(8,128)(2,1)} %get-tuple-element.80.dz_ref, ...), custom_call_target="tpu_custom_call" | custom-call | tf_op jit(solution)/shard_map/input_grad/pallas_call | solution.py:680
  396.6 9.5 %bitcast_convert_fusion = bf16[768,1920]{1,0:T(8,128)(2,1)} fusion(bf16[3,512,768]{2,1,0:T(8,128)(2,1)} %get-tuple-element.70.nrm_ref, bf16[3,512,1920]{2,1,0:T(8,128)(2,1)} %convert_dynamic-update-slice_fusion.dxd_ref), kind=kOutput, calls=%fused_computation | convolution fusion | flops 4531322880 | bytes 11206656 | tf_op jit(solution)/shard_map/dot_general | solution.py:1165
  407.0 67.8 %reduce.5 = (f32[24,1920]{1,0:T(8,128)}, f32[24,1536]{1,0:T(8,128)}, f32[2,24,768]{2,1,0:T(8,128)}, f32[8,128]{1,0:T(8,128)}) custom-call(bf16[4,2,2,2,24,1920]{5,4,3,2,1,0:T(8,128)(2,1)} %bitcast.70, bf16[4,2,2,2,24,1536]{5,4,3,2,1,0:T(8,128)(2,1)} %bitcast.73, bf16[4,2,2,2,2,24,768]{6,5,4,3,2,1,0:T(8,128)(2,1)} %bitcast.74, f32[32,8,128]{2,1,0:T(8,128)} %bitcast.75), custom_call_target="tpu_custom_call" | custom-call | tf_op jit(solution)/shard_map/reduce/pallas_call | solution.py:1147
  474.8 1.3 slice.172
  476.1 1.3 slice.176
  478.0 1.4 fusion.5
  480.1 1.7 pad_maximum_fusion
  481.9 1.6 copy.68
  (81 shorter events, 25.4 us)
Async XLA Ops:
  7.2 117.8 %copy-start.8 = (f32[24]{0:T(128)S(1)}, f32[24]{0:T(128)}, u32[]{:S(2)}) copy-start(f32[24]{0:T(128)} %param.23) | copy-start | bytes 292
  7.2 158.1 %all-gather.5.cloned.1.call-start = ((), (), s32[]{:S(2)}) async-start(), calls=%async_computation | async-start | bytes 6635520 | tf_op jit(solution)/shard_map/all_gather | solution.py:1216
  8.1 79.4 %collective-permute-start = (bf16[3,16,768]{2,1,0:T(8,128)(2,1)S(1)}, bf16[3,16,768]{2,1,0:T(8,128)(2,1)S(1)}, u32[]{:S(2)}, u32[]{:S(2)}) collective-permute-start(bf16[3,16,768]{2,1,0:T(8,128)(2,1)S(1)} %slice.177), channel_id=1, source_target_pairs={{0,1},{1,2},{2,3},{4,5},{5,6},{6,7},{8,9},{9,10},{10,11},{12,13},{... | collective-permute-start | bytes 221192 | tf_op jit(solution)/shard_map/ppermute | solution.py:1161
  82.4 0.7 copy-start.2
  86.2 0.6 copy-start.1
  87.5 0.6 copy-start.3
  124.0 139.7 %all-gather.7.cloned.1.call-start = ((), (), s32[]{:S(2)}) async-start(), calls=%async_computation.1 | async-start | bytes 5898240 | tf_op jit(solution)/shard_map/all_gather | solution.py:1220
  226.2 11.5 %slice-start = ((s8[4718592]{0:T(1024)(128)(4,1)}), s8[524288]{0:T(1024)(128)(4,1)S(1)}, s32[]{:S(2)}) async-start(s8[4718592]{0:T(1024)(128)(4,1)} %bitcast.91), calls=%async_computation.2 | async-start | bytes 1048576
  229.1 8.6 %copy-start = (bf16[3,512,768]{2,1,0:T(8,128)(2,1)S(1)}, bf16[3,512,768]{2,1,0:T(8,128)(2,1)}, u32[]{:S(2)}) copy-start(bf16[3,512,768]{2,1,0:T(8,128)(2,1)} %get-tuple-element.79.dbr_ref) | copy-start | bytes 7077892
  229.1 8.6 %slice-start.1 = ((s8[4718592]{0:T(1024)(128)(4,1)}), s8[4194304]{0:T(1024)(128)(4,1)S(1)}, s32[]{:S(2)}) async-start(s8[4718592]{0:T(1024)(128)(4,1)} %bitcast.91), calls=%async_computation.3 | async-start | bytes 8388608
  263.6 102.3 %copy-start.9 = (f32[24]{0:T(128)S(1)}, f32[24]{0:T(128)}, u32[]{:S(2)}) copy-start(f32[24]{0:T(128)} %param.22) | copy-start | bytes 292
  368.0 3.7 collective-permute-start.1
  396.6 9.5 %copy-start.6 = (f32[8,768]{1,0:T(8,128)S(1)}, f32[8,768]{1,0:T(8,128)}, u32[]{:S(2)}) copy-start(f32[8,768]{1,0:T(8,128)} %get-tuple-element.92) | copy-start | bytes 73732
  396.6 9.6 %copy-start.7 = (f32[72]{0:T(128)S(1)}, f32[72]{0:T(128)}, u32[]{:S(2)}) copy-start(f32[72]{0:T(128)} %pad_maximum_fusion.1) | copy-start | bytes 868
  396.6 9.6 %copy-start.4 = (f32[32,48]{1,0:T(8,128)S(1)}, f32[32,48]{1,0:T(8,128)}, u32[]{:S(2)}) copy-start(f32[32,48]{1,0:T(8,128)} %reshape.241) | copy-start | bytes 18436
  396.6 9.6 %copy-start.5 = (f32[32,56]{1,0:T(8,128)S(1)}, f32[32,56]{1,0:T(8,128)}, u32[]{:S(2)}) copy-start(f32[32,56]{1,0:T(8,128)} %reshape.242) | copy-start | bytes 21508
Sparse Core Ops, SparseCore 0:
  124.1 41.1 all-gather.4
  225.6 38.0 all-gather.6

commit v2 on v1

--- a/solution.py
+++ b/solution.py
@@ -58,15 +58,16 @@
     return op(ah, bh) + op(al, bh) + op(ah, bl)
 
 
-def expander():
+def fill_expander(ref):
     head = lax.broadcasted_iota(jnp.int32, (LN, DI), 0)
     lane = lax.broadcasted_iota(jnp.int32, (LN, DI), 1)
-    return jnp.where(head == lane // HD, 1.0, 0.0).astype(BF)
-
-
-def expand(v, e):
-    top, low = halves(v)
-    return nn(top, e) + nn(low, e)
+    e = jnp.where(head == lane // HD, 1.0, 0.0).astype(BF)
+    ref[0:LN] = e
+    ref[LN:] = e
+
+
+def expand(v, e2):
+    return nn(jnp.concatenate(halves(v), axis=1), e2[...])
 
 
 def lower_mask(strict):
@@ -114,6 +115,7 @@
     nx,
     xw,
     state,
+    e2,
     *,
     first,
 ):
@@ -146,7 +148,10 @@
     step_ref[...] = (jnp.maximum(dt_raw, 0.0) + jnp.log1p(jnp.exp(-jnp.abs(dt_raw)))) * mask
     sig_ref[...] = mask / (1.0 + jnp.exp(-dt_raw))
 
-    e = expander()
+    @pl.when(pl.program_id(0) == 0)
+    def _():
+        fill_expander(e2)
+
     tri = jnp.where(lower_mask(False), 1.0, 0.0)
     state[...] = jnp.zeros_like(state)
 
@@ -157,7 +162,7 @@
         ld = exact_nn(tri, step * rate_ref[...])
         l_ref[rows, :] = ld
         end = ld[CL - 1 :]
-        tail = expand(step * jnp.exp(end - ld), e)
+        tail = expand(step * jnp.exp(end - ld), e2)
         for j in range(XBC // LN):
             ext = ci_ref[pl.ds(base, CL + 8), lanes(j)]
             run = conv_running(ext, cw_ref[:, lanes(j)], cb_ref[:, lanes(j)])
@@ -167,13 +172,13 @@
                 xw[:, lanes(j)] = (act * tail[:, lanes(j)]).astype(BF)
         b = act_ref[rows, DI : DI + NS].astype(BF)
         sloc_ref[k] = state[...].astype(BF)
-        keep = expand(jnp.exp(jnp.broadcast_to(end, (8, LN))), e)[0:1]
+        keep = expand(jnp.exp(jnp.broadcast_to(end, (8, LN))), e2)[0:1]
         state[...] = keep * state[...] + tn(b, xw[...])
         return total + end
 
     total = lax.fori_loop(0, chunks, chunk, jnp.zeros((1, LN), F32))
     s_ref[0:NS] = state[...].astype(BF)
-    keep = expand(jnp.exp(jnp.broadcast_to(total, (8, LN))), e)[0:1]
+    keep = expand(jnp.exp(jnp.broadcast_to(total, (8, LN))), e2)[0:1]
     top, low = halves(keep)
     s_ref[NS : NS + 16] = jnp.concatenate([top, low, jnp.zeros((14, DI), BF)], axis=0)
 
@@ -240,15 +245,89 @@
             pltpu.VMEM((piece + 16, D), BF),
             pltpu.VMEM((CL, DI), BF),
             pltpu.VMEM((NS, DI), F32),
+            pltpu.VMEM((2 * LN, DI), BF),
         ],
         compiler_params=pltpu.CompilerParams(vmem_limit_bytes=LIMIT),
         name="project",
     )(valid, tokens, halo, gain, w_xd, cw, cb, dtb, rate)
 
 
+class Exchange:
+    def __init__(self, own, sib, out, got, swap_send, swap_recv, far_send, far_recv, giver):
+        dp, seq = lax.axis_index("dp"), lax.axis_index("seq")
+        self.x, self.c = seq // 2, seq % 2
+        self.sibling = (dp, self.x * 2 + 1 - self.c)
+        self.across = (dp, (1 - self.x) * 2 + self.c)
+        self.own, self.sib, self.out, self.got = own, sib, out, got
+        self.sems = (swap_send, swap_recv, far_send, far_recv)
+        self.giver = giver
+
+    def greet(self):
+        barrier = pltpu.get_barrier_semaphore()
+        for other in (self.sibling, self.across):
+            pl.semaphore_signal(barrier, inc=1, device_id=other, device_id_type=pl.DeviceIdType.MESH)
+        pl.semaphore_wait(barrier, 2)
+
+    def swap(self, i):
+        return pltpu.make_async_remote_copy(
+            src_ref=self.own.at[i],
+            dst_ref=self.sib.at[i],
+            send_sem=self.sems[0].at[i],
+            recv_sem=self.sems[1].at[i],
+            device_id=self.sibling,
+            device_id_type=pl.DeviceIdType.MESH,
+        )
+
+    def far(self, i):
+        return pltpu.make_async_remote_copy(
+            src_ref=self.out.at[i],
+            dst_ref=self.got.at[i],
+            send_sem=self.sems[2].at[i],
+            recv_sem=self.sems[3].at[i],
+            device_id=self.across,
+            device_id_type=pl.DeviceIdType.MESH,
+        )
+
+    def decay(self, ref, i):
+        return ref[i, NS : NS + 1].astype(F32) + ref[i, NS + 1 : NS + 2].astype(F32)
+
+    def begin(self, count, coefficients):
+        self.greet()
+        for i in range(count):
+            self.swap(i).start()
+        for i in range(count):
+            self.swap(i).wait_recv()
+
+            @pl.when(self.x == self.giver)
+            def _():
+                f, g = coefficients(self.decay(self.own, i), self.decay(self.sib, i))
+                self.out[i] = (f * self.own[i, 0:NS].astype(F32) + g * self.sib[i, 0:NS].astype(F32)).astype(BF)
+                self.far(i).start()
+
+    def end(self, count):
+        for i in range(count):
+            self.swap(i).wait_send()
+
+            @pl.when(self.x == self.giver)
+            def _():
+                self.far(i).wait_send()
+
+
+def exchange_scratch(count):
+    dma = pltpu.SemaphoreType.DMA((count,))
+    return [
+        pltpu.VMEM((count, SROWS, DI), BF),
+        pltpu.VMEM((count, NS, DI), BF),
+        pltpu.VMEM((count, NS, DI), BF),
+        dma,
+        dma,
+        dma,
+        dma,
+    ]
+
+
 def mix_kernel(
     vlen_ref,
-    place_ref,
     x_ref,
     cot_ref,
     nrm_ref,
@@ -256,7 +335,7 @@
     step_ref,
     l_ref,
     sloc_ref,
-    sg_ref,
+    s_ref,
     wz_ref,
     wo_ref,
     gg_ref,
@@ -267,35 +346,34 @@
     dz_ref,
     dy_ref,
     y_ref,
-    sst_ref,
+    incoming,
     dsin_ref,
     ggrad_ref,
     zs,
     dgn,
-    incoming,
     dsacc,
     yf,
     work,
-    *,
+    e2,
+    sib,
+    out,
+    got,
+    *sems,
     first,
-    places,
+    count,
 ):
     piece = x_ref.shape[0]
     chunks = piece // CL
-    valid = vlen_ref[first + pl.program_id(0)]
-    place = place_ref[0]
-
-    @pl.when(pl.program_id(0) == 0)
+    section = pl.program_id(0)
+    valid = vlen_ref[first + section]
+    states = Exchange(s_ref, sib, out, got, *sems, giver=0)
+    even = states.c == 0
+
+    @pl.when(section == 0)
     def _():
         ggrad_ref[...] = jnp.zeros_like(ggrad_ref)
-
-    incoming[...] = jnp.zeros_like(incoming)
-    for j in range(places - 1):
-
-        @pl.when(j < place)
-        def _():
-            keep = sg_ref[j, NS : NS + 1].astype(F32) + sg_ref[j, NS + 1 : NS + 2].astype(F32)
-            incoming[...] = keep * incoming[...] + sg_ref[j, 0:NS].astype(F32)
+        fill_expander(e2)
+        states.begin(count, lambda own, sibs: (jnp.where(even, sibs, 1.0), jnp.where(even, 1.0, own)))
 
     row = lax.broadcasted_iota(jnp.int32, (piece, 1), 0)
     live = row < valid
@@ -305,24 +383,29 @@
         zs[:, cols] = nn(nrm_ref[...], wz_ref[:, cols])
         dgn[:, cols] = nt(dbr_ref[...], wo_ref[cols, :])
 
-    e = expander()
+    @pl.when(states.x == 0)
+    def _():
+        incoming[...] = jnp.where(even, 0.0, 1.0) * sib[section, 0:NS].astype(F32)
+
+    @pl.when(states.x == 1)
+    def _():
+        states.far(section).wait_recv()
+        f = jnp.where(even, 1.0, states.decay(sib, section))
+        incoming[...] = f * got[section].astype(F32) + jnp.where(even, 0.0, 1.0) * sib[section, 0:NS].astype(F32)
+
     low = lower_mask(False)
     left, right = half_masks()
     dsacc[...] = jnp.zeros_like(dsacc)
 
-    def chunk(k, prefix):
+    def chunk(k, before):
         base = pl.multiple_of(k * CL, CL)
         rows = pl.ds(base, CL)
         step = step_ref[rows, :]
         ld = l_ref[rows, :]
         ldt = ld.T
-        end = ld[CL - 1 :]
-        before = expand(jnp.exp(jnp.broadcast_to(prefix, (8, LN))), e)[0:1]
-        startf = before * incoming[...] + sloc_ref[k].astype(F32)
-        start = startf.astype(BF)
-        sst_ref[k] = startf
-        step_e = expand(step, e)
-        grow = expand(jnp.exp(ld), e)
+        start = (before * incoming[...] + sloc_ref[k].astype(F32)).astype(BF)
+        step_e = expand(step, e2)
+        grow = expand(jnp.exp(ld), e2)
         b = act_ref[rows, DI : DI + NS].astype(BF)
         c, c_low = halves(act_ref[rows, DI + NS :])
         scores = jnp.where(low, nt(c, b), 0.0)
@@ -367,35 +450,38 @@
             dz_ref[rows, lanes(j)] = (du * full * (s + sz * (1.0 - s))).astype(BF)
             work[:, lanes(j)] = (dy * grow[:, lanes(j)]).astype(BF)
         dsacc[...] += before * tn(c, work[...])
-        return prefix + end
-
-    lax.fori_loop(0, chunks, chunk, jnp.zeros((1, LN), F32))
-    dsin_ref[...] = dsacc[...].astype(BF)
+        return before * grow[CL - 1 :]
+
+    lax.fori_loop(0, chunks, chunk, jnp.ones((1, DI), F32))
+    dsin_ref[0:NS] = dsacc[...].astype(BF)
+    dsin_ref[NS:] = s_ref[section, NS:]
     for j in range(D // 256):
         cols = slice(j * 256, (j + 1) * 256)
         branch = nn(gn_ref[...], wo_ref[:, cols])
         out_ref[:, cols] = jnp.where(live, x_ref[:, cols].astype(F32) + branch, 0.0).astype(BF)
 
-
-def mix(first, count, valid, place, tokens, cot, normed, act, step, ld, sloc, gathered, w_z, w_o, gg, dsk):
+    @pl.when(section == count - 1)
+    def _():
+        states.end(count)
+
+
+def mix(first, count, valid, tokens, cot, normed, act, step, ld, sloc, s, w_z, w_o, gg, dsk):
     piece = tokens.shape[1]
     chunks = piece // CL
-    places = gathered.shape[0]
     sds = jax.ShapeDtypeStruct
     return pl.pallas_call(
-        partial(mix_kernel, first=first, places=places),
+        partial(mix_kernel, first=first, count=count),
         grid=(count,),
         in_specs=[
-            SMEM,
             SMEM,
             per((piece, D), first),
             per((piece, D), first),
             per((piece, D)),
-            per((piece, XBC), **ONE),
+            per((piece, XBC)),
             per((piece, LN)),
             per((piece, LN)),
-            per((chunks, NS, DI), **ONE),
-            pl.BlockSpec((places, None, SROWS, DI), lambda i: (0, i, 0, 0), **ONE),
+            per((chunks, NS, DI)),
+            kept((count, SROWS, DI)),
             kept((D, DI)),
             kept((DI, D)),
             whole((1, DI)),
@@ -408,8 +494,8 @@
             per((piece, DI)),
             per((piece, DI)),
             per((piece, DI)),
-            per((chunks, NS, DI)),
             per((NS, DI)),
+            per((SROWS, DI)),
             whole((8, DI)),
         ],
         out_shape=[
@@ -419,34 +505,34 @@
             sds((count, piece, DI), BF),
             sds((count, piece, DI), F32),
             sds((count, piece, DI), F32),
-            sds((count, chunks, NS, DI), F32),
-            sds((count, NS, DI), BF),
+            sds((count, NS, DI), F32),
+            sds((count, SROWS, DI), BF),
             sds((8, DI), F32),
         ],
         scratch_shapes=[
             pltpu.VMEM((piece, DI), F32),
             pltpu.VMEM((piece, DI), F32),
             pltpu.VMEM((NS, DI), F32),
-            pltpu.VMEM((NS, DI), F32),
             pltpu.VMEM((CL, DI), F32),
             pltpu.VMEM((CL, DI), BF),
-        ],
-        compiler_params=pltpu.CompilerParams(vmem_limit_bytes=LIMIT),
+            pltpu.VMEM((2 * LN, DI), BF),
+        ]
+        + exchange_scratch(count),
+        compiler_params=pltpu.CompilerParams(vmem_limit_bytes=LIMIT, collective_id=2, has_side_effects=True),
         name="mix",
-    )(valid, place, tokens, cot, normed, act, step, ld, sloc, gathered, w_z, w_o, gg, dsk)
+    )(valid, tokens, cot, normed, act, step, ld, sloc, s, w_z, w_o, gg, dsk)
 
 
 def scan_back_kernel(
-    place_ref,
     ci_ref,
     step_ref,
     l_ref,
     sig_ref,
     dy_ref,
     y_ref,
-    sst_ref,
-    dsg_ref,
-    keep_ref,
+    inc_ref,
+    sloc_ref,
+    dsin_ref,
     cw_ref,
     cb_ref,
     rate_ref,
@@ -464,28 +550,44 @@
     xdt,
     xt,
     dr,
-    *,
-    places,
+    e2,
+    u_top,
+    u_low,
+    fs,
+    vs,
+    dyg,
+    start,
+    sib,
+    out,
+    got,
+    *sems,
+    count,
 ):
     piece = dy_ref.shape[0]
     chunks = piece // CL
-    place = place_ref[0]
-
-    @pl.when(pl.program_id(0) == 0)
+    section = pl.program_id(0)
+    states = Exchange(dsin_ref, sib, out, got, *sems, giver=1)
+    even = states.c == 0
+    one_if_even = jnp.where(even, 1.0, 0.0)
+
+    @pl.when(section == 0)
     def _():
         cgrad_ref[...] = jnp.zeros_like(cgrad_ref)
         hgrad_ref[...] = jnp.zeros_like(hgrad_ref)
         skip_ref[...] = jnp.zeros_like(skip_ref)
-
-    ds[...] = jnp.zeros_like(ds)
-    for j in reversed(range(1, places)):
-
-        @pl.when(j > place)
-        def _():
-            keep = keep_ref[j, 0:1].astype(F32) + keep_ref[j, 1:2].astype(F32)
-            ds[...] = keep * ds[...] + dsg_ref[j].astype(F32)
-
-    e = expander()
+        fill_expander(e2)
+        states.begin(count, lambda own, sibs: (jnp.where(even, 1.0, sibs), jnp.where(even, own, 1.0)))
+
+    @pl.when(states.x == 1)
+    def _():
+        ds[...] = one_if_even * sib[section, 0:NS].astype(F32)
+
+    @pl.when(states.x == 0)
+    def _():
+        states.far(section).wait_recv()
+        f = jnp.where(even, states.decay(sib, section), 1.0)
+        ds[...] = f * got[section].astype(F32) + one_if_even * sib[section, 0:NS].astype(F32)
+
     upper = jnp.logical_not(lower_mask(True))
     upper_one = jnp.where(upper, 1.0, 0.0)
     before_one = jnp.where(lower_mask(True), 1.0, 0.0)
@@ -500,10 +602,15 @@
         ld = l_ref[rows, :]
         ldt = ld.T
         end = ld[CL - 1 :]
-        step_e = expand(step, e)
-        grow = expand(jnp.exp(ld), e)
-        tail = expand(jnp.exp(end - ld), e)
-        keep = expand(jnp.exp(jnp.broadcast_to(end, (8, LN))), e)[0:1]
+        prefix = jnp.zeros((8, LN), F32)
+        for j in range(chunks - 1):
+            prefix = prefix + jnp.where(j < k, 1.0, 0.0) * l_ref[j * CL + CL - 1 : j * CL + CL, :]
+        before = expand(jnp.exp(prefix), e2)[0:1]
+        start[...] = before * inc_ref[...] + sloc_ref[k].astype(F32)
+        step_e = expand(step, e2)
+        grow = expand(jnp.exp(ld), e2)
+        tail = expand(jnp.exp(end - ld), e2)
+        keep = grow[CL - 1 :]
         for j in range(XBC // LN):
             ext = ci_ref[pl.ds(base, CL + 8), lanes(j)]
             run = conv_running(ext, cw_ref[:, lanes(j)], cb_ref[:, lanes(j)])
@@ -518,23 +625,15 @@
         b = xa[:, DI : DI + NS].astype(BF)
         c = xa[:, DI + NS :].astype(BF)
         scores = jnp.where(upper, nt(b, c), 0.0)
-        dsb = ds[...].astype(BF)
-        start = sst_ref[k]
+        dact[:, 0:DI] = nn(b, ds[...].astype(BF)) * tail
         dscores = jnp.zeros((CL, CL), F32)
-        db = three(nt, xt[...], ds[...])
-        dc = jnp.zeros((CL, NS), F32)
-        r_u = jnp.zeros((CL, LN), F32)
-        r_f = jnp.zeros((CL, LN), F32)
-        r_v = jnp.zeros((CL, LN), F32)
-        r_c = jnp.zeros((8, LN), F32)
         for j in range(DI // LN):
-            et = e[:, lanes(j)]
             dyf = dy_ref[rows, lanes(j)]
             dyb, dyl = halves(dyf)
             block = jnp.concatenate([dyb * left, dyb * right], axis=0)
+            block_low = jnp.concatenate([dyl * left, dyl * right], axis=0)
             xdb, xdl = halves(xdt[:, lanes(j)])
-            dmix = nt(xdb, block)
-            dmix = dmix + nt(xdl, block) + nt(xdb, jnp.concatenate([dyl * left, dyl * right], axis=0))
+            dmix = nt(jnp.concatenate([xdb, xdl], axis=1), jnp.concatenate([block, block], axis=1)) + nt(xdb, block_low)
             mixes = []
             for p, h in enumerate((2 * j, 2 * j + 1)):
                 gap = jnp.minimum(ldt[h : h + 1, :] - ld[:, h : h + 1], 0.0)
@@ -542,29 +641,30 @@
                 mixes.append((w * scores).astype(BF))
                 dscores = dscores + dmix[:, lanes(p)] * w
             diag = nn(jnp.concatenate(mixes, axis=1), block)
-            far = nn(b, dsb[:, lanes(j)]) * tail[:, lanes(j)]
+            far = dact[:, lanes(j)]
             xdf = xdb.astype(F32)
-            u_top, u_low = halves(dyb.astype(F32) * y_ref[rows, lanes(j)] - xdf * diag)
-            r_u = r_u + nt(u_top, et) + nt(u_low, et)
-            r_f = r_f + nt((xdf * far).astype(BF), et)
+            u_top[:, lanes(j)], u_low[:, lanes(j)] = halves(dyb.astype(F32) * y_ref[rows, lanes(j)] - xdf * diag)
+            fs[:, lanes(j)] = (xdf * far).astype(BF)
             dxd = diag + far
             x = xa[:, lanes(j)]
-            r_v = r_v + nt((x * dxd).astype(BF), et)
+            vs[:, lanes(j)] = (x * dxd).astype(BF)
             dact[:, lanes(j)] = dxd * step_e[:, lanes(j)] + dsk_ref[:, lanes(j)] * dyf
             skip_ref[:, lanes(j)] += jnp.sum((dyf * x).reshape(CL // 8, 8, LN), axis=0)
-            dygf = dyf * grow[:, lanes(j)]
-            dyg = dygf.astype(BF)
-            st = start[:, lanes(j)]
-            dc = dc + three(nt, dygf, st)
-            dsj = ds[:, lanes(j)]
-            const = jnp.sum((st * dsj).reshape(NS // 8, 8, LN), axis=0) * keep[:, lanes(j)]
-            c_top, c_low = halves(const)
-            r_c = r_c + nt(c_top, et) + nt(c_low, et)
-            ds[:, lanes(j)] = keep[:, lanes(j)] * dsj + tn(c, dyg)
+            dyg[:, lanes(j)] = dyf * grow[:, lanes(j)]
+        e = e2[0:LN]
+        const = jnp.sum((start[...] * ds[...]).reshape(NS // 8, 8, DI), axis=0) * keep
+        c_top, c_low = halves(const)
+        r_c = jnp.sum(nt(c_top, e) + nt(c_low, e), axis=0, keepdims=True)
+        r_u = nt(u_top[...], e) + nt(u_low[...], e)
+        r_f = nt(fs[...], e)
+        r_v = nt(vs[...], e)
+        db = three(nt, xt[...], ds[...])
+        dc = three(nt, dyg[...], start[...])
+        ds[...] = keep * ds[...] + tn(c, dyg[...].astype(BF))
         dsc = jnp.where(upper, dscores, 0.0).astype(BF)
         dact[:, DI : DI + NS] = db + nn(dsc, c)
         dact[:, DI + NS :] = dc + tn(dsc, b)
-        da = exact_nn(upper_one, r_u) + exact_nn(before_one, r_f) + jnp.sum(r_c, axis=0, keepdims=True)
+        da = exact_nn(upper_one, r_u) + exact_nn(before_one, r_f) + r_c
         dstep = r_v + rate_ref[...] * da
         ddt = dstep * sig_ref[rows, :]
         hgrad_ref[0:8] += jnp.sum(ddt.reshape(CL // 8, 8, LN), axis=0)
@@ -573,13 +673,14 @@
         for j in range(XBC // LN):
             g = dact[:, lanes(j)] * dsl[:, lanes(j)]
             dr[0:CL, lanes(j)] = g
-            ext = ci_ref[pl.ds(base, CL + 8), lanes(j)]
+            ci = ci_ref[pl.ds(base + 8, CL), lanes(j)]
             gext = dr[:, lanes(j)]
             total = jnp.zeros((CL, LN), F32)
             for tap in range(DCONV):
-                total = total + gext[DCONV - 1 - tap : DCONV - 1 - tap + CL] * cw_ref[tap : tap + 1, lanes(j)]
-                part = g * ext[5 + tap : 5 + tap + CL]
-                cgrad_ref[8 * tap : 8 * tap + 8, lanes(j)] += jnp.sum(part.reshape(CL // 8, 8, LN), axis=0)
+                later = DCONV - 1 - tap
+                shifted = gext[later : later + CL] if later else g
+                total = total + shifted * cw_ref[tap : tap + 1, lanes(j)]
+                cgrad_ref[8 * tap : 8 * tap + 8, lanes(j)] += jnp.sum((shifted * ci).reshape(CL // 8, 8, LN), axis=0)
             cgrad_ref[32:40, lanes(j)] += jnp.sum(g.reshape(CL // 8, 8, LN), axis=0)
             dxd_ref[rows, lanes(j)] = total.astype(BF)
 
@@ -592,27 +693,33 @@
 
     lax.fori_loop(0, chunks, chunk, 0)
     edge_ref[...] = dr[CL:]
-
-
-def scan_back(count, place, ci, step, ld, sig, dy, y, sst, dsg, gathered, cw, cb, rate, dsk):
+    for tap in range(DCONV - 1):
+        later = DCONV - 1 - tap
+        part = dr[CL : CL + later] * ci_ref[8 - later : 8]
+        cgrad_ref[8 * tap : 8 * tap + 1] += jnp.sum(part, axis=0, keepdims=True)
+
+    @pl.when(section == count - 1)
+    def _():
+        states.end(count)
+
+
+def scan_back(count, ci, step, ld, sig, dy, y, inc, sloc, dsin, cw, cb, rate, dsk):
     piece = dy.shape[1]
     chunks = piece // CL
-    places = gathered.shape[0]
     sds = jax.ShapeDtypeStruct
     return pl.pallas_call(
-        partial(scan_back_kernel, places=places),
+        partial(scan_back_kernel, count=count),
         grid=(count,),
         in_specs=[
-            SMEM,
             per((piece + 8, XBC)),
             per((piece, LN)),
             per((piece, LN)),
             per((piece, LN)),
             per((piece, DI)),
             per((piece, DI)),
+            per((NS, DI)),
             per((chunks, NS, DI)),
-            pl.BlockSpec((places, None, NS, DI), lambda i: (0, i, 0, 0), **ONE),
-            pl.BlockSpec((places, None, 16, DI), lambda i: (0, i, NS // 16, 0)),
+            kept((count, SROWS, DI)),
             whole((DCONV, XBC)),
             whole((1, XBC)),
             whole((1, LN)),
@@ -642,10 +749,18 @@
             pltpu.VMEM((CL, DI), F32),
             pltpu.VMEM((CL, DI), F32),
             pltpu.VMEM((CL + 8, XBC), F32),
-        ],
-        compiler_params=pltpu.CompilerParams(vmem_limit_bytes=LIMIT),
+            pltpu.VMEM((2 * LN, DI), BF),
+            pltpu.VMEM((CL, DI), BF),
+            pltpu.VMEM((CL, DI), BF),
+            pltpu.VMEM((CL, DI), BF),
+            pltpu.VMEM((CL, DI), BF),
+            pltpu.VMEM((CL, DI), F32),
+            pltpu.VMEM((NS, DI), F32),
+        ]
+        + exchange_scratch(count),
+        compiler_params=pltpu.CompilerParams(vmem_limit_bytes=LIMIT, collective_id=3, has_side_effects=True),
         name="scan_back",
-    )(place, ci, step, ld, sig, dy, y, sst, dsg, gathered, cw, cb, rate, dsk)
+    )(ci, step, ld, sig, dy, y, inc, sloc, dsin, cw, cb, rate, dsk)
 
 
 def input_grad_kernel(x_ref, dbr_ref, g_ref, dz_ref, dxd_ref, wz_ref, wx_ref, out_ref, gain_ref, dn):
@@ -1202,7 +1317,6 @@
 
     halo = pass_on(tokens[:, piece - 16 :], "seq", 1)
     valid = lengths[:, 0].astype(jnp.int32) - place.astype(jnp.int32) * piece
-    where_am_i = place.astype(jnp.int32).reshape(1)
     lane_pad = ((0, 0), (0, LN - NH))
     dtb = jnp.pad(dt_bias[None], lane_pad)
     rate = -jnp.exp(a_log)
@@ -1213,13 +1327,11 @@
     normed, ci, act, step, ld, sig, sloc, s = project(
         first, count, valid, tokens, halo, gain, w_xd, cw, cb, dtb, rate_row
     )
-    gathered = lax.all_gather(s, "seq")
-    out, gn, dbr, dz, dy, y, sst, dsin, ggrad = mix(
-        first, count, valid, where_am_i, tokens, cot, normed, act, step, ld, sloc, gathered, w_z, w_o, gg, dsk
+    out, gn, dbr, dz, dy, y, inc, dsin, ggrad = mix(
+        first, count, valid, tokens, cot, normed, act, step, ld, sloc, s, w_z, w_o, gg, dsk
     )
-    dsg = lax.all_gather(dsin, "seq")
     dxd, fix, edge, cgrad, hgrad, skip = scan_back(
-        count, where_am_i, ci, step, ld, sig, dy, y, sst, dsg, gathered, cw, cb, rate_row, dsk
+        count, ci, step, ld, sig, dy, y, inc, sloc, dsin, cw, cb, rate_row, dsk
     )
     next_edge = pass_on(edge, "seq", -1)[:, : DCONV - 1]
     late = []

time: 491 us -> 409 us (0.83)
  waiting for transfers between devices: 59.6 us -> 0.01 us
  between operations: 14.3 us -> 0.98 us
  Pallas kernels: 348 us -> 343 us
    all_gather x2 -> x0, waiting for transfers between devices: 59.6 us -> none  [the longest x1 38.9 us: local(): gathered = lax.all_gather(s, 'seq')]
  transfers between devices with their start and end apart: 4 -> 2, of which waited for: 2 -> 0; matrix products, arithmetic and copies ran while one was open for 7% -> 8% of each run, Pallas kernels for 13% -> 15%
where the time goes in v2:
time: 409 us; the launch traced here: 408 us
  Pallas kernels  343 us (84%)
  local copies, waits for them, and re-layouts  24.2 us (6%)
  matrix products  23.3 us (6%)
  other arithmetic  12.5 us (3%)
    pallas_call x1, Pallas kernels, scan_back(): pl.pallas_call(partial(scan_back_kernel, count=count), grid=(count,), in_...  108 us
    pallas_call x1, Pallas kernels, reduce(): pl.pallas_call(partial(reduce_kernel, depth=depth, ranks=ranks, names=nam...  65.8 us
    pallas_call x1, Pallas kernels, gather(): pl.pallas_call(partial(gather_kernel, depth=depth, ranks=ranks), in_specs...  63.1 us
    pallas_call x1, Pallas kernels, mix(): pl.pallas_call(partial(mix_kernel, first=first, count=count), grid=(count...  51.2 us
    pallas_call x1, Pallas kernels, project(): pl.pallas_call(partial(project_kernel, first=first), grid=(count,), in_sp...  36.1 us
    dot_general x3, matrix products, contract_rows(): lax.dot_general(left, right, (((0, 1), (0, 1)), ((), ())), preferred_elem...  23.3 us
    pallas_call x1, Pallas kernels, input_grad(): pl.pallas_call(input_grad_kernel, grid=(count,), in_specs=[per((piece, D)...  19.5 us
  transfers between devices with their start and end apart: 2, of which 0 were waited for; matrix products, arithmetic and copies ran while one was open for 8% of the time, Pallas kernels for 15%

profile of v2, /device:TPU:0, one launch (start us, length us, event | category | flops | bytes accessed | tf_op | source)
XLA Modules:
  0.0 407.9 jit_solution(18396526429398792749)
XLA Ops:
  0.6 0.9 slice.177
  1.5 2.4 collective-permute-start
  3.9 1.0 convert_element_type.27
  7.0 1.6 convert_element_type.28
  9.2 1.4 fusion.2.small_in
  10.6 63.1 %gather.1 = (bf16[4,2,2,2,24,1920]{5,4,3,2,1,0:T(8,128)(2,1)}, bf16[4,2,2,2,24,1536]{5,4,3,2,1,0:T(8,128)(2,1)}, bf16[4,2,2,2,2,24,768]{6,5,4,3,2,1,0:T(8,128)(2,1)}, f32[32,8,128]{2,1,0:T(8,128)}) custom-call(bf16[24,1920]{1,0:T(8,128)(2,1)} %pad.25.xd_in, bf16[24,1536]{1,0:T(8,128)(2,1)} %slice.179.z_in, bf16[2,24,768]{2,1,0:T(8,128)(2,1)} %bitcast.77, ...), custom_call_target="tpu_custom_call" | custom-call | tf_op jit(solution)/shard_map/gather/pallas_call | solution.py:1062
  73.6 0.9 copy.56
  74.7 1.2 subtract_bitcast_fusion.vlen_ref
  76.8 1.2 pad.27.dtb_ref
  83.9 36.1 %project.1 = (bf16[3,512,768]{2,1,0:T(8,128)(2,1)}, f32[3,520,1792]{2,1,0:T(8,128)}, f32[3,512,1792]{2,1,0:T(8,128)}, f32[3,512,128]{2,1,0:T(8,128)}, f32[3,512,...) custom-call(s32[3]{0:T(128)} %subtract_bitcast_fusion.vlen_ref, ...), custom_call_target="tpu_custom_call" | custom-call | tf_op jit(solution)/shard_map/project/pallas_call | solution.py:210
  120.0 51.2 %mix.1 = (bf16[3,512,768]{2,1,0:T(8,128)(2,1)}, bf16[3,512,1536]{2,1,0:T(8,128)(2,1)}, bf16[3,512,768]{2,1,0:T(8,128)(2,1)}, bf16[3,512,1536]{2,1,0:T(8,128)(2,1...) custom-call(s32[3]{0:T(128)} %subtract_bitcast_fusion.vlen_ref, ...), custom_call_target="tpu_custom_call" | custom-call | tf_op jit(solution)/shard_map/mix/pallas_call | solution.py:472
  171.3 107.6 %scan_back.1 = (bf16[3,512,1920]{2,1,0:T(8,128)(2,1)}, f32[3,16,1792]{2,1,0:T(8,128)}, f32[3,8,1792]{2,1,0:T(8,128)}, f32[40,1792]{1,0:T(8,128)}, f32[16,128]{1,0:T(8,128)}, /*index=5*/f32[8,1536]{1,0:T(8,128)}) custom-call(f32[3,520,1792]{2,1,0:T(8,128)} %get-tuple-element.81.ci_ref, f32[3,512,128]{2,1,0:T(8,128)} %get-tuple-element.72.step_ref, ...), custom_call_target="tpu_custom_call" | custom-call | tf_op jit(solution)/shard_map/scan_back/pallas_call | solution.py:710
  280.6 1.0 bitcast_reduce_fusion
  281.6 1.3 collective-permute-start.1
  282.9 8.4 %bitcast_convert_fusion.2 = bf16[768,1536]{1,0:T(8,128)(2,1)} fusion(bf16[3,512,768]{2,1,0:T(8,128)(2,1)} %get-tuple-element.70.nrm_ref, bf16[3,512,1536]{2,1,0:T(8,128)(2,1)} %get-tuple-element.80.dz_ref), kind=kOutput, calls=%fused_computation.2 | convolution fusion | flops 3625058304 | bytes 9437184 | tf_op jit(solution)/shard_map/dot_general | solution.py:1280
  291.4 5.4 %bitcast_convert_fusion.1 = bf16[1536,768]{1,0:T(8,128)(2,1)} fusion(bf16[3,512,1536]{2,1,0:T(8,128)(2,1)S(1)} %copy-done.11, bf16[3,512,768]{2,1,0:T(8,128)(2,1)S(1)} %copy-done), kind=kOutput, calls=%fused_computation.1 | convolution fusion | flops 3625058304 | bytes 9437184 | tf_op jit(solution)/shard_map/dot_general | solution.py:1280
  301.2 19.5 %input_grad.1 = (bf16[3,512,768]{2,1,0:T(8,128)(2,1)}, f32[8,768]{1,0:T(8,128)}) custom-call(bf16[3,512,768]{2,1,0:T(8,128)(2,1)} %bitcast.59, bf16[3,512,768]{2,1,0:T(8,128)(2,1)} %get-tuple-element.79.dbr_ref, f32[1,768]{1,0:T(1,128)} %reshape.225.g_ref, bf16[3,512,1536]{2,1,0:T(8,128)(2,1)} %get-tuple-element.80.dz_ref, ...), custom_call_target="tpu_custom_call" | custom-call | tf_op jit(solution)/shard_map/input_grad/pallas_call | solution.py:795
  320.8 9.5 %bitcast_convert_fusion = bf16[768,1920]{1,0:T(8,128)(2,1)} fusion(bf16[3,512,768]{2,1,0:T(8,128)(2,1)} %get-tuple-element.70.nrm_ref, bf16[3,512,1920]{2,1,0:T(8,128)(2,1)} %convert_dynamic-update-slice_fusion.dxd_ref), kind=kOutput, calls=%fused_computation | convolution fusion | flops 4531322880 | bytes 11206656 | tf_op jit(solution)/shard_map/dot_general | solution.py:1280
  331.2 65.8 %reduce.5 = (f32[24,1920]{1,0:T(8,128)}, f32[24,1536]{1,0:T(8,128)}, f32[2,24,768]{2,1,0:T(8,128)}, f32[8,128]{1,0:T(8,128)}) custom-call(bf16[4,2,2,2,24,1920]{5,4,3,2,1,0:T(8,128)(2,1)} %bitcast.64, bf16[4,2,2,2,24,1536]{5,4,3,2,1,0:T(8,128)(2,1)} %bitcast.68, bf16[4,2,2,2,2,24,768]{6,5,4,3,2,1,0:T(8,128)(2,1)} %bitcast.69, f32[32,8,128]{2,1,0:T(8,128)} %bitcast.70), custom_call_target="tpu_custom_call" | custom-call | tf_op jit(solution)/shard_map/reduce/pallas_call | solution.py:1262
  397.0 1.3 slice.172
  398.3 1.3 slice.176
  400.2 1.4 fusion.5
  402.3 1.7 pad_maximum_fusion
  404.0 3.2 copy.62
  (77 shorter events, 18.7 us)
Async XLA Ops:
  1.5 81.8 %collective-permute-start = (bf16[3,16,768]{2,1,0:T(8,128)(2,1)S(1)}, bf16[3,16,768]{2,1,0:T(8,128)(2,1)S(1)}, u32[]{:S(2)}, u32[]{:S(2)}) collective-permute-start(bf16[3,16,768]{2,1,0:T(8,128)(2,1)S(1)} %slice.177), channel_id=1, source_target_pairs={{0,1},{1,2},{2,3},{4,5},{5,6},{6,7},{8,9},{9,10},{10,11},{12,13},{... | collective-permute-start | bytes 221192 | tf_op jit(solution)/shard_map/ppermute | solution.py:1276
  83.3 0.6 copy-start.3
  171.3 108.3 %copy-start.12 = (f32[24]{0:T(128)S(1)}, f32[24]{0:T(128)}, u32[]{:S(2)}) copy-start(f32[24]{0:T(128)} %param.22) | copy-start | bytes 292
  281.6 18.3 %collective-permute-start.1 = (f32[3,8,1792]{2,1,0:T(8,128)}, f32[3,8,1792]{2,1,0:T(8,128)S(1)}, u32[]{:S(2)}, u32[]{:S(2)}) collective-permute-start(f32[3,8,1792]{2,1,0:T(8,128)} %get-tuple-element.89), channel_id=1, source_target_pairs={{1,0},{2,1},{3,2},{5,4},{6,5},{7,6},{9,8},{10,9},{11,10},{13,12},{... | collective-permute-start | bytes 516104 | tf_op jit(solution)/shard_map/ppermute | solution.py:1276
  282.9 8.5 %copy-start = (bf16[3,512,768]{2,1,0:T(8,128)(2,1)S(1)}, bf16[3,512,768]{2,1,0:T(8,128)(2,1)}, u32[]{:S(2)}) copy-start(bf16[3,512,768]{2,1,0:T(8,128)(2,1)} %get-tuple-element.79.dbr_ref) | copy-start | bytes 7077892
  282.9 8.4 %copy-start.11 = (bf16[3,512,1536]{2,1,0:T(8,128)(2,1)S(1)}, bf16[3,512,1536]{2,1,0:T(8,128)(2,1)}, u32[]{:S(2)}) copy-start(bf16[3,512,1536]{2,1,0:T(8,128)(2,1)} %get-tuple-element.91) | copy-start | bytes 14155780
  291.4 7.0 %copy-start.6 = (f32[8,1536]{1,0:T(8,128)S(1)}, f32[8,1536]{1,0:T(8,128)}, u32[]{:S(2)}) copy-start(f32[8,1536]{1,0:T(8,128)} %get-tuple-element.93) | copy-start | bytes 147460
  291.4 8.5 %copy-start.7 = (f32[1792]{0:T(1024)S(1)}, f32[1792]{0:T(1024)}, u32[]{:S(2)}) copy-start(f32[1792]{0:T(1024)} %mul.70) | copy-start | bytes 21508
  291.4 8.5 %copy-start.8 = (f32[1792]{0:T(1024)S(1)}, f32[1792]{0:T(1024)}, u32[]{:S(2)}) copy-start(f32[1792]{0:T(1024)} %mul.65) | copy-start | bytes 21508
  291.4 8.6 %copy-start.1 = (f32[3,16,1792]{2,1,0:T(8,128)S(1)}, f32[3,16,1792]{2,1,0:T(8,128)}, u32[]{:S(2)}) copy-start(f32[3,16,1792]{2,1,0:T(8,128)} %get-tuple-element.88) | copy-start | bytes 1032196
  320.7 9.5 %copy-start.9 = (f32[8,768]{1,0:T(8,128)S(1)}, f32[8,768]{1,0:T(8,128)}, u32[]{:S(2)}) copy-start(f32[8,768]{1,0:T(8,128)} %get-tuple-element.92) | copy-start | bytes 73732
  320.7 9.6 %copy-start.10 = (f32[72]{0:T(128)S(1)}, f32[72]{0:T(128)}, u32[]{:S(2)}) copy-start(f32[72]{0:T(128)} %pad_maximum_fusion.1) | copy-start | bytes 868
  320.7 9.6 %copy-start.4 = (f32[32,56]{1,0:T(8,128)S(1)}, f32[32,56]{1,0:T(8,128)}, u32[]{:S(2)}) copy-start(f32[32,56]{1,0:T(8,128)} %reshape.238) | copy-start | bytes 21508
  320.7 9.6 %copy-start.5 = (f32[32,48]{1,0:T(8,128)S(1)}, f32[32,48]{1,0:T(8,128)}, u32[]{:S(2)}) copy-start(f32[32,48]{1,0:T(8,128)} %reshape.237) | copy-start | bytes 18436
  397.0 10.3 %copy-start.2 = (f32[2,24,768]{2,1,0:T(8,128)S(1)}, f32[2,24,768]{2,1,0:T(8,128)}, u32[]{:S(2)}) copy-start(f32[2,24,768]{2,1,0:T(8,128)} %get-tuple-element.100) | copy-start | bytes 442372

commit v3 on v2

v3 whole, which is shorter than its diff:
```python
from functools import partial

import jax
import jax.numpy as jnp
from jax import lax
from jax.experimental import pallas as pl
from jax.experimental.pallas import tpu as pltpu
from jax.sharding import PartitionSpec as P

D = 768
NH = 24
HD = 64
NS = 128
DCONV = 4
CL = 128
DI = 1536
XBC = 1792
PROJ = 3352
XD = 1920
XA = 1024
LN = 128
EPSILON = 1e-05

F32 = jnp.float32
BF = jnp.bfloat16
SROWS = 144


def nn(a, b):
    return lax.dot_general(a, b, (((1,), (0,)), ((), ())), preferred_element_type=F32)


def nt(a, b):
    return lax.dot_general(a, b, (((1,), (1,)), ((), ())), preferred_element_type=F32)


def tn(a, b):
    return lax.dot_general(a, b, (((0,), (0,)), ((), ())), preferred_element_type=F32)


def exact_nn(a, b):
    return lax.dot_general(
        a, b, (((1,), (0,)), ((), ())), precision=lax.Precision.HIGHEST, preferred_element_type=F32
    )


def sigmoid(v):
    return 0.5 * jnp.tanh(0.5 * v) + 0.5


def halves(v):
    top = v.astype(BF)
    return top, (v - top.astype(F32)).astype(BF)


def three(op, a, b):
    ah, al = halves(a)
    bh, bl = halves(b)
    return op(ah, bh) + op(al, bh) + op(ah, bl)


def fill_expander(ref):
    head = lax.broadcasted_iota(jnp.int32, (LN, DI), 0)
    lane = lax.broadcasted_iota(jnp.int32, (LN, DI), 1)
    e = jnp.where(head == lane // HD, 1.0, 0.0).astype(BF)
    ref[0:LN] = e
    ref[LN:] = e


def expand(v, e2):
    return nn(jnp.concatenate(halves(v), axis=1), e2[...])


def lower_mask(strict):
    row = lax.broadcasted_iota(jnp.int32, (CL, CL), 0)
    col = lax.broadcasted_iota(jnp.int32, (CL, CL), 1)
    return row > col if strict else row >= col


def half_masks():
    lane = lax.broadcasted_iota(jnp.int32, (1, 2 * HD), 1)
    left = jnp.where(lane < HD, 1.0, 0.0).astype(BF)
    right = jnp.where(lane < HD, 0.0, 1.0).astype(BF)
    return left, right


def lanes(j):
    return slice(j * LN, (j + 1) * LN)


def conv_running(ci_ref, j, base, cw, cb):
    total = cb
    for tap in range(DCONV):
        total = total + ci_ref[j, pl.ds(base + 5 + tap, CL), :] * cw[tap : tap + 1]
    return total


MESH_ID = pl.DeviceIdType.MESH
BOTH = slice(None)


class Here:
    def __init__(self, depth):
        dp, seq = lax.axis_index("dp"), lax.axis_index("seq")
        self.depth = depth
        self.levels = depth.bit_length() - 1
        self.z, self.y = dp // 2, dp % 2
        self.x, self.c = seq // 2, seq % 2
        self.rank = dp * 4 + seq

    def device(self, z=None, y=None, x=None, c=None):
        z = self.z if z is None else z
        y = self.y if y is None else y
        x = self.x if x is None else x
        c = self.c if c is None else c
        return (z * 2 + y, x * 2 + c)

    def across(self, level):
        size = 1 << level
        return self.z + size * (1 - 2 * ((self.z // size) % 2))

    def block(self, level):
        size = 1 << level
        return (self.z // size) * size, size

    def block_across(self, level):
        size = 1 << level
        return (self.z // size) * size + size * (1 - 2 * ((self.z // size) % 2)), size

    def partners(self):
        near = [self.device(c=1 - self.c), self.device(x=1 - self.x), self.device(y=1 - self.y)]
        return near + [self.device(z=self.across(level)) for level in range(self.levels)]

    def greet_partners(self):
        barrier = pltpu.get_barrier_semaphore()
        others = self.partners()
        for other in others:
            pl.semaphore_signal(barrier, inc=1, device_id=other, device_id_type=MESH_ID)
        pl.semaphore_wait(barrier, len(others))

    def greet_all(self, ranks):
        barrier = pltpu.get_barrier_semaphore()

        def hail(i, carry):
            other = (self.rank + i) % ranks
            pl.semaphore_signal(barrier, inc=1, device_id=(other // 4, other % 4), device_id_type=MESH_ID)
            return carry

        lax.fori_loop(1, ranks, hail, 0)
        pl.semaphore_wait(barrier, ranks - 1)


class Plan:
    def __init__(self, send, recv):
        self.send, self.recv, self.made, self.segments = send, recv, [], [[]]

    def do(self, action):
        self.segments[-1].append(action)

    def copy(self, i, source, target, device):
        return pltpu.make_async_remote_copy(
            src_ref=source,
            dst_ref=target,
            send_sem=self.send.at[i],
            recv_sem=self.recv.at[i],
            device_id=device,
            device_id_type=MESH_ID,
        )

    def start(self, parts, device):
        waits = []
        for source, target, landing in parts:
            i = len(self.made)
            copy = self.copy(i, source, target, device)
            self.do(copy.start)
            self.made.append(copy)
            waits.append(self.copy(i, source, landing, device))
        return waits

    def arrived(self, waits):
        for w in waits:
            self.do(w.wait_recv)

    def trace(self, streams):
        streams = list(streams)
        while streams:
            for stream in list(streams):
                try:
                    next(stream)
                except StopIteration:
                    streams.remove(stream)
            self.segments.append([])

    def run(self, n):
        for action in self.segments[n]:
            action()

    def run_from(self, n):
        for k in range(n, len(self.segments)):
            self.run(k)
        for copy in self.made:
            copy.wait_send()


def everyone(rank, ranks, source, target, send, recv):
    def one(i):
        other = (rank + i) % ranks
        return pltpu.make_async_remote_copy(
            src_ref=source(other),
            dst_ref=target(rank),
            send_sem=send.at[i],
            recv_sem=recv.at[i],
            device_id=(other // 4, other % 4),
            device_id_type=MESH_ID,
        )

    def begin(i, carry):
        one(i).start()
        return carry

    def end(i, carry):
        copy = one(i)
        copy.wait_send()
        copy.wait_recv()
        return carry

    return (lambda: lax.fori_loop(1, ranks, begin, 0)), (lambda: lax.fori_loop(1, ranks, end, 0))


def gather_stream(here, plan, ref, first):
    z, y, x, c = here.z, here.y, here.x, here.c
    a_dev = here.device(x=1 - x) if first == "x" else here.device(y=1 - y)
    b_dev = here.device(y=1 - y) if first == "x" else here.device(x=1 - x)
    sibling = here.device(c=1 - c)
    cores = []

    def mine(zs, core):
        return ref.at[zs, y, x, core]

    def a_there(zs, core):
        return ref.at[zs, y, 1 - x, core] if first == "x" else ref.at[zs, 1 - y, x, core]

    def line(zs, core):
        return ref.at[zs, y, BOTH, core] if first == "x" else ref.at[zs, BOTH, x, core]

    def line_there(zs, core):
        return ref.at[zs, 1 - y, BOTH, core] if first == "x" else ref.at[zs, BOTH, 1 - x, core]

    def to_core(where, zs):
        cores.extend(plan.start([(where(zs, c), where(zs, c), where(zs, 1 - c))], sibling))

    def start_a(zs):
        waits = plan.start([(mine(zs, c), mine(zs, c), a_there(zs, c))], a_dev)
        to_core(mine, zs)
        return waits

    def start_b(zs, waits):
        plan.arrived(waits)
        out = plan.start([(line(zs, c), line(zs, c), line_there(zs, c))], b_dev)
        to_core(a_there, zs)
        return out

    sets = [pl.ds(z, 1)]
    waiting_a, waiting_b = [], []
    for level in range(here.levels):
        base, size = here.block(level)
        far, _ = here.block_across(level)
        own, theirs = pl.ds(base, size), pl.ds(far, size)
        zwait = plan.start([(mine(own, c), mine(own, c), mine(theirs, c))], here.device(z=here.across(level)))
        waiting_a.append((sets[-1], start_a(sets[-1])))
        sets.append(theirs)
        yield
        if level:
            zs, w = waiting_a.pop(0)
            waiting_b.append((zs, start_b(zs, w)))
        plan.arrived(zwait)
    waiting_a.append((sets[-1], start_a(sets[-1])))
    while waiting_a:
        yield
        zs, w = waiting_a.pop(0)
        waiting_b.append((zs, start_b(zs, w)))
    while waiting_b:
        yield
        zs, w = waiting_b.pop(0)
        plan.arrived(w)
        to_core(line_there, zs)
    yield
    plan.arrived(cores)


def gather_copies(levels):
    return 2 * (levels + 5 * (levels + 1))


def gather_kernel(
    w_in, small_in, xa_out, xb_out, small_out, xa_in, xb_in, send, recv, ssend, srecv, place_sem, *, depth, ranks
):
    here = Here(depth)
    xa_in[...] = w_in[:, DI : DI + XA].astype(BF)
    xb_in[...] = jnp.zeros_like(xb_in)
    xb_in[:, : PROJ - DI - XA] = w_in[:, DI + XA :].astype(BF)
    slot = (here.z, here.y, here.x, here.c)
    own = [
        pltpu.make_async_copy(xa_in, xa_out.at[slot], place_sem.at[0]),
        pltpu.make_async_copy(xb_in, xb_out.at[slot], place_sem.at[1]),
        pltpu.make_async_copy(small_in, small_out.at[here.rank], place_sem.at[2]),
    ]
    here.greet_all(ranks)
    for copy in own:
        copy.start()
    start, finish = everyone(here.rank, ranks, lambda other: small_in, lambda rank: small_out.at[rank], ssend, srecv)
    for copy in own:
        copy.wait()
    plan = Plan(send, recv)
    plan.trace([gather_stream(here, plan, xa_out, "x"), gather_stream(here, plan, xb_out, "y")])
    plan.run(0)
    start()
    plan.run_from(1)
    finish()


ANY = pl.BlockSpec(memory_space=pl.ANY)
IN_VMEM = pl.BlockSpec(memory_space=pltpu.VMEM)


def gather(w_in, small, depth):
    ranks = depth * 8
    rows = w_in.shape[0]
    lead = (depth, 2, 2, 2)
    sds = jax.ShapeDtypeStruct
    n = gather_copies(depth.bit_length() - 1)
    dma = pltpu.SemaphoreType.DMA
    return pl.pallas_call(
        partial(gather_kernel, depth=depth, ranks=ranks),
        in_specs=[IN_VMEM] * 2,
        out_specs=[ANY] * 3,
        out_shape=[
            sds(lead + (rows, XA), BF),
            sds(lead + (rows, XD - XA), BF),
            sds((ranks,) + small.shape, small.dtype),
        ],
        scratch_shapes=[
            pltpu.VMEM((rows, XA), BF),
            pltpu.VMEM((rows, XD - XA), BF),
            dma((n,)),
            dma((n,)),
            dma((ranks,)),
            dma((ranks,)),
            dma((3,)),
        ],
        compiler_params=pltpu.CompilerParams(collective_id=0, has_side_effects=True),
        name="gather",
    )(w_in, small)


def reduce_stream(here, plan, item, first):
    part, acc, core_in, line_in, side_in, z_in, put, own_sem = item
    z, y, x, c = here.z, here.y, here.x, here.c
    one_dev = here.device(y=1 - y) if first == "y" else here.device(x=1 - x)
    two_dev = here.device(x=1 - x) if first == "y" else here.device(y=1 - y)
    sibling = here.device(c=1 - c)
    sets = []
    for level in reversed(range(here.levels)):
        sets.append(here.block_across(level))
    sets.append((z, 1))
    slots = [pl.ds(zs[0], zs[1]) for zs in sets]
    mine = pltpu.make_async_copy(part.at[BOTH, BOTH, BOTH, c], acc, own_sem)
    plan.do(mine.start)

    def add(target, source):
        acc[target] = (acc[target].astype(F32) + source.astype(F32)).astype(BF)

    def line_add(zs):
        for k in range(zs[1]):
            for a in range(2):
                for b in range(2):
                    add((zs[0] + k, a, b), core_in[zs[0] + k, a, b])

    def side_add(zs):
        for k in range(zs[1]):
            for a in range(2):
                add((zs[0] + k, y, a) if first == "y" else (zs[0] + k, a, x), line_in[zs[0] + k, a])

    def last_add(zs):
        for k in range(zs[1]):
            add((zs[0] + k, y, x), side_in[zs[0] + k])

    cores = [plan.start([(part.at[s, BOTH, BOTH, 1 - c], core_in.at[s], core_in.at[s])], sibling) for s in slots]
    plan.do(mine.wait)
    yield
    lines, sides = [], []
    n = len(sets)
    for step in range(n + 2):
        if step < n:
            s = slots[step]
            plan.arrived(cores[step])
            plan.do(partial(line_add, sets[step]))
            give = acc.at[s, 1 - y, BOTH] if first == "y" else acc.at[s, BOTH, 1 - x]
            lines.append(plan.start([(give, line_in.at[s], line_in.at[s])], one_dev))
        if 1 <= step <= n:
            s = slots[step - 1]
            plan.arrived(lines[step - 1])
            plan.do(partial(side_add, sets[step - 1]))
            give = acc.at[s, y, 1 - x] if first == "y" else acc.at[s, 1 - y, x]
            sides.append(plan.start([(give, side_in.at[s], side_in.at[s])], two_dev))
        if step >= 2:
            plan.arrived(sides[step - 2])
            plan.do(partial(last_add, sets[step - 2]))
            if step == 2:
                level = here.levels - 1
                s, size = slots[0], sets[0][1]
                zwait = plan.start(
                    [(acc.at[s, y, x], z_in[0].at[0:size], z_in[0].at[0:size])], here.device(z=here.across(level))
                )
        yield

    def z_add(base, size, got):
        for k in range(size):
            add((base + k, y, x), got[k])

    def z_end(base, got):
        put(got[0].astype(F32) + acc[base, y, x].astype(F32))

    for at_level, level in enumerate(reversed(range(here.levels))):
        base, size = here.block(level)
        plan.arrived(zwait)
        if level:
            plan.do(partial(z_add, base, size, z_in[at_level]))
            far, size = here.block_across(level - 1)
            landing = z_in[at_level + 1].at[0:size]
            zwait = plan.start(
                [(acc.at[pl.ds(far, size), y, x], landing, landing)], here.device(z=here.across(level - 1))
            )
            yield
        else:
            plan.do(partial(z_end, base, z_in[at_level]))


def reduce_copies(levels):
    return 2 * (3 * (levels + 1) + levels)


def reduce_scratch(depth, tile):
    levels = depth.bit_length() - 1
    return [
        pltpu.VMEM((depth, 2, 2) + tile, BF),
        pltpu.VMEM((depth, 2, 2) + tile, BF),
        pltpu.VMEM((depth, 2) + tile, BF),
        pltpu.VMEM((depth,) + tile, BF),
    ] + [pltpu.VMEM((1 << level,) + tile, BF) for level in reversed(range(levels))]


def reduce_items(here, plan, parts, outs, scratch, own_sems):
    each = 4 + here.levels
    streams = []
    for k, first in enumerate(("y", "x")):
        bufs = scratch[k * each : (k + 1) * each]

        def put(v, k=k):
            outs[k][...] = v

        item = (parts[k], *bufs[:4], bufs[4:], put, own_sems.at[k])
        streams.append(reduce_stream(here, plan, item, first))
    plan.trace(streams)


def reduce_kernel(pa, pb, small_in, oa, ob, small_out, send, recv, ssend, srecv, small_got, own_sems, *scratch, depth, ranks):
    here = Here(depth)
    here.greet_all(ranks)
    start, finish = everyone(
        here.rank, ranks, lambda other: small_in.at[other], lambda rank: small_got.at[rank], ssend, srecv
    )
    plan = Plan(send, recv)
    reduce_items(here, plan, (pa, pb), (oa, ob), scratch, own_sems)
    plan.run(0)
    start()
    plan.run_from(1)
    finish()

    def add(i, total):
        return total + jnp.where(i == here.rank, small_in[i], small_got[i])

    small_out[...] = lax.fori_loop(0, ranks, add, jnp.zeros(small_out.shape, F32))


def reduce(pa, pb, small, depth):
    ranks = depth * 8
    sds = jax.ShapeDtypeStruct
    dma = pltpu.SemaphoreType.DMA
    n = reduce_copies(depth.bit_length() - 1)
    scratch = [dma((n,)), dma((n,)), dma((ranks,)), dma((ranks,)), pltpu.VMEM(small.shape, F32), dma((2,))]
    for part in (pa, pb):
        scratch += reduce_scratch(depth, part.shape[-2:])
    return pl.pallas_call(
        partial(reduce_kernel, depth=depth, ranks=ranks),
        in_specs=[ANY, ANY, IN_VMEM],
        out_specs=[IN_VMEM] * 3,
        out_shape=[sds(a.shape[4:], F32) for a in (pa, pb)] + [sds(small.shape[1:], F32)],
        scratch_shapes=scratch,
        compiler_params=pltpu.CompilerParams(collective_id=1, has_side_effects=True, vmem_limit_bytes=LIMIT),
        name="reduce",
    )(pa, pb, small)


def whole(shape):
    return pl.BlockSpec(shape, lambda i: (0,) * len(shape))


def kept(shape):
    return pl.BlockSpec(shape, lambda i: (0,) * len(shape), pipeline_mode=pl.Buffered(1))


def per(shape, first=0):
    rest = (0,) * len(shape)
    return pl.BlockSpec((None,) + shape, lambda i: (first + i,) + rest)


SMEM = pl.BlockSpec(memory_space=pltpu.SMEM)
LIMIT = 67_000_000


def project_kernel(
    vlen_ref,
    x_ref,
    xh_ref,
    g_ref,
    wa_ref,
    wb_ref,
    cw_ref,
    cb_ref,
    dtb_ref,
    rate_ref,
    win_ref,
    wo_ref,
    nrm_ref,
    ci_ref,
    act_ref,
    step_ref,
    l_ref,
    sig_ref,
    sloc_ref,
    s_ref,
    z_out,
    o_out,
    nx,
    xw,
    state,
    e2,
    z_in,
    o_in,
    send,
    recv,
    place_sem,
    *,
    first,
    count,
    depth,
):
    piece = x_ref.shape[0]
    chunks = piece // CL
    section = pl.program_id(0)
    valid = vlen_ref[first + section]
    here = Here(depth)
    slot = (here.z, here.y, here.x, here.c)
    own = [
        pltpu.make_async_copy(z_in, z_out.at[slot], place_sem.at[0]),
        pltpu.make_async_copy(o_in, o_out.at[slot], place_sem.at[1]),
    ]
    plan = Plan(send, recv)
    plan.trace([gather_stream(here, plan, z_out, "x"), gather_stream(here, plan, o_out, "y")])

    @pl.when(section == 0)
    def _():
        z_in[...] = win_ref[:, 0:DI].astype(BF)
        o_in[...] = wo_ref[...].astype(BF)
        here.greet_partners()
        for copy in own:
            copy.start()
        for copy in own:
            copy.wait()
        plan.run(0)

    def norm(v):
        v = v.astype(F32)
        r = lax.rsqrt(jnp.mean(v * v, axis=-1, keepdims=True) + EPSILON)
        return (v * r * g_ref[...]).astype(BF)

    nx[0:16] = norm(xh_ref[...])

    def norm_rows(i, c):
        rows = pl.ds(pl.multiple_of(i * 64, 64), 64)
        v = norm(x_ref[rows, :])
        nx[pl.ds(pl.multiple_of(i * 64 + 16, 16), 64), :] = v
        nrm_ref[rows, :] = v
        return c

    lax.fori_loop(0, piece // 64, norm_rows, 0)

    for j in range(XBC // 256):
        w = wa_ref[:, j * 256 : (j + 1) * 256] if j < XA // 256 else wb_ref[:, j * 256 - XA : (j + 1) * 256 - XA]
        ci = nn(nx[...], w)
        ci_ref[2 * j] = ci[8:, :LN]
        ci_ref[2 * j + 1] = ci[8:, LN:]
    dt_raw = nn(nx[16:], wb_ref[:, XBC - XA :]) + dtb_ref[...]
    row = lax.broadcasted_iota(jnp.int32, (piece, LN), 0)
    mask = jnp.where(row < valid, 1.0, 0.0)
    step_ref[...] = (jnp.maximum(dt_raw, 0.0) + jnp.log1p(jnp.exp(-jnp.abs(dt_raw)))) * mask
    sig_ref[...] = mask / (1.0 + jnp.exp(-dt_raw))

    @pl.when(pl.program_id(0) == 0)
    def _():
        fill_expander(e2)

    tri = jnp.where(lower_mask(False), 1.0, 0.0)
    state[...] = jnp.zeros_like(state)

    slots = count * chunks
    late = slots // 2 + 1
    steps = min(len(plan.segments) - 1, slots - late + 1)

    def chunk(k, total):
        base = pl.multiple_of(k * CL, CL)
        rows = pl.ds(base, CL)
        for n in range(steps):

            @pl.when(section * chunks + k == (late + n - 1 if n else 0))
            def _():
                plan.run(n + 1)

        step = step_ref[rows, :]
        ld = exact_nn(tri, step * rate_ref[...])
        l_ref[rows, :] = ld
        end = ld[CL - 1 :]
        tail = expand(step * jnp.exp(end - ld), e2)
        for j in range(XBC // LN):
            run = conv_running(ci_ref, j, base, cw_ref[:, lanes(j)], cb_ref[:, lanes(j)])
            act = run * sigmoid(run)
            act_ref[rows, lanes(j)] = act
            if j < DI // LN:
                xw[:, lanes(j)] = (act * tail[:, lanes(j)]).astype(BF)
        b = act_ref[rows, DI : DI + NS].astype(BF)
        sloc_ref[k] = state[...].astype(BF)
        keep = expand(jnp.exp(jnp.broadcast_to(end, (8, LN))), e2)[0:1]
        state[...] = keep * state[...] + tn(b, xw[...])
        return total + end

    total = lax.fori_loop(0, chunks, chunk, jnp.zeros((1, LN), F32))
    s_ref[0:NS] = state[...].astype(BF)
    keep = expand(jnp.exp(jnp.broadcast_to(total, (8, LN))), e2)[0:1]
    top, low = halves(keep)
    s_ref[NS : NS + 16] = jnp.concatenate([top, low, jnp.zeros((14, DI), BF)], axis=0)

    @pl.when(section == count - 1)
    def _():
        plan.run_from(steps + 1)


def project(first, count, depth, valid, tokens, halo, gain, wa, wb, cw, cb, dtb, rate, w_in, w_out):
    piece = tokens.shape[1]
    chunks = piece // CL
    lead = (depth, 2, 2, 2)
    n = gather_copies(depth.bit_length() - 1)
    sds = jax.ShapeDtypeStruct
    dma = pltpu.SemaphoreType.DMA
    return pl.pallas_call(
        partial(project_kernel, first=first, count=count, depth=depth),
        grid=(count,),
        in_specs=[
            SMEM,
            per((piece, D), first),
            per((16, D), first),
            whole((1, D)),
            kept((D, XA)),
            kept((D, XD - XA)),
            whole((DCONV, XBC)),
            whole((1, XBC)),
            whole((1, LN)),
            whole((1, LN)),
            kept(w_in.shape),
            kept(w_out.shape),
        ],
        out_specs=[
            per((piece, D)),
            per((XBC // LN, piece + 8, LN)),
            per((piece, XBC)),
            per((piece, LN)),
            per((piece, LN)),
            per((piece, LN)),
            per((chunks, NS, DI)),
            per((SROWS, DI)),
            ANY,
            ANY,
        ],
        out_shape=[
            sds((count, piece, D), BF),
            sds((count, XBC // LN, piece + 8, LN), F32),
            sds((count, piece, XBC), F32),
            sds((count, piece, LN), F32),
            sds((count, piece, LN), F32),
            sds((count, piece, LN), F32),
            sds((count, chunks, NS, DI), BF),
            sds((count, SROWS, DI), BF),
            sds(lead + (w_in.shape[0], DI), BF),
            sds(lead + w_out.shape, BF),
        ],
        scratch_shapes=[
            pltpu.VMEM((piece + 16, D), BF),
            pltpu.VMEM((CL, DI), BF),
            pltpu.VMEM((NS, DI), F32),
            pltpu.VMEM((2 * LN, DI), BF),
            pltpu.VMEM((w_in.shape[0], DI), BF),
            pltpu.VMEM(w_out.shape, BF),
            dma((n,)),
            dma((n,)),
            dma((2,)),
        ],
        compiler_params=pltpu.CompilerParams(vmem_limit_bytes=LIMIT, collective_id=4, has_side_effects=True),
        name="project",
    )(valid, tokens, halo, gain, wa, wb, cw, cb, dtb, rate, w_in, w_out)


class Exchange:
    def __init__(self, own, sib, out, got, swap_send, swap_recv, far_send, far_recv, giver):
        dp, seq = lax.axis_index("dp"), lax.axis_index("seq")
        self.x, self.c = seq // 2, seq % 2
        self.sibling = (dp, self.x * 2 + 1 - self.c)
        self.across = (dp, (1 - self.x) * 2 + self.c)
        self.own, self.sib, self.out, self.got = own, sib, out, got
        self.sems = (swap_send, swap_recv, far_send, far_recv)
        self.giver = giver

    def greet(self):
        barrier = pltpu.get_barrier_semaphore()
        for other in (self.sibling, self.across):
            pl.semaphore_signal(barrier, inc=1, device_id=other, device_id_type=pl.DeviceIdType.MESH)
        pl.semaphore_wait(barrier, 2)

    def swap(self, i):
        return pltpu.make_async_remote_copy(
            src_ref=self.own.at[i],
            dst_ref=self.sib.at[i],
            send_sem=self.sems[0].at[i],
            recv_sem=self.sems[1].at[i],
            device_id=self.sibling,
            device_id_type=pl.DeviceIdType.MESH,
        )

    def far(self, i):
        return pltpu.make_async_remote_copy(
            src_ref=self.out.at[i],
            dst_ref=self.got.at[i],
            send_sem=self.sems[2].at[i],
            recv_sem=self.sems[3].at[i],
            device_id=self.across,
            device_id_type=pl.DeviceIdType.MESH,
        )

    def decay(self, ref, i):
        return ref[i, NS : NS + 1].astype(F32) + ref[i, NS + 1 : NS + 2].astype(F32)

    def begin(self, count):
        for i in range(count):
            self.swap(i).start()

    def hand_over(self, i, coefficients):
        self.swap(i).wait_recv()

        @pl.when(self.x == self.giver)
        def _():
            f, g = coefficients(self.decay(self.own, i), self.decay(self.sib, i))
            self.out[i] = (f * self.own[i, 0:NS].astype(F32) + g * self.sib[i, 0:NS].astype(F32)).astype(BF)
            self.far(i).start()

    def end(self, count):
        for i in range(count):
            self.swap(i).wait_send()

            @pl.when(self.x == self.giver)
            def _():
                self.far(i).wait_send()


def exchange_scratch(count):
    dma = pltpu.SemaphoreType.DMA((count,))
    return [
        pltpu.VMEM((count, SROWS, DI), BF),
        pltpu.VMEM((count, NS, DI), BF),
        pltpu.VMEM((count, NS, DI), BF),
        dma,
        dma,
        dma,
        dma,
    ]


def mix_kernel(
    vlen_ref,
    x_ref,
    cot_ref,
    nrm_ref,
    act_ref,
    step_ref,
    l_ref,
    sloc_ref,
    s_ref,
    wz_ref,
    wo_ref,
    gg_ref,
    dsk_ref,
    out_ref,
    gn_ref,
    dbr_ref,
    dz_ref,
    dy_ref,
    y_ref,
    incoming,
    dsin_ref,
    ggrad_ref,
    zs,
    dgn,
    dsacc,
    yf,
    work,
    e2,
    sib,
    out,
    got,
    *sems,
    first,
    count,
):
    piece = x_ref.shape[0]
    chunks = piece // CL
    section = pl.program_id(0)
    valid = vlen_ref[first + section]
    states = Exchange(s_ref, sib, out, got, *sems, giver=0)
    even = states.c == 0
    weigh = lambda own, sibs: (jnp.where(even, sibs, 1.0), jnp.where(even, 1.0, own))

    @pl.when(section == 0)
    def _():
        ggrad_ref[...] = jnp.zeros_like(ggrad_ref)
        fill_expander(e2)
        states.greet()
        states.begin(count)
        states.hand_over(0, weigh)

    row = lax.broadcasted_iota(jnp.int32, (piece, 1), 0)
    live = row < valid
    dbr_ref[...] = jnp.where(live, cot_ref[...].astype(F32), 0.0).astype(BF)
    for j in range(DI // 256):
        cols = slice(j * 256, (j + 1) * 256)
        zs[:, cols] = nn(nrm_ref[...], wz_ref[:, cols])
        dgn[:, cols] = nt(dbr_ref[...], wo_ref[cols, :])

    @pl.when(states.x == 0)
    def _():
        incoming[...] = jnp.where(even, 0.0, 1.0) * sib[section, 0:NS].astype(F32)

    @pl.when(states.x == 1)
    def _():
        states.far(section).wait_recv()
        f = jnp.where(even, 1.0, states.decay(sib, section))
        incoming[...] = f * got[section].astype(F32) + jnp.where(even, 0.0, 1.0) * sib[section, 0:NS].astype(F32)

    low = lower_mask(False)
    left, right = half_masks()
    dsacc[...] = jnp.zeros_like(dsacc)

    def chunk(k, before):
        base = pl.multiple_of(k * CL, CL)
        rows = pl.ds(base, CL)
        for n in range(1, count):

            @pl.when((section == 0) & (k == n - 1))
            def _():
                states.hand_over(n, weigh)

        step = step_ref[rows, :]
        ld = l_ref[rows, :]
        ldt = ld.T
        start = (before * incoming[...] + sloc_ref[k].astype(F32)).astype(BF)
        step_e = expand(step, e2)
        grow = expand(jnp.exp(ld), e2)
        b = act_ref[rows, DI : DI + NS].astype(BF)
        c, c_low = halves(act_ref[rows, DI + NS :])
        scores = jnp.where(low, nt(c, b), 0.0)
        squares = jnp.zeros((CL, LN), F32)
        for j in range(DI // LN):
            x = act_ref[rows, lanes(j)]
            xd = (x * step_e[:, lanes(j)]).astype(BF)
            mixes = []
            for h in (2 * j, 2 * j + 1):
                gap = jnp.minimum(ld[:, h : h + 1] - ldt[h : h + 1, :], 0.0)
                mixes.append((jnp.exp(gap) * scores).astype(BF))
            block = jnp.concatenate([xd * left, xd * right], axis=0)
            st = start[:, lanes(j)]
            y = nn(jnp.concatenate(mixes, axis=1), block) + (nn(c, st) + nn(c_low, st)) * grow[:, lanes(j)]
            y_ref[rows, lanes(j)] = y
            full = y + dsk_ref[:, lanes(j)] * x
            yf[:, lanes(j)] = full
            z = zs[rows, lanes(j)]
            u = full * (z * sigmoid(z))
            squares = squares + u * u
        r = lax.rsqrt(jnp.sum(squares, axis=-1, keepdims=True) * (1.0 / DI) + EPSILON)
        inner = jnp.zeros((CL, LN), F32)
        for j in range(DI // LN):
            z = zs[rows, lanes(j)]
            v = yf[:, lanes(j)] * (z * sigmoid(z)) * r
            gain = gg_ref[:, lanes(j)]
            gn_ref[rows, lanes(j)] = (v * gain).astype(BF)
            dg = dgn[rows, lanes(j)]
            gv = dg * v
            ggrad_ref[:, lanes(j)] += jnp.sum(gv.reshape(CL // 8, 8, LN), axis=0)
            inner = inner + gv * gain
        q = jnp.sum(inner, axis=-1, keepdims=True) * (1.0 / DI)
        for j in range(DI // LN):
            z = zs[rows, lanes(j)]
            s = sigmoid(z)
            sz = z * s
            full = yf[:, lanes(j)]
            v = full * sz * r
            du = r * (dgn[rows, lanes(j)] * gg_ref[:, lanes(j)] - v * q)
            dy = du * sz
            dy_ref[rows, lanes(j)] = dy
            dz_ref[rows, lanes(j)] = (du * full * (s + sz * (1.0 - s))).astype(BF)
            work[:, lanes(j)] = (dy * grow[:, lanes(j)]).astype(BF)
        dsacc[...] += before * tn(c, work[...])
        return before * grow[CL - 1 :]

    lax.fori_loop(0, chunks, chunk, jnp.ones((1, DI), F32))
    dsin_ref[0:NS] = dsacc[...].astype(BF)
    dsin_ref[NS:] = s_ref[section, NS:]
    for j in range(D // 256):
        cols = slice(j * 256, (j + 1) * 256)
        branch = nn(gn_ref[...], wo_ref[:, cols])
        out_ref[:, cols] = jnp.where(live, x_ref[:, cols].astype(F32) + branch, 0.0).astype(BF)

    @pl.when(section == count - 1)
    def _():
        states.end(count)


def mix(first, count, valid, tokens, cot, normed, act, step, ld, sloc, s, w_z, w_o, gg, dsk):
    piece = tokens.shape[1]
    chunks = piece // CL
    sds = jax.ShapeDtypeStruct
    return pl.pallas_call(
        partial(mix_kernel, first=first, count=count),
        grid=(count,),
        in_specs=[
            SMEM,
            per((piece, D), first),
            per((piece, D), first),
            per((piece, D)),
            per((piece, XBC)),
            per((piece, LN)),
            per((piece, LN)),
            per((chunks, NS, DI)),
            kept((count, SROWS, DI)),
            kept((D, DI)),
            kept((DI, D)),
            whole((1, DI)),
            whole((1, DI)),
        ],
        out_specs=[
            per((piece, D)),
            per((piece, DI)),
            per((piece, D)),
            per((piece, DI)),
            per((piece, DI)),
            per((piece, DI)),
            per((NS, DI)),
            per((SROWS, DI)),
            whole((8, DI)),
        ],
        out_shape=[
            sds((count, piece, D), BF),
            sds((count, piece, DI), BF),
            sds((count, piece, D), BF),
            sds((count, piece, DI), BF),
            sds((count, piece, DI), F32),
            sds((count, piece, DI), F32),
            sds((count, NS, DI), F32),
            sds((count, SROWS, DI), BF),
            sds((8, DI), F32),
        ],
        scratch_shapes=[
            pltpu.VMEM((piece, DI), F32),
            pltpu.VMEM((piece, DI), F32),
            pltpu.VMEM((NS, DI), F32),
            pltpu.VMEM((CL, DI), F32),
            pltpu.VMEM((CL, DI), BF),
            pltpu.VMEM((2 * LN, DI), BF),
        ]
        + exchange_scratch(count),
        compiler_params=pltpu.CompilerParams(vmem_limit_bytes=LIMIT, collective_id=2, has_side_effects=True),
        name="mix",
    )(valid, tokens, cot, normed, act, step, ld, sloc, s, w_z, w_o, gg, dsk)


def scan_back_kernel(
    ci_ref,
    step_ref,
    l_ref,
    sig_ref,
    dy_ref,
    y_ref,
    inc_ref,
    sloc_ref,
    dsin_ref,
    cw_ref,
    cb_ref,
    rate_ref,
    dsk_ref,
    part_a,
    part_b,
    dxa_ref,
    dxb_ref,
    fix_ref,
    edge_ref,
    cgrad_ref,
    hgrad_ref,
    skip_ref,
    shard_a,
    shard_b,
    ds,
    xa,
    dsl,
    dact,
    xdt,
    xt,
    dr,
    e2,
    u_top,
    u_low,
    fs,
    vs,
    dyg,
    start,
    sib,
    out,
    got,
    swap_send,
    swap_recv,
    far_send,
    far_recv,
    send,
    recv,
    own_sems,
    *scratch,
    count,
    depth,
):
    piece = dy_ref.shape[0]
    chunks = piece // CL
    section = pl.program_id(0)
    states = Exchange(dsin_ref, sib, out, got, swap_send, swap_recv, far_send, far_recv, giver=1)
    here = Here(depth)
    plan = Plan(send, recv)
    reduce_items(here, plan, (part_a, part_b), (shard_a, shard_b), scratch, own_sems)
    even = states.c == 0
    one_if_even = jnp.where(even, 1.0, 0.0)
    weigh = lambda own, sibs: (jnp.where(even, 1.0, sibs), jnp.where(even, own, 1.0))

    @pl.when(section == 0)
    def _():
        cgrad_ref[...] = jnp.zeros_like(cgrad_ref)
        hgrad_ref[...] = jnp.zeros_like(hgrad_ref)
        skip_ref[...] = jnp.zeros_like(skip_ref)
        fill_expander(e2)
        here.greet_partners()
        states.begin(count)
        plan.run(0)
        states.hand_over(0, weigh)

    upper = jnp.logical_not(lower_mask(True))
    upper_one = jnp.where(upper, 1.0, 0.0)
    before_one = jnp.where(lower_mask(True), 1.0, 0.0)
    left, right = half_masks()
    dr[:, CL:] = jnp.zeros((XBC // LN, 8, LN), F32)
    steps = min(len(plan.segments) - 1, count * chunks)

    def chunk(i, carry):
        k = chunks - 1 - i
        base = pl.multiple_of(k * CL, CL)
        rows = pl.ds(base, CL)
        for n in range(steps):

            @pl.when(section * chunks + i == n)
            def _():
                plan.run(n + 1)

        for n in range(1, count):

            @pl.when((section == 0) & (i == n))
            def _():
                states.hand_over(n, weigh)

        step = step_ref[rows, :]
        ld = l_ref[rows, :]
        ldt = ld.T
        end = ld[CL - 1 :]
        prefix = jnp.zeros((8, LN), F32)
        for j in range(chunks - 1):
            prefix = prefix + jnp.where(j < k, 1.0, 0.0) * l_ref[j * CL + CL - 1 : j * CL + CL, :]
        before = expand(jnp.exp(prefix), e2)[0:1]
        start[...] = before * inc_ref[...] + sloc_ref[k].astype(F32)
        step_e = expand(step, e2)
        grow = expand(jnp.exp(ld), e2)
        tail = expand(jnp.exp(end - ld), e2)
        keep = grow[CL - 1 :]
        for j in range(XBC // LN):
            run = conv_running(ci_ref, j, base, cw_ref[:, lanes(j)], cb_ref[:, lanes(j)])
            s = sigmoid(run)
            a = run * s
            xa[:, lanes(j)] = a
            dsl[:, lanes(j)] = s + a * (1.0 - s)
            if j < DI // LN:
                xd = a * step_e[:, lanes(j)]
                xdt[:, lanes(j)] = xd
                xt[:, lanes(j)] = xd * tail[:, lanes(j)]

        @pl.when((i == 0) & (states.x == 1))
        def _():
            ds[...] = one_if_even * sib[section, 0:NS].astype(F32)

        @pl.when((i == 0) & (states.x == 0))
        def _():
            states.far(section).wait_recv()
            f = jnp.where(even, states.decay(sib, section), 1.0)
            ds[...] = f * got[section].astype(F32) + one_if_even * sib[section, 0:NS].astype(F32)

        b = xa[:, DI : DI + NS].astype(BF)
        c = xa[:, DI + NS :].astype(BF)
        scores = jnp.where(upper, nt(b, c), 0.0)
        dact[:, 0:DI] = nn(b, ds[...].astype(BF)) * tail
        dscores = jnp.zeros((CL, CL), F32)
        for j in range(DI // LN):
            dyf = dy_ref[rows, lanes(j)]
            dyb, dyl = halves(dyf)
            block = jnp.concatenate([dyb * left, dyb * right], axis=0)
            block_low = jnp.concatenate([dyl * left, dyl * right], axis=0)
            xdb, xdl = halves(xdt[:, lanes(j)])
            dmix = nt(jnp.concatenate([xdb, xdl], axis=1), jnp.concatenate([block, block], axis=1)) + nt(xdb, block_low)
            mixes = []
            for p, h in enumerate((2 * j, 2 * j + 1)):
                gap = jnp.minimum(ldt[h : h + 1, :] - ld[:, h : h + 1], 0.0)
                w = jnp.exp(gap)
                mixes.append((w * scores).astype(BF))
                dscores = dscores + dmix[:, lanes(p)] * w
            diag = nn(jnp.concatenate(mixes, axis=1), block)
            far = dact[:, lanes(j)]
            xdf = xdb.astype(F32)
            u_top[:, lanes(j)], u_low[:, lanes(j)] = halves(dyb.astype(F32) * y_ref[rows, lanes(j)] - xdf * diag)
            fs[:, lanes(j)] = (xdf * far).astype(BF)
            dxd = diag + far
            x = xa[:, lanes(j)]
            vs[:, lanes(j)] = (x * dxd).astype(BF)
            dact[:, lanes(j)] = dxd * step_e[:, lanes(j)] + dsk_ref[:, lanes(j)] * dyf
            skip_ref[:, lanes(j)] += jnp.sum((dyf * x).reshape(CL // 8, 8, LN), axis=0)
            dyg[:, lanes(j)] = dyf * grow[:, lanes(j)]
        e = e2[0:LN]
        const = jnp.sum((start[...] * ds[...]).reshape(NS // 8, 8, DI), axis=0) * keep
        c_top, c_low = halves(const)
        r_c = jnp.sum(nt(c_top, e) + nt(c_low, e), axis=0, keepdims=True)
        r_u = nt(u_top[...], e) + nt(u_low[...], e)
        r_f = nt(fs[...], e)
        r_v = nt(vs[...], e)
        db = three(nt, xt[...], ds[...])
        dc = three(nt, dyg[...], start[...])
        ds[...] = keep * ds[...] + tn(c, dyg[...].astype(BF))
        dsc = jnp.where(upper, dscores, 0.0).astype(BF)
        dact[:, DI : DI + NS] = db + nn(dsc, c)
        dact[:, DI + NS :] = dc + tn(dsc, b)
        da = exact_nn(upper_one, r_u) + exact_nn(before_one, r_f) + r_c
        dstep = r_v + rate_ref[...] * da
        ddt = dstep * sig_ref[rows, :]
        hgrad_ref[0:8] += jnp.sum(ddt.reshape(CL // 8, 8, LN), axis=0)
        hgrad_ref[8:16] += jnp.sum((da * step).reshape(CL // 8, 8, LN), axis=0)
        dxb_ref[rows, XBC - XA :] = ddt.astype(BF)
        for j in range(XBC // LN):
            g = dact[:, lanes(j)] * dsl[:, lanes(j)]
            dr[j, 0:CL] = g
            ci = ci_ref[j, pl.ds(base + 8, CL), :]
            total = g * cw_ref[DCONV - 1 : DCONV, lanes(j)]
            last = 8 * (DCONV - 1)
            cgrad_ref[last : last + 8, lanes(j)] += jnp.sum((g * ci).reshape(CL // 8, 8, LN), axis=0)
            for tap in range(DCONV - 1):
                later = DCONV - 1 - tap
                shifted = dr[j, later : later + CL, :]
                total = total + shifted * cw_ref[tap : tap + 1, lanes(j)]
                cgrad_ref[8 * tap : 8 * tap + 8, lanes(j)] += jnp.sum((shifted * ci).reshape(CL // 8, 8, LN), axis=0)
            cgrad_ref[32:40, lanes(j)] += jnp.sum(g.reshape(CL // 8, 8, LN), axis=0)
            if j < XA // LN:
                dxa_ref[rows, lanes(j)] = total.astype(BF)
            else:
                dxb_ref[rows, lanes(j - XA // LN)] = total.astype(BF)

            @pl.when(i == 0)
            def _():
                fix_ref[:, lanes(j)] = total[CL - 16 :]

            dr[j, CL:] = g[0:8]
        return carry

    lax.fori_loop(0, chunks, chunk, 0)
    for j in range(XBC // LN):
        edge_ref[:, lanes(j)] = dr[j, CL:]
        for tap in range(DCONV - 1):
            later = DCONV - 1 - tap
            part = dr[j, CL : CL + later] * ci_ref[j, 8 - later : 8]
            cgrad_ref[8 * tap : 8 * tap + 1, lanes(j)] += jnp.sum(part, axis=0, keepdims=True)

    @pl.when(section == count - 1)
    def _():
        states.end(count)
        plan.run_from(steps + 1)


def scan_back(count, depth, ci, step, ld, sig, dy, y, inc, sloc, dsin, cw, cb, rate, dsk, part_a, part_b):
    piece = dy.shape[1]
    chunks = piece // CL
    n = reduce_copies(depth.bit_length() - 1)
    sds = jax.ShapeDtypeStruct
    dma = pltpu.SemaphoreType.DMA
    return pl.pallas_call(
        partial(scan_back_kernel, count=count, depth=depth),
        grid=(count,),
        in_specs=[
            per((XBC // LN, piece + 8, LN)),
            per((piece, LN)),
            per((piece, LN)),
            per((piece, LN)),
            per((piece, DI)),
            per((piece, DI)),
            per((NS, DI)),
            per((chunks, NS, DI)),
            kept((count, SROWS, DI)),
            whole((DCONV, XBC)),
            whole((1, XBC)),
            whole((1, LN)),
            whole((1, DI)),
            ANY,
            ANY,
        ],
        out_specs=[
            per((piece, XA)),
            per((piece, XD - XA)),
            per((16, XBC)),
            per((8, XBC)),
            whole((40, XBC)),
            whole((16, LN)),
            whole((8, DI)),
            whole(part_a.shape[4:]),
            whole(part_b.shape[4:]),
        ],
        out_shape=[
            sds((count, piece, XA), BF),
            sds((count, piece, XD - XA), BF),
            sds((count, 16, XBC), F32),
            sds((count, 8, XBC), F32),
            sds((40, XBC), F32),
            sds((16, LN), F32),
            sds((8, DI), F32),
            sds(part_a.shape[4:], F32),
            sds(part_b.shape[4:], F32),
        ],
        scratch_shapes=[
            pltpu.VMEM((NS, DI), F32),
            pltpu.VMEM((CL, XBC), F32),
            pltpu.VMEM((CL, XBC), F32),
            pltpu.VMEM((CL, XBC), F32),
            pltpu.VMEM((CL, DI), F32),
            pltpu.VMEM((CL, DI), F32),
            pltpu.VMEM((XBC // LN, CL + 8, LN), F32),
            pltpu.VMEM((2 * LN, DI), BF),
            pltpu.VMEM((CL, DI), BF),
            pltpu.VMEM((CL, DI), BF),
            pltpu.VMEM((CL, DI), BF),
            pltpu.VMEM((CL, DI), BF),
            pltpu.VMEM((CL, DI), F32),
            pltpu.VMEM((NS, DI), F32),
        ]
        + exchange_scratch(count)
        + [dma((n,)), dma((n,)), dma((2,))]
        + reduce_scratch(depth, part_a.shape[-2:])
        + reduce_scratch(depth, part_b.shape[-2:]),
        compiler_params=pltpu.CompilerParams(vmem_limit_bytes=LIMIT, collective_id=3, has_side_effects=True),
        name="scan_back",
    )(ci, step, ld, sig, dy, y, inc, sloc, dsin, cw, cb, rate, dsk, part_a, part_b)


def patch_kernel(a_ref, b_ref, fix_ref, edge_ref, cw_ref, oa_ref, ob_ref, work):
    work[0:13] = fix_ref[0:13]
    for j in range(DCONV - 1):
        row = fix_ref[13 + j : 14 + j]
        for tap in range(j + 1):
            row = row + cw_ref[tap : tap + 1] * edge_ref[j - tap : j - tap + 1]
        work[13 + j : 14 + j] = row
    oa_ref[...] = work[:, :XA].astype(BF)
    ob_ref[:, : XBC - XA] = work[:, XA:].astype(BF)
    ob_ref[:, XBC - XA :] = b_ref[:, XBC - XA :]


def patch(dxa, dxb, fix, edge, cw):
    count, piece, _ = dxa.shape
    last = piece // 16 - 1
    tail = lambda n: pl.BlockSpec((None, 16, n), lambda i: (i, last, 0))
    return pl.pallas_call(
        patch_kernel,
        grid=(count,),
        in_specs=[tail(XA), tail(XD - XA), per((16, XBC)), per((8, XBC)), whole((DCONV, XBC))],
        out_specs=[tail(XA), tail(XD - XA)],
        out_shape=[jax.ShapeDtypeStruct(a.shape, BF) for a in (dxa, dxb)],
        scratch_shapes=[pltpu.VMEM((16, XBC), F32)],
        input_output_aliases={0: 0, 1: 1},
        name="patch",
    )(dxa, dxb, fix, edge, cw)


def input_grad_kernel(x_ref, dbr_ref, g_ref, dz_ref, dxa_ref, dxb_ref, wz_ref, wa_ref, wb_ref, out_ref, gain_ref, dn):
    piece = x_ref.shape[0]

    @pl.when(pl.program_id(0) == 0)
    def _():
        gain_ref[...] = jnp.zeros_like(gain_ref)

    for j in range(D // 256):
        cols = slice(j * 256, (j + 1) * 256)
        dn[:, cols] = (
            nt(dz_ref[...], wz_ref[cols, :]) + nt(dxa_ref[...], wa_ref[cols, :]) + nt(dxb_ref[...], wb_ref[cols, :])
        )

    def rows_of(i, c):
        rows = pl.ds(pl.multiple_of(i * 64, 64), 64)
        x = x_ref[rows, :].astype(F32)
        d = dn[rows, :]
        r = lax.rsqrt(jnp.mean(x * x, axis=-1, keepdims=True) + EPSILON)
        v = x * r
        gain_ref[...] += jnp.sum((d * v).reshape(8, 8, D), axis=0)
        dv = d * g_ref[...]
        q = jnp.mean(dv * v, axis=-1, keepdims=True)
        out_ref[rows, :] = (dbr_ref[rows, :].astype(F32) + r * (dv - v * q)).astype(BF)
        return c

    lax.fori_loop(0, piece // 64, rows_of, 0)


def input_grad(first, count, tokens, dbr, gain, dz, dxa, dxb, w_z, wa, wb):
    piece = tokens.shape[1]
    sds = jax.ShapeDtypeStruct
    return pl.pallas_call(
        input_grad_kernel,
        grid=(count,),
        in_specs=[
            per((piece, D), first),
            per((piece, D)),
            whole((1, D)),
            per((piece, DI)),
            per((piece, XA)),
            per((piece, XD - XA)),
            kept((D, DI)),
            kept((D, XA)),
            kept((D, XD - XA)),
        ],
        out_specs=[per((piece, D)), whole((8, D))],
        out_shape=[sds((count, piece, D), BF), sds((8, D), F32)],
        scratch_shapes=[pltpu.VMEM((piece, D), F32)],
        compiler_params=pltpu.CompilerParams(vmem_limit_bytes=LIMIT),
        name="input_grad",
    )(tokens, dbr, gain, dz, dxa, dxb, w_z, wa, wb)


def assemble_kernel(z, a, b, o, t, win, wo, g0, g1, g2, g3, h0, h1, h2):
    win[:, 0:DI] = z[...]
    win[:, DI : DI + XA] = a[...]
    win[:, DI + XA :] = b[:, : PROJ - DI - XA]
    wo[...] = o[...]
    g0[...] = t[0:1, : g0.shape[1]]
    g1[...] = t[1:2, : g1.shape[1]]
    g2[...] = t[2:3, : g2.shape[1]]
    g3[...] = t[3 : 3 + DCONV, : g3.shape[1]]
    last = t[7:8, :]
    h0[...] = last[:, 0:NH]
    h1[...] = last[:, NH : 2 * NH]
    h2[...] = last[:, 2 * NH : 3 * NH]


def assemble(z, a, b, o, t, n0, n1, n2):
    shapes = [(z.shape[0], PROJ), o.shape, (1, n0), (1, n1), (1, n2), (DCONV, n2), (1, NH), (1, NH), (1, NH)]
    return pl.pallas_call(
        assemble_kernel,
        in_specs=[IN_VMEM] * 5,
        out_specs=[IN_VMEM] * 9,
        out_shape=[jax.ShapeDtypeStruct(v, F32) for v in shapes],
        name="assemble",
    )(z, a, b, o, t)


def pass_on(block, axis, distance):
    devices = range(lax.axis_size(axis))
    route = [(i - distance, i) for i in devices if i - distance in devices]
    return lax.ppermute(block, axis, route)


def contract_rows(left, right):
    return lax.dot_general(left, right, (((0, 1), (0, 1)), ((), ())), preferred_element_type=F32)


def local(
    tokens,
    norm_gain,
    w_in,
    conv_weight,
    conv_bias,
    dt_bias,
    a_log,
    d_skip,
    gated_gain,
    w_out,
    lengths,
    cotangent,
):
    ranks = lax.axis_size("dp") * lax.axis_size("seq")
    place = lax.axis_index("seq")
    tokens = tokens[:, 0]
    cot = cotangent[:, 0]
    batches, piece, _ = tokens.shape
    rows = w_in.shape[0]

    depth = lax.axis_size("dp") // 2
    n0, n1, n2 = norm_gain.shape[0], gated_gain.shape[0], conv_bias.shape[0]
    widen = lambda v: jnp.pad(v, ((0, 0), (0, LN - v.shape[1])))
    small = [norm_gain[None], gated_gain[None], conv_bias[None], conv_weight]
    small = jnp.pad(jnp.concatenate([widen(v) for v in small]), ((0, 1), (0, 0)))
    wa, wb, small = gather(w_in, small, depth)
    wa, wb = wa.reshape(D, XA), wb.reshape(D, XD - XA)
    gain = small[:, 0, :n0].reshape(1, D)
    gg = small[:, 1, :n1].reshape(1, DI)
    cb = small[:, 2, :n2].reshape(1, XBC)
    cw = small[:, 3 : 3 + DCONV, :n2].transpose(1, 0, 2).reshape(DCONV, XBC)

    halo = pass_on(tokens[:, piece - 16 :], "seq", 1)
    valid = lengths[:, 0].astype(jnp.int32) - place.astype(jnp.int32) * piece
    lane_pad = ((0, 0), (0, LN - NH))
    dtb = jnp.pad(dt_bias[None], lane_pad)
    rate = -jnp.exp(a_log)
    rate_row = jnp.pad(rate[None], lane_pad)
    dsk = jnp.repeat(d_skip, HD)[None]

    first, count = 0, batches
    normed, ci, act, step, ld, sig, sloc, s, w_z, w_o = project(
        first, count, depth, valid, tokens, halo, gain, wa, wb, cw, cb, dtb, rate_row, w_in, w_out
    )
    w_z, w_o = w_z.reshape(D, DI), w_o.reshape(DI, D)
    out, gn, dbr, dz, dy, y, inc, dsin, ggrad = mix(
        first, count, valid, tokens, cot, normed, act, step, ld, sloc, s, w_z, w_o, gg, dsk
    )
    lead = (depth, 2, 2, 2)
    grad_wo = contract_rows(gn, dbr).astype(BF).reshape(lead + (n1, D))
    grad_wz = contract_rows(normed, dz).astype(BF).reshape(lead + (rows, DI))
    dxa, dxb, fix, edge, cgrad, hgrad, skip, shard_wo, shard_wz = scan_back(
        count, depth, ci, step, ld, sig, dy, y, inc, sloc, dsin, cw, cb, rate_row, dsk, grad_wo, grad_wz
    )
    dxa, dxb = patch(dxa, dxb, fix, pass_on(edge, "seq", -1), cw)
    tgrad, gain_grad = input_grad(first, count, tokens, dbr, gain, dz, dxa, dxb, w_z, wa, wb)
    grad_wa = contract_rows(normed, dxa).astype(BF).reshape(lead + (rows, XA))
    grad_wb = contract_rows(normed, dxb).astype(BF).reshape(lead + (rows, XD - XA))

    grad_cw = cgrad[:32].reshape(DCONV, 8, XBC).sum(1)
    heads = hgrad.reshape(2, 8, LN).sum(1)[:, :NH]
    heads = jnp.concatenate([heads[0], heads[1] * rate, skip.sum(0).reshape(NH, HD).sum(1)])
    split = lambda v, n: jnp.pad(v.reshape(-1, ranks, n).transpose(1, 0, 2), ((0, 0), (0, 0), (0, LN - n)))
    packed = jnp.concatenate(
        [
            split(gain_grad.sum(0), n0),
            split(ggrad.sum(0), n1),
            split(cgrad[32:].sum(0), n2),
            split(grad_cw, n2),
            jnp.broadcast_to(jnp.pad(heads, (0, LN - 3 * NH)), (ranks, 1, LN)),
        ],
        axis=1,
    )
    shard_wa, shard_wb, total = reduce(grad_wa, grad_wb, packed, depth)
    shard_win, shard_wo, g0, g1, g2, g3, h0, h1, h2 = assemble(shard_wz, shard_wa, shard_wb, shard_wo, total, n0, n1, n2)
    return (
        out[:, None],
        tgrad[:, None],
        g0.reshape(n0),
        shard_win,
        g3,
        g2.reshape(n2),
        h0.reshape(NH),
        h1.reshape(NH),
        h2.reshape(NH),
        g1.reshape(n1),
        shard_wo,
    )


def solution(mesh):
    shard = P(("dp", "seq"))
    row_shard = P(("dp", "seq"), None)
    col_shard = P(None, ("dp", "seq"))
    acts = P(None, "dp", "seq", None)
    return jax.shard_map(
        local,
        mesh=mesh,
        in_specs=(
            acts,
            shard,
            row_shard,
            col_shard,
            shard,
            P(),
            P(),
            P(),
            shard,
            row_shard,
            P(None, "dp"),
            acts,
        ),
        out_specs=(
            acts,
            acts,
            shard,
            row_shard,
            col_shard,
            shard,
            P(),
            P(),
            P(),
            shard,
            row_shard,
        ),
        check_vma=False,
    )
```

time: 409 us -> 356 us (0.87)
  Pallas kernels: 343 us -> 301 us
  local copies, waits for them, and re-layouts: 24.2 us -> 17.6 us
  other arithmetic: 12.5 us -> 6.95 us
    pallas_call x1, Pallas kernels: 63.1 us -> 34.7 us  [gather(): pl.pallas_call(partial(gather_kernel, depth=depth, ranks=ranks), in_specs...]
    pallas_call x3 -> x5, Pallas kernels: 209 us -> 194 us  [the longest x1 109 us: scan_back(): pl.pallas_call(partial(scan_back_kernel, count=count, depth=depth), grid=...]
    reshape x13 -> x3, local copies, waits for them, and re-layouts: 5.9 us -> 0.85 us  [the longest x1 0.7 us: local(): cw = small[:, 3:3 + DCONV, :n2].transpose(1, 0, 2).reshape(DCONV, XBC)]
    dot_general x3 -> x4, matrix products: 23.3 us -> 25.5 us  [contract_rows(): lax.dot_general(left, right, (((0, 1), (0, 1)), ((), ())), preferred_elem...]
  transfers between devices with their start and end apart: 2 -> 2, of which waited for: 0 -> 1; matrix products, arithmetic and copies ran while one was open for 8% -> 4% of each run, Pallas kernels for 15% -> 10%
where the time goes in v3:
time: 356 us
  Pallas kernels  301 us (85%)
  matrix products  25.5 us (7%)
  local copies, waits for them, and re-layouts  17.6 us (5%)
  other arithmetic  6.95 us (2%)
  starting transfers between devices  3.68 us (1%)
    pallas_call x1, Pallas kernels, scan_back(): pl.pallas_call(partial(scan_back_kernel, count=count, depth=depth), grid=...  109 us
    pallas_call x1, Pallas kernels, mix(): pl.pallas_call(partial(mix_kernel, first=first, count=count), grid=(count...  51.8 us
    pallas_call x1, Pallas kernels, project(): pl.pallas_call(partial(project_kernel, first=first, count=count, depth=de...  47.4 us
    pallas_call x1, Pallas kernels, gather(): pl.pallas_call(partial(gather_kernel, depth=depth, ranks=ranks), in_specs...  34.7 us
    pallas_call x1, Pallas kernels, reduce(): pl.pallas_call(partial(reduce_kernel, depth=depth, ranks=ranks), in_specs...  32.6 us
    dot_general x4, matrix products, contract_rows(): lax.dot_general(left, right, (((0, 1), (0, 1)), ((), ())), preferred_elem...  25.5 us
    pallas_call x1, Pallas kernels, input_grad(): pl.pallas_call(input_grad_kernel, grid=(count,), in_specs=[per((piece, D)...  19.8 us
  transfers between devices with their start and end apart: 2, of which 1 were waited for; matrix products, arithmetic and copies ran while one was open for 4% of the time, Pallas kernels for 10%

profile of v3, /device:TPU:0, one launch (start us, length us, event | category | flops | bytes accessed | tf_op | source)
XLA Modules:
  0.0 355.5 jit_solution(12013328867107365839)
XLA Ops:
  0.6 0.9 slice.39
  1.5 2.4 collective-permute-start
  5.3 34.7 %gather.1 = (bf16[4,2,2,2,24,1024]{5,4,3,2,1,0:T(8,128)(2,1)}, bf16[4,2,2,2,24,896]{5,4,3,2,1,0:T(8,128)(2,1)}, f32[32,8,128]{2,1,0:T(8,128)}) custom-call(f32[24,3352]{1,0:T(8,128)} %win_ref.1, f32[8,128]{1,0:T(8,128)} %pad.50.small_in), custom_call_target="tpu_custom_call" | custom-call | tf_op jit(solution)/shard_map/gather/pallas_call | solution.py:333
  40.0 1.0 slice_reduce_fusion.1
  41.0 1.0 slice_reduce_fusion.2
  41.9 0.9 slice_bitcast_fusion
  42.9 1.2 pad.51.dtb_ref
  48.0 1.2 subtract_bitcast_fusion.vlen_ref
  49.1 0.9 slice_reduce_fusion.3
  52.1 47.4 %project.1 = (bf16[3,512,768]{2,1,0:T(8,128)(2,1)}, f32[3,14,520,128]{3,2,1,0:T(8,128)}, f32[3,512,1792]{2,1,0:T(8,128)}, f32[3,512,128]{2,1,0:T(8,128)}, f32[3,...) custom-call(s32[3]{0:T(128)} %subtract_bitcast_fusion.vlen_ref, ...), custom_call_target="tpu_custom_call" | custom-call | tf_op jit(solution)/shard_map/project/pallas_call | solution.py:665
  99.5 51.8 %mix.1 = (bf16[3,512,768]{2,1,0:T(8,128)(2,1)}, bf16[3,512,1536]{2,1,0:T(8,128)(2,1)}, bf16[3,512,768]{2,1,0:T(8,128)(2,1)}, bf16[3,512,1536]{2,1,0:T(8,128)(2,1...) custom-call(s32[3]{0:T(128)} %subtract_bitcast_fusion.vlen_ref, ...), custom_call_target="tpu_custom_call" | custom-call | tf_op jit(solution)/shard_map/mix/pallas_call | solution.py:948
  151.3 8.5 %bitcast_convert_fusion = bf16[768,1536]{1,0:T(8,128)(2,1)} fusion(bf16[3,512,768]{2,1,0:T(8,128)(2,1)} %get-tuple-element.61.nrm_ref, bf16[3,512,1536]{2,1,0:T(8,128)(2,1)} %get-tuple-element.71.dz_ref), kind=kOutput, calls=%fused_computation | convolution fusion | flops 3625058304 | bytes 9437184 | tf_op jit(solution)/shard_map/dot_general | solution.py:1408
  159.8 5.2 %bitcast_convert_fusion.1 = bf16[1536,768]{1,0:T(8,128)(2,1)} fusion(bf16[3,512,1536]{2,1,0:T(8,128)(2,1)S(1)} %copy-done.6, bf16[3,512,768]{2,1,0:T(8,128)(2,1)S(1)} %copy-done.1), kind=kOutput, calls=%fused_computation.1 | convolution fusion | flops 3625058304 | bytes 9437184 | tf_op jit(solution)/shard_map/dot_general | solution.py:1408
  165.0 109.4 %scan_back.1 = (bf16[3,512,1024]{2,1,0:T(8,128)(2,1)}, bf16[3,512,896]{2,1,0:T(8,128)(2,1)}, f32[3,16,1792]{2,1,0:T(8,128)}, f32[3,8,1792]{2,1,0:T(8,128)}, f32[...) custom-call(f32[3,14,520,128]{3,2,1,0:T(8,128)} %get-tuple-element.72.ci_, ...), custom_call_target="tpu_custom_call" | custom-call | tf_op jit(solution)/shard_map/scan_back/pallas_call | solution.py:1227
  277.0 1.0 bitcast_reduce_fusion
  278.1 1.3 collective-permute-start.1
  279.4 0.8 slice_reduce_fusion
  282.2 3.0 patch.1
  285.2 5.6 %bitcast_convert_fusion.2 = bf16[768,1024]{1,0:T(8,128)(2,1)} fusion(bf16[3,512,768]{2,1,0:T(8,128)(2,1)S(1)} %copy-done, bf16[3,512,1024]{2,1,0:T(8,128)(2,1)} %get-tuple-element.83.dxa_ref), kind=kOutput, calls=%fused_computation.2 | convolution fusion | flops 2416705536 | bytes 7077888 | tf_op jit(solution)/shard_map/dot_general | solution.py:1408
  290.8 19.8 %input_grad.1 = (bf16[3,512,768]{2,1,0:T(8,128)(2,1)}, f32[8,768]{1,0:T(8,128)}) custom-call(bf16[3,512,768]{2,1,0:T(8,128)(2,1)} %bitcast.63, bf16[3,512,768]{2,1,0:T(8,128)(2,1)} %get-tuple-element.70.dbr_ref, f32[1,768]{1,0:T(1,128)} %reshape_squeeze.9.g_ref, bf16[3,512,1536]{2,1,0:T(8,128)(2,1)} %get-tuple-element.71.dz_ref, ...), custom_call_target="tpu_custom_call" | custom-call | tf_op jit(solution)/shard_map/input_grad/pallas_call | solution.py:1353
  310.7 6.2 %bitcast_convert_fusion.3 = bf16[768,896]{1,0:T(8,128)(2,1)} fusion(bf16[3,512,768]{2,1,0:T(8,128)(2,1)} %get-tuple-element.61.nrm_ref, bf16[3,512,896]{2,1,0:T(8,128)(2,1)} %get-tuple-element.84.dxb_ref), kind=kOutput, calls=%fused_computation.3 | convolution fusion | flops 2114617344 | bytes 6488064 | tf_op jit(solution)/shard_map/dot_general | solution.py:1408
  317.9 32.6 %reduce.13 = (f32[24,1024]{1,0:T(8,128)}, f32[24,896]{1,0:T(8,128)}, f32[8,128]{1,0:T(8,128)}) custom-call(bf16[4,2,2,2,24,1024]{5,4,3,2,1,0:T(8,128)(2,1)} %bitcast.75, bf16[4,2,2,2,24,896]{5,4,3,2,1,0:T(8,128)(2,1)} %bitcast.76, f32[32,8,128]{2,1,0:T(8,128)} %concatenate.11.small_in), custom_call_target="tpu_custom_call" | custom-call | tf_op jit(solution)/shard_map/reduce/pallas_call | solution.py:494
  350.4 1.9 assemble.1
  352.3 3.2 copy.59
  (49 shorter events, 12.9 us)
Async XLA Ops:
  1.5 49.9 %collective-permute-start = (bf16[3,16,768]{2,1,0:T(8,128)(2,1)S(1)}, bf16[3,16,768]{2,1,0:T(8,128)(2,1)S(1)}, u32[]{:S(2)}, u32[]{:S(2)}) collective-permute-start(bf16[3,16,768]{2,1,0:T(8,128)(2,1)S(1)} %slice.39), channel_id=1, source_target_pairs={{0,1},{1,2},{2,3},{4,5},{5,6},{6,7},{8,9},{9,10},{10,11},{12,13},{... | collective-permute-start | bytes 221192 | tf_op jit(solution)/shard_map/ppermute | solution.py:1404
  51.5 0.6 copy-start.4
  151.3 8.5 %copy-start.1 = (bf16[3,512,768]{2,1,0:T(8,128)(2,1)S(1)}, bf16[3,512,768]{2,1,0:T(8,128)(2,1)}, u32[]{:S(2)}) copy-start(bf16[3,512,768]{2,1,0:T(8,128)(2,1)} %get-tuple-element.70.dbr_ref) | copy-start | bytes 7077892
  151.3 8.5 %copy-start.6 = (bf16[3,512,1536]{2,1,0:T(8,128)(2,1)S(1)}, bf16[3,512,1536]{2,1,0:T(8,128)(2,1)}, u32[]{:S(2)}) copy-start(bf16[3,512,1536]{2,1,0:T(8,128)(2,1)} %get-tuple-element.78) | copy-start | bytes 14155780
  165.0 110.1 %copy-start.7 = (f32[24]{0:T(128)S(1)}, f32[24]{0:T(128)}, u32[]{:S(2)}) copy-start(f32[24]{0:T(128)} %param.18) | copy-start | bytes 292
  278.1 3.5 collective-permute-start.1
  281.6 0.7 copy-start.3
  282.2 3.0 copy-start
  310.7 6.3 %copy-start.5 = (f32[8,768]{1,0:T(8,128)S(1)}, f32[8,768]{1,0:T(8,128)}, u32[]{:S(2)}) copy-start(f32[8,768]{1,0:T(8,128)} %get-tuple-element.87) | copy-start | bytes 73732
  310.7 6.4 %copy-start.2 = (f32[32,4,128]{2,1,0:T(4,128)S(1)}, f32[32,4,128]{2,1,0:T(4,128)}, u32[]{:S(2)}) copy-start(f32[32,4,128]{2,1,0:T(4,128)} %pad.56) | copy-start | bytes 196612

commit v4 on v3

--- a/solution.py
+++ b/solution.py
@@ -293,37 +293,117 @@
 
 
 def gather_kernel(
-    w_in, small_in, xa_out, xb_out, small_out, xa_in, xb_in, send, recv, ssend, srecv, place_sem, *, depth, ranks
+    w_in,
+    g_in,
+    gg_in,
+    cb_in,
+    cw_in,
+    dtb_in,
+    alog_in,
+    dsk_in,
+    tok_in,
+    xa_out,
+    xb_out,
+    halo,
+    gain,
+    gg,
+    cb,
+    cw,
+    dtb,
+    rate,
+    dsk,
+    xa_in,
+    xb_in,
+    small_in,
+    small,
+    send,
+    recv,
+    ssend,
+    srecv,
+    place_sem,
+    halo_sem,
+    *,
+    depth,
+    ranks,
 ):
     here = Here(depth)
     xa_in[...] = w_in[:, DI : DI + XA].astype(BF)
     xb_in[...] = jnp.zeros_like(xb_in)
     xb_in[:, : PROJ - DI - XA] = w_in[:, DI + XA :].astype(BF)
+    n0, n1, n2 = g_in.shape[1], gg_in.shape[1], cb_in.shape[1]
+    small_in[...] = jnp.zeros_like(small_in)
+    small_in[0:1, :n0] = g_in[...]
+    small_in[1:2, :n1] = gg_in[...]
+    small_in[2:3, :n2] = cb_in[...]
+    small_in[3 : 3 + DCONV, :n2] = cw_in[...]
     slot = (here.z, here.y, here.x, here.c)
     own = [
         pltpu.make_async_copy(xa_in, xa_out.at[slot], place_sem.at[0]),
         pltpu.make_async_copy(xb_in, xb_out.at[slot], place_sem.at[1]),
-        pltpu.make_async_copy(small_in, small_out.at[here.rank], place_sem.at[2]),
+        pltpu.make_async_copy(small_in, small.at[here.rank], place_sem.at[2]),
     ]
+    seq = here.x * 2 + here.c
+    dp = here.z * 2 + here.y
+    piece = tok_in.shape[1]
+    after = pltpu.make_async_remote_copy(
+        src_ref=tok_in.at[:, pl.ds(piece - 16, 16)],
+        dst_ref=halo,
+        send_sem=halo_sem.at[0],
+        recv_sem=halo_sem.at[1],
+        device_id=(dp, (seq + 1) % 4),
+        device_id_type=MESH_ID,
+    )
+
+    @pl.when(seq == 0)
+    def _():
+        halo[...] = jnp.zeros_like(halo)
+
     here.greet_all(ranks)
     for copy in own:
         copy.start()
-    start, finish = everyone(here.rank, ranks, lambda other: small_in, lambda rank: small_out.at[rank], ssend, srecv)
+    start, finish = everyone(here.rank, ranks, lambda other: small_in, lambda rank: small.at[rank], ssend, srecv)
     for copy in own:
         copy.wait()
     plan = Plan(send, recv)
     plan.trace([gather_stream(here, plan, xa_out, "x"), gather_stream(here, plan, xb_out, "y")])
     plan.run(0)
     start()
-    plan.run_from(1)
+
+    @pl.when(seq < 3)
+    def _():
+        after.start()
+
+    dtb[...] = jnp.zeros_like(dtb)
+    dtb[:, 0:NH] = dtb_in[...]
+    rate[...] = jnp.zeros_like(rate)
+    rate[:, 0:NH] = -jnp.exp(alog_in[...])
+    for h in range(NH):
+        dsk[:, h * HD : (h + 1) * HD] = jnp.broadcast_to(dsk_in[:, h : h + 1], (1, HD))
+    plan.run(1)
+    plan.run(2)
     finish()
+    for r in range(ranks):
+        gain[:, r * n0 : (r + 1) * n0] = small[r, 0:1, :n0]
+        gg[:, r * n1 : (r + 1) * n1] = small[r, 1:2, :n1]
+        cb[:, r * n2 : (r + 1) * n2] = small[r, 2:3, :n2]
+        cw[:, r * n2 : (r + 1) * n2] = small[r, 3 : 3 + DCONV, :n2]
+
+    @pl.when(seq > 0)
+    def _():
+        after.wait_recv()
+
+    @pl.when(seq < 3)
+    def _():
+        after.wait_send()
+
+    plan.run_from(3)
 
 
 ANY = pl.BlockSpec(memory_space=pl.ANY)
 IN_VMEM = pl.BlockSpec(memory_space=pltpu.VMEM)
 
 
-def gather(w_in, small, depth):
+def gather(w_in, gain, gg, cb, cw, dtb, alog, dsk, tokens, depth):
     ranks = depth * 8
     rows = w_in.shape[0]
     lead = (depth, 2, 2, 2)
@@ -332,25 +412,35 @@
     dma = pltpu.SemaphoreType.DMA
     return pl.pallas_call(
         partial(gather_kernel, depth=depth, ranks=ranks),
-        in_specs=[IN_VMEM] * 2,
-        out_specs=[ANY] * 3,
+        in_specs=[IN_VMEM] * 8 + [ANY],
+        out_specs=[ANY] * 2 + [IN_VMEM] * 8,
         out_shape=[
             sds(lead + (rows, XA), BF),
             sds(lead + (rows, XD - XA), BF),
-            sds((ranks,) + small.shape, small.dtype),
+            sds((tokens.shape[0], 16, D), BF),
+            sds((1, D), F32),
+            sds((1, DI), F32),
+            sds((1, XBC), F32),
+            sds((DCONV, XBC), F32),
+            sds((1, LN), F32),
+            sds((1, LN), F32),
+            sds((1, DI), F32),
         ],
         scratch_shapes=[
             pltpu.VMEM((rows, XA), BF),
             pltpu.VMEM((rows, XD - XA), BF),
+            pltpu.VMEM((8, LN), F32),
+            pltpu.VMEM((ranks, 8, LN), F32),
             dma((n,)),
             dma((n,)),
             dma((ranks,)),
             dma((ranks,)),
             dma((3,)),
+            dma((2,)),
         ],
         compiler_params=pltpu.CompilerParams(collective_id=0, has_side_effects=True),
         name="gather",
-    )(w_in, small)
+    )(w_in, gain, gg, cb, cw, dtb, alog, dsk, tokens)
 
 
 def reduce_stream(here, plan, item, first):
@@ -464,7 +554,28 @@
     plan.trace(streams)
 
 
-def reduce_kernel(pa, pb, small_in, oa, ob, small_out, send, recv, ssend, srecv, small_got, own_sems, *scratch, depth, ranks):
+def reduce_kernel(
+    pa,
+    pb,
+    gain_ref,
+    gg_ref,
+    conv_ref,
+    head_ref,
+    rate_ref,
+    oa,
+    ob,
+    small_out,
+    send,
+    recv,
+    ssend,
+    srecv,
+    small_in,
+    small_got,
+    own_sems,
+    *scratch,
+    depth,
+    ranks,
+):
     here = Here(depth)
     here.greet_all(ranks)
     start, finish = everyone(
@@ -473,33 +584,53 @@
     plan = Plan(send, recv)
     reduce_items(here, plan, (pa, pb), (oa, ob), scratch, own_sems)
     plan.run(0)
+    small_in[...] = jnp.zeros_like(small_in)
+    total = lambda v: jnp.sum(v, axis=0, keepdims=True)
+    gain, gg = total(gain_ref[...]), total(gg_ref[...])
+    taps = [total(conv_ref[8 * t : 8 * t + 8]) for t in range(DCONV + 1)]
+    heads = [
+        total(head_ref[0:8])[:, :NH],
+        (total(head_ref[8:16]) * rate_ref[...])[:, :NH],
+        total(head_ref[16:24])[:, :NH],
+    ]
+    n0, n1, n2 = D // ranks, DI // ranks, XBC // ranks
+    for r in range(ranks):
+        small_in[r, 0:1, :n0] = gain[:, r * n0 : (r + 1) * n0]
+        small_in[r, 1:2, :n1] = gg[:, r * n1 : (r + 1) * n1]
+        small_in[r, 2:3, :n2] = taps[DCONV][:, r * n2 : (r + 1) * n2]
+        for t in range(DCONV):
+            small_in[r, 3 + t : 4 + t, :n2] = taps[t][:, r * n2 : (r + 1) * n2]
+        for k in range(3):
+            small_in[r, 7:8, k * NH : (k + 1) * NH] = heads[k]
+    plan.run(1)
     start()
-    plan.run_from(1)
+    plan.run_from(2)
     finish()
 
-    def add(i, total):
-        return total + jnp.where(i == here.rank, small_in[i], small_got[i])
+    def add(i, sum_so_far):
+        return sum_so_far + jnp.where(i == here.rank, small_in[i], small_got[i])
 
     small_out[...] = lax.fori_loop(0, ranks, add, jnp.zeros(small_out.shape, F32))
 
 
-def reduce(pa, pb, small, depth):
+def reduce(pa, pb, gain, gg, conv, head, rate, depth):
     ranks = depth * 8
     sds = jax.ShapeDtypeStruct
     dma = pltpu.SemaphoreType.DMA
     n = reduce_copies(depth.bit_length() - 1)
-    scratch = [dma((n,)), dma((n,)), dma((ranks,)), dma((ranks,)), pltpu.VMEM(small.shape, F32), dma((2,))]
+    small = pltpu.VMEM((ranks, 8, LN), F32)
+    scratch = [dma((n,)), dma((n,)), dma((ranks,)), dma((ranks,)), small, small, dma((2,))]
     for part in (pa, pb):
         scratch += reduce_scratch(depth, part.shape[-2:])
     return pl.pallas_call(
         partial(reduce_kernel, depth=depth, ranks=ranks),
-        in_specs=[ANY, ANY, IN_VMEM],
+        in_specs=[ANY] * 2 + [IN_VMEM] * 5,
         out_specs=[IN_VMEM] * 3,
-        out_shape=[sds(a.shape[4:], F32) for a in (pa, pb)] + [sds(small.shape[1:], F32)],
+        out_shape=[sds(a.shape[4:], F32) for a in (pa, pb)] + [sds((8, LN), F32)],
         scratch_shapes=scratch,
         compiler_params=pltpu.CompilerParams(collective_id=1, has_side_effects=True, vmem_limit_bytes=LIMIT),
         name="reduce",
-    )(pa, pb, small)
+    )(pa, pb, gain, gg, conv, head, rate)
 
 
 def whole(shape):
@@ -559,8 +690,8 @@
     piece = x_ref.shape[0]
     chunks = piece // CL
     section = pl.program_id(0)
-    valid = vlen_ref[first + section]
     here = Here(depth)
+    valid = vlen_ref[first + section, 0] - (here.x * 2 + here.c) * piece
     slot = (here.z, here.y, here.x, here.c)
     own = [
         pltpu.make_async_copy(z_in, z_out.at[slot], place_sem.at[0]),
@@ -795,7 +926,6 @@
 
 def mix_kernel(
     vlen_ref,
-    x_ref,
     cot_ref,
     nrm_ref,
     act_ref,
@@ -807,7 +937,6 @@
     wo_ref,
     gg_ref,
     dsk_ref,
-    out_ref,
     gn_ref,
     dbr_ref,
     dz_ref,
@@ -829,10 +958,10 @@
     first,
     count,
 ):
-    piece = x_ref.shape[0]
+    piece = cot_ref.shape[0]
     chunks = piece // CL
     section = pl.program_id(0)
-    valid = vlen_ref[first + section]
+    valid = vlen_ref[first + section, 0] - lax.axis_index("seq") * piece
     states = Exchange(s_ref, sib, out, got, *sems, giver=0)
     even = states.c == 0
     weigh = lambda own, sibs: (jnp.where(even, sibs, 1.0), jnp.where(even, 1.0, own))
@@ -931,18 +1060,13 @@
     lax.fori_loop(0, chunks, chunk, jnp.ones((1, DI), F32))
     dsin_ref[0:NS] = dsacc[...].astype(BF)
     dsin_ref[NS:] = s_ref[section, NS:]
-    for j in range(D // 256):
-        cols = slice(j * 256, (j + 1) * 256)
-        branch = nn(gn_ref[...], wo_ref[:, cols])
-        out_ref[:, cols] = jnp.where(live, x_ref[:, cols].astype(F32) + branch, 0.0).astype(BF)
-
     @pl.when(section == count - 1)
     def _():
         states.end(count)
 
 
-def mix(first, count, valid, tokens, cot, normed, act, step, ld, sloc, s, w_z, w_o, gg, dsk):
-    piece = tokens.shape[1]
+def mix(first, count, valid, cot, normed, act, step, ld, sloc, s, w_z, w_o, gg, dsk):
+    piece = cot.shape[1]
     chunks = piece // CL
     sds = jax.ShapeDtypeStruct
     return pl.pallas_call(
@@ -950,7 +1074,6 @@
         grid=(count,),
         in_specs=[
             SMEM,
-            per((piece, D), first),
             per((piece, D), first),
             per((piece, D)),
             per((piece, XBC)),
@@ -964,7 +1087,6 @@
             whole((1, DI)),
         ],
         out_specs=[
-            per((piece, D)),
             per((piece, DI)),
             per((piece, D)),
             per((piece, DI)),
@@ -975,7 +1097,6 @@
             whole((8, DI)),
         ],
         out_shape=[
-            sds((count, piece, D), BF),
             sds((count, piece, DI), BF),
             sds((count, piece, D), BF),
             sds((count, piece, DI), BF),
@@ -996,7 +1117,7 @@
         + exchange_scratch(count),
         compiler_params=pltpu.CompilerParams(vmem_limit_bytes=LIMIT, collective_id=2, has_side_effects=True),
         name="mix",
-    )(valid, tokens, cot, normed, act, step, ld, sloc, s, w_z, w_o, gg, dsk)
+    )(valid, cot, normed, act, step, ld, sloc, s, w_z, w_o, gg, dsk)
 
 
 def scan_back_kernel(
@@ -1021,9 +1142,9 @@
     edge_ref,
     cgrad_ref,
     hgrad_ref,
-    skip_ref,
     shard_a,
     shard_b,
+    skip_ref,
     ds,
     xa,
     dsl,
@@ -1214,6 +1335,8 @@
 
     @pl.when(section == count - 1)
     def _():
+        top, low = halves(skip_ref[...])
+        hgrad_ref[16:24] = nt(top, e2[0:LN]) + nt(low, e2[0:LN])
         states.end(count)
         plan.run_from(steps + 1)
 
@@ -1250,8 +1373,7 @@
             per((16, XBC)),
             per((8, XBC)),
             whole((40, XBC)),
-            whole((16, LN)),
-            whole((8, DI)),
+            whole((24, LN)),
             whole(part_a.shape[4:]),
             whole(part_b.shape[4:]),
         ],
@@ -1261,12 +1383,12 @@
             sds((count, 16, XBC), F32),
             sds((count, 8, XBC), F32),
             sds((40, XBC), F32),
-            sds((16, LN), F32),
-            sds((8, DI), F32),
+            sds((24, LN), F32),
             sds(part_a.shape[4:], F32),
             sds(part_b.shape[4:], F32),
         ],
         scratch_shapes=[
+            pltpu.VMEM((8, DI), F32),
             pltpu.VMEM((NS, DI), F32),
             pltpu.VMEM((CL, XBC), F32),
             pltpu.VMEM((CL, XBC), F32),
@@ -1319,8 +1441,29 @@
     )(dxa, dxb, fix, edge, cw)
 
 
-def input_grad_kernel(x_ref, dbr_ref, g_ref, dz_ref, dxa_ref, dxb_ref, wz_ref, wa_ref, wb_ref, out_ref, gain_ref, dn):
+def input_grad_kernel(
+    vlen_ref,
+    x_ref,
+    dbr_ref,
+    g_ref,
+    gn_ref,
+    dz_ref,
+    dxa_ref,
+    dxb_ref,
+    wo_ref,
+    wz_ref,
+    wa_ref,
+    wb_ref,
+    block_ref,
+    out_ref,
+    gain_ref,
+    dn,
+    *,
+    first,
+):
     piece = x_ref.shape[0]
+    valid = vlen_ref[first + pl.program_id(0), 0] - lax.axis_index("seq") * piece
+    live = lax.broadcasted_iota(jnp.int32, (piece, 1), 0) < valid
 
     @pl.when(pl.program_id(0) == 0)
     def _():
@@ -1328,6 +1471,8 @@
 
     for j in range(D // 256):
         cols = slice(j * 256, (j + 1) * 256)
+        branch = nn(gn_ref[...], wo_ref[:, cols])
+        block_ref[:, cols] = jnp.where(live, x_ref[:, cols].astype(F32) + branch, 0.0).astype(BF)
         dn[:, cols] = (
             nt(dz_ref[...], wz_ref[cols, :]) + nt(dxa_ref[...], wa_ref[cols, :]) + nt(dxb_ref[...], wb_ref[cols, :])
         )
@@ -1347,29 +1492,32 @@
     lax.fori_loop(0, piece // 64, rows_of, 0)
 
 
-def input_grad(first, count, tokens, dbr, gain, dz, dxa, dxb, w_z, wa, wb):
+def input_grad(first, count, valid, tokens, dbr, gain, gn, dz, dxa, dxb, w_o, w_z, wa, wb):
     piece = tokens.shape[1]
     sds = jax.ShapeDtypeStruct
     return pl.pallas_call(
-        input_grad_kernel,
+        partial(input_grad_kernel, first=first),
         grid=(count,),
         in_specs=[
+            SMEM,
             per((piece, D), first),
             per((piece, D)),
             whole((1, D)),
             per((piece, DI)),
+            per((piece, DI)),
             per((piece, XA)),
             per((piece, XD - XA)),
+            kept((DI, D)),
             kept((D, DI)),
             kept((D, XA)),
             kept((D, XD - XA)),
         ],
-        out_specs=[per((piece, D)), whole((8, D))],
-        out_shape=[sds((count, piece, D), BF), sds((8, D), F32)],
+        out_specs=[per((piece, D)), per((piece, D)), whole((8, D))],
+        out_shape=[sds((count, piece, D), BF), sds((count, piece, D), BF), sds((8, D), F32)],
         scratch_shapes=[pltpu.VMEM((piece, D), F32)],
         compiler_params=pltpu.CompilerParams(vmem_limit_bytes=LIMIT),
         name="input_grad",
-    )(tokens, dbr, gain, dz, dxa, dxb, w_z, wa, wb)
+    )(valid, tokens, dbr, gain, gn, dz, dxa, dxb, w_o, w_z, wa, wb)
 
 
 def assemble_kernel(z, a, b, o, t, win, wo, g0, g1, g2, g3, h0, h1, h2):
@@ -1422,8 +1570,6 @@
     lengths,
     cotangent,
 ):
-    ranks = lax.axis_size("dp") * lax.axis_size("seq")
-    place = lax.axis_index("seq")
     tokens = tokens[:, 0]
     cot = cotangent[:, 0]
     batches, piece, _ = tokens.shape
@@ -1431,58 +1577,40 @@
 
     depth = lax.axis_size("dp") // 2
     n0, n1, n2 = norm_gain.shape[0], gated_gain.shape[0], conv_bias.shape[0]
-    widen = lambda v: jnp.pad(v, ((0, 0), (0, LN - v.shape[1])))
-    small = [norm_gain[None], gated_gain[None], conv_bias[None], conv_weight]
-    small = jnp.pad(jnp.concatenate([widen(v) for v in small]), ((0, 1), (0, 0)))
-    wa, wb, small = gather(w_in, small, depth)
+    wa, wb, halo, gain, gg, cb, cw, dtb, rate, dsk = gather(
+        w_in,
+        norm_gain[None],
+        gated_gain[None],
+        conv_bias[None],
+        conv_weight,
+        dt_bias[None],
+        a_log[None],
+        d_skip[None],
+        tokens,
+        depth,
+    )
     wa, wb = wa.reshape(D, XA), wb.reshape(D, XD - XA)
-    gain = small[:, 0, :n0].reshape(1, D)
-    gg = small[:, 1, :n1].reshape(1, DI)
-    cb = small[:, 2, :n2].reshape(1, XBC)
-    cw = small[:, 3 : 3 + DCONV, :n2].transpose(1, 0, 2).reshape(DCONV, XBC)
-
-    halo = pass_on(tokens[:, piece - 16 :], "seq", 1)
-    valid = lengths[:, 0].astype(jnp.int32) - place.astype(jnp.int32) * piece
-    lane_pad = ((0, 0), (0, LN - NH))
-    dtb = jnp.pad(dt_bias[None], lane_pad)
-    rate = -jnp.exp(a_log)
-    rate_row = jnp.pad(rate[None], lane_pad)
-    dsk = jnp.repeat(d_skip, HD)[None]
 
     first, count = 0, batches
     normed, ci, act, step, ld, sig, sloc, s, w_z, w_o = project(
-        first, count, depth, valid, tokens, halo, gain, wa, wb, cw, cb, dtb, rate_row, w_in, w_out
+        first, count, depth, lengths, tokens, halo, gain, wa, wb, cw, cb, dtb, rate, w_in, w_out
     )
     w_z, w_o = w_z.reshape(D, DI), w_o.reshape(DI, D)
-    out, gn, dbr, dz, dy, y, inc, dsin, ggrad = mix(
-        first, count, valid, tokens, cot, normed, act, step, ld, sloc, s, w_z, w_o, gg, dsk
+    gn, dbr, dz, dy, y, inc, dsin, ggrad = mix(
+        first, count, lengths, cot, normed, act, step, ld, sloc, s, w_z, w_o, gg, dsk
     )
     lead = (depth, 2, 2, 2)
     grad_wo = contract_rows(gn, dbr).astype(BF).reshape(lead + (n1, D))
     grad_wz = contract_rows(normed, dz).astype(BF).reshape(lead + (rows, DI))
-    dxa, dxb, fix, edge, cgrad, hgrad, skip, shard_wo, shard_wz = scan_back(
-        count, depth, ci, step, ld, sig, dy, y, inc, sloc, dsin, cw, cb, rate_row, dsk, grad_wo, grad_wz
+    dxa, dxb, fix, edge, cgrad, hgrad, shard_wo, shard_wz = scan_back(
+        count, depth, ci, step, ld, sig, dy, y, inc, sloc, dsin, cw, cb, rate, dsk, grad_wo, grad_wz
     )
     dxa, dxb = patch(dxa, dxb, fix, pass_on(edge, "seq", -1), cw)
-    tgrad, gain_grad = input_grad(first, count, tokens, dbr, gain, dz, dxa, dxb, w_z, wa, wb)
+    out, tgrad, gain_grad = input_grad(first, count, lengths, tokens, dbr, gain, gn, dz, dxa, dxb, w_o, w_z, wa, wb)
     grad_wa = contract_rows(normed, dxa).astype(BF).reshape(lead + (rows, XA))
     grad_wb = contract_rows(normed, dxb).astype(BF).reshape(lead + (rows, XD - XA))
 
-    grad_cw = cgrad[:32].reshape(DCONV, 8, XBC).sum(1)
-    heads = hgrad.reshape(2, 8, LN).sum(1)[:, :NH]
-    heads = jnp.concatenate([heads[0], heads[1] * rate, skip.sum(0).reshape(NH, HD).sum(1)])
-    split = lambda v, n: jnp.pad(v.reshape(-1, ranks, n).transpose(1, 0, 2), ((0, 0), (0, 0), (0, LN - n)))
-    packed = jnp.concatenate(
-        [
-            split(gain_grad.sum(0), n0),
-            split(ggrad.sum(0), n1),
-            split(cgrad[32:].sum(0), n2),
-            split(grad_cw, n2),
-            jnp.broadcast_to(jnp.pad(heads, (0, LN - 3 * NH)), (ranks, 1, LN)),
-        ],
-        axis=1,
-    )
-    shard_wa, shard_wb, total = reduce(grad_wa, grad_wb, packed, depth)
+    shard_wa, shard_wb, total = reduce(grad_wa, grad_wb, gain_grad, ggrad, cgrad, hgrad, rate, depth)
     shard_win, shard_wo, g0, g1, g2, g3, h0, h1, h2 = assemble(shard_wz, shard_wa, shard_wb, shard_wo, total, n0, n1, n2)
     return (
         out[:, None],

time: 356 us -> 333 us (0.935)
  local copies, waits for them, and re-layouts: 17.6 us -> 1.99 us
  other arithmetic: 6.95 us -> 0 us
    pallas_call x1, Pallas kernels: 51.8 us -> 45.3 us  [mix(): pl.pallas_call(partial(mix_kernel, first=first, count=count), grid=(count...]
    pallas_call x1, Pallas kernels: 19.8 us -> 25.1 us  [input_grad(): pl.pallas_call(partial(input_grad_kernel, first=first), grid=(count,), in...]
    reduce_sum x7 -> x0, other arithmetic: 4.33 us -> none  [the longest x1 1.01 us: local(): grad_cw = cgrad[:32].reshape(DCONV, 8, XBC).sum(1)]
    slice x4 -> x0, local copies, waits for them, and re-layouts: 3.76 us -> none  [the longest x1 0.96 us: local(): gg = small[:, 1, :n1].reshape(1, DI)]
  transfers between devices with their start and end apart: 2 -> 1, of which waited for: 1 -> 1; matrix products, arithmetic and copies ran while one was open for 4% -> 0% of each run, Pallas kernels for 10% -> 0%
where the time goes in v4:
time: 333 us; the launch traced here: 332 us
  Pallas kernels  300 us (90%)
  matrix products  25.6 us (8%)
    pallas_call x1, Pallas kernels, scan_back(): pl.pallas_call(partial(scan_back_kernel, count=count, depth=depth), grid=...  110 us
    pallas_call x1, Pallas kernels, project(): pl.pallas_call(partial(project_kernel, first=first, count=count, depth=de...  47.7 us
    pallas_call x1, Pallas kernels, mix(): pl.pallas_call(partial(mix_kernel, first=first, count=count), grid=(count...  45.3 us
    pallas_call x1, Pallas kernels, gather(): pl.pallas_call(partial(gather_kernel, depth=depth, ranks=ranks), in_specs...  35.4 us
    pallas_call x1, Pallas kernels, reduce(): pl.pallas_call(partial(reduce_kernel, depth=depth, ranks=ranks), in_specs...  32.3 us
    dot_general x4, matrix products, contract_rows(): lax.dot_general(left, right, (((0, 1), (0, 1)), ((), ())), preferred_elem...  25.6 us
    pallas_call x1, Pallas kernels, input_grad(): pl.pallas_call(partial(input_grad_kernel, first=first), grid=(count,), in...  25.1 us
  transfers between devices with their start and end apart: 1, of which 1 were waited for; matrix products, arithmetic and copies ran while one was open for 0% of the time, Pallas kernels for 0%

profile of v4, /device:TPU:0, one launch (start us, length us, event | category | flops | bytes accessed | tf_op | source)
XLA Modules:
  0.0 332.2 jit_solution(11228075574522796)
XLA Ops:
  0.6 1.3 copy.29.vlen_ref
  2.0 35.4 %gather.1 = (bf16[4,2,2,2,24,1024]{5,4,3,2,1,0:T(8,128)(2,1)}, bf16[4,2,2,2,24,896]{5,4,3,2,1,0:T(8,128)(2,1)}, bf16[3,16,768]{2,1,0:T(8,128)(2,1)}, f32[1,768]{...) custom-call(f32[24,3352]{1,0:T(8,128)} %win_ref.1, ...), custom_call_target="tpu_custom_call" | custom-call | tf_op jit(solution)/shard_map/gather/pallas_call | solution.py:413
  37.4 47.7 %project.1 = (bf16[3,512,768]{2,1,0:T(8,128)(2,1)}, f32[3,14,520,128]{3,2,1,0:T(8,128)}, f32[3,512,1792]{2,1,0:T(8,128)}, f32[3,512,128]{2,1,0:T(8,128)}, f32[3,...) custom-call(s32[3,1]{1,0:T(4,128)} %copy.29.vlen_ref, ...), custom_call_target="tpu_custom_call" | custom-call | tf_op jit(solution)/shard_map/project/pallas_call | solution.py:796
  85.1 45.3 %mix.1 = (bf16[3,512,1536]{2,1,0:T(8,128)(2,1)}, bf16[3,512,768]{2,1,0:T(8,128)(2,1)}, bf16[3,512,1536]{2,1,0:T(8,128)(2,1)}, f32[3,512,1536]{2,1,0:T(8,128)}, f...) custom-call(s32[3,1]{1,0:T(4,128)} %copy.29.vlen_ref, ...), custom_call_target="tpu_custom_call" | custom-call | tf_op jit(solution)/shard_map/mix/pallas_call | solution.py:1072
  130.4 0.0 copy-start
  130.4 0.0 copy-start.2
  130.4 8.5 %bitcast_convert_fusion = bf16[768,1536]{1,0:T(8,128)(2,1)} fusion(bf16[3,512,768]{2,1,0:T(8,128)(2,1)} %get-tuple-element.72.nrm_ref, bf16[3,512,1536]{2,1,0:T(8,128)(2,1)} %get-tuple-element.84.dz_ref), kind=kOutput, calls=%fused_computation | convolution fusion | flops 3625058304 | bytes 9437184 | tf_op jit(solution)/shard_map/dot_general | solution.py:1556
  138.9 0.0 copy-done
  138.9 0.0 copy-done.2
  138.9 5.2 %bitcast_convert_fusion.1 = bf16[1536,768]{1,0:T(8,128)(2,1)} fusion(bf16[3,512,1536]{2,1,0:T(8,128)(2,1)S(1)} %copy-done, bf16[3,512,768]{2,1,0:T(8,128)(2,1)S(1)} %copy-done.2), kind=kOutput, calls=%fused_computation.1 | convolution fusion | flops 3625058304 | bytes 9437184 | tf_op jit(solution)/shard_map/dot_general | solution.py:1556
  144.0 109.7 %scan_back.1 = (bf16[3,512,1024]{2,1,0:T(8,128)(2,1)}, bf16[3,512,896]{2,1,0:T(8,128)(2,1)}, f32[3,16,1792]{2,1,0:T(8,128)}, f32[3,8,1792]{2,1,0:T(8,128)}, f32[...) custom-call(f32[3,14,520,128]{3,2,1,0:T(8,128)} %get-tuple-element.85.ci_ref, ...), custom_call_target="tpu_custom_call" | custom-call | tf_op jit(solution)/shard_map/scan_back/pallas_call | solution.py:1350
  253.8 1.3 collective-permute-start
  255.1 2.2 collective-permute-done.edge_ref
  257.3 0.0 copy-start.3
  257.3 0.7 copy-done.3
  258.0 0.0 copy-start.1
  258.0 3.0 patch.1
  261.0 0.0 copy-done.1
  261.0 5.7 %bitcast_convert_fusion.2 = bf16[768,1024]{1,0:T(8,128)(2,1)} fusion(bf16[3,512,768]{2,1,0:T(8,128)(2,1)S(1)} %copy-done.1, bf16[3,512,1024]{2,1,0:T(8,128)(2,1)} %get-tuple-element.95.dxa_ref), kind=kOutput, calls=%fused_computation.2 | convolution fusion | flops 2416705536 | bytes 7077888 | tf_op jit(solution)/shard_map/dot_general | solution.py:1556
  266.7 25.1 %input_grad.1 = (bf16[3,512,768]{2,1,0:T(8,128)(2,1)}, bf16[3,512,768]{2,1,0:T(8,128)(2,1)}, f32[8,768]{1,0:T(8,128)}) custom-call(s32[3,1]{1,0:T(4,128)} %copy.29.vlen_ref, bf16[3,512,768]{2,1,0:T(8,128)(2,1)} %bitcast.46, bf16[3,512,768]{2,1,0:T(8,128)(2,1)} %get-tuple-element.82.dbr_ref, f32[1,768]{1,0:T(1,128)} %get-tuple-element.65.g_ref, ...), custom_call_target="tpu_custom_call" | custom-call | tf_op jit(solution)/shard_map/input_grad/pallas_call | solution.py:1498
  291.8 6.3 %bitcast_convert_fusion.3 = bf16[768,896]{1,0:T(8,128)(2,1)} fusion(bf16[3,512,768]{2,1,0:T(8,128)(2,1)} %get-tuple-element.72.nrm_ref, bf16[3,512,896]{2,1,0:T(8,128)(2,1)} %get-tuple-element.96.dxb_ref), kind=kOutput, calls=%fused_computation.3 | convolution fusion | flops 2114617344 | bytes 6488064 | tf_op jit(solution)/shard_map/dot_general | solution.py:1556
  298.1 32.3 %reduce.1 = (f32[24,1024]{1,0:T(8,128)}, f32[24,896]{1,0:T(8,128)}, f32[8,128]{1,0:T(8,128)}) custom-call(bf16[4,2,2,2,24,1024]{5,4,3,2,1,0:T(8,128)(2,1)} %bitcast.58, bf16[4,2,2,2,24,896]{5,4,3,2,1,0:T(8,128)(2,1)} %bitcast.59, f32[8,768]{1,0:T(8,128)} %get-tuple-element.100.gain_ref, f32[8,1536]{1,0:T(8,128)} %get-tuple-element.101.gg_ref, ...), custom_call_target="tpu_custom_call" | custom-call | tf_op jit(solution)/shard_map/reduce/pallas_call | solution.py:625
  330.4 1.9 assemble.1
Async XLA Ops:
  130.4 8.5 %copy-start = (bf16[3,512,1536]{2,1,0:T(8,128)(2,1)S(1)}, bf16[3,512,1536]{2,1,0:T(8,128)(2,1)}, u32[]{:S(2)}) copy-start(bf16[3,512,1536]{2,1,0:T(8,128)(2,1)} %get-tuple-element.83.gn_ref) | copy-start | bytes 14155780
  130.4 8.5 %copy-start.2 = (bf16[3,512,768]{2,1,0:T(8,128)(2,1)S(1)}, bf16[3,512,768]{2,1,0:T(8,128)(2,1)}, u32[]{:S(2)}) copy-start(bf16[3,512,768]{2,1,0:T(8,128)(2,1)} %get-tuple-element.82.dbr_ref) | copy-start | bytes 7077892
  253.8 3.5 %collective-permute-start = (f32[3,8,1792]{2,1,0:T(8,128)}, f32[3,8,1792]{2,1,0:T(8,128)S(1)}, u32[]{:S(2)}, u32[]{:S(2)}) collective-permute-start(f32[3,8,1792]{2,1,0:T(8,128)} %get-tuple-element.94), channel_id=1, source_target_pairs={{1,0},{2,1},{3,2},{5,4},{6,5},{7,6},{9,8},{10,9},{11,10},{13,12},{... | collective-permute-start | bytes 516104 | tf_op jit(solution)/shard_map/ppermute | solution.py:1552
  257.3 0.7 copy-start.3
  258.0 3.0 copy-start.1
